TPU v7x, 32 devices: a whole 2x2x4 slice. The times are simulated.
32 devices in a mesh: tm: 8 (over z, x), head: 4 (over y, core).
Axes of the slice: x: 2, y: 2, z: 4, core: 2. Of those that a mesh axis runs over, the one named last changes fastest.
Arguments:
- queries: bfloat16 [18432, 1024], P(('tm', 'head')), may hold values from -8 to 8
- keys: bfloat16 [18432, 1024], P(('tm', 'head')), may hold values from -8 to 8
- values: bfloat16 [18432, 1024], P(('tm', 'head')), may hold values from -6 to 6
- tile_list: int32 [48, 7], P('tm'), may hold values from 0 to 47, as said below
- tile_count: int32 [48], P('tm'), may hold values from 1 to 7
Outputs:
- attended: bfloat16 [18432, 1024], P(('tm', 'head'))
Inputs may be any that keep to these rules, and one draw needn't show every extreme that they name: `tile_list`: row t lists distinct tiles of t's time slab (tiles t // 6 * 6 and on) and of the slabs just before and after it; the first slot is t itself; every slot holds such a tile, also past the count.
All inputs are finite; a program needn't handle non-finite values.
Results may differ from a plain program's by a relative error of at most 0.0046.
Values may be sent and summed in bfloat16 or wider, within the bound.
No kernel may reach another device: no remote copies, remote signals or barrier semaphores. Data moves between devices by JAX's collectives and lax.ppermute only.
A program may use at most 64 MiB of HBM per device.

v0:
```python
import functools

import jax
import jax.numpy as jnp
from jax import lax
from jax.experimental import pallas as pl
from jax.experimental.pallas import tpu as pltpu
from jax.sharding import Mesh, PartitionSpec as P


HD = 128
TILE = 384
UNROLL = 4
LOG2E = 1.4426950408889634
SPLIT_VMEM = 61 * 2**20
AXES = ("group", "member", "head")

ANY = pl.BlockSpec(memory_space=pl.ANY)
HBM = pl.BlockSpec(memory_space=pltpu.HBM)
SMEM = pl.BlockSpec(memory_space=pltpu.SMEM)
VMEM = pl.BlockSpec(memory_space=pltpu.VMEM)


def split_kernel_q(count, arrays, meta_ref, *refs):
    sources, targets = refs[:arrays], refs[arrays : arrays + count]
    stage, in_sems, out_sems = refs[arrays + count :]
    width = stage.shape[-1]

    def read(step, array):
        column = pl.multiple_of((meta_ref[0] ^ step) * width, width)
        return pltpu.make_async_copy(
            sources[array].at[:, pl.ds(column, width)], stage.at[step, array], in_sems.at[step, array]
        )

    def write(step):
        return pltpu.make_async_copy(stage.at[step], targets[step], out_sems.at[step])

    order = list(range(count - 1, -1, -1))
    for step in order:
        for array in range(arrays):
            read(step, array).start()
    for step in order:
        for array in range(arrays):
            read(step, array).wait()
        write(step).start()
    for step in order:
        write(step).wait()


def split_queries(meta, sources, count):
    tokens, row_width = sources[0].shape
    arrays = len(sources)
    piece = (arrays, tokens, row_width // count)
    return pl.pallas_call(
        functools.partial(split_kernel_q, count, arrays),
        in_specs=[SMEM] + [HBM] * arrays,
        out_specs=[ANY] * count,
        out_shape=[jax.ShapeDtypeStruct(piece, sources[0].dtype)] * count,
        scratch_shapes=[
            pltpu.VMEM((count,) + piece, sources[0].dtype),
            pltpu.SemaphoreType.DMA((count, arrays)),
            pltpu.SemaphoreType.DMA((count,)),
        ],
        compiler_params=pltpu.CompilerParams(vmem_limit_bytes=8 * 2**20),
        name="split_queries",
    )(meta, *sources)


def split_kernel(layout, meta_ref, *refs):
    sources, targets = refs[:2], refs[2 : 2 + len(layout)]
    stage, in_sems, out_sems = refs[2 + len(layout) :]
    width = stage.shape[-1]

    def read(slot, step, array):
        column = pl.multiple_of((meta_ref[0] ^ step) * width, width)
        return pltpu.make_async_copy(
            sources[array].at[:, pl.ds(column, width)], stage.at[slot, array], in_sems.at[slot, array]
        )

    reads, writes, slot = [], [], 0
    for index, steps in enumerate(layout):
        reads.append([read(slot + k, s, array) for k, s in enumerate(steps) for array in range(2)])
        block = stage.at[slot] if len(steps) == 1 else stage.at[pl.ds(slot, len(steps))]
        writes.append(pltpu.make_async_copy(block, targets[index], out_sems.at[index]))
        slot += len(steps)
    for copies in reads:
        for copy in copies:
            copy.start()
    for copies, write in zip(reads, writes):
        for copy in copies:
            copy.wait()
        write.start()
    for write in writes:
        write.wait()


def split_heads(meta, keys, values, layout, members):
    tokens, row_width = keys.shape
    piece = (2, tokens, row_width // members)
    shapes = [piece if len(steps) == 1 else (len(steps),) + piece for steps in layout]
    return pl.pallas_call(
        functools.partial(split_kernel, layout),
        in_specs=[SMEM] + [HBM] * 2,
        out_specs=[ANY] * len(layout),
        out_shape=[jax.ShapeDtypeStruct(shape, keys.dtype) for shape in shapes],
        scratch_shapes=[
            pltpu.VMEM((members,) + piece, keys.dtype),
            pltpu.SemaphoreType.DMA((members, 2)),
            pltpu.SemaphoreType.DMA((len(layout),)),
        ],
        compiler_params=pltpu.CompilerParams(vmem_limit_bytes=SPLIT_VMEM),
        name="split_heads",
    )(meta, keys, values)


def join_kernel(count, meta_ref, *refs):
    sources, target, sems = refs[:count], refs[count], refs[count + 1]
    width = sources[0].shape[-1]
    copies = []
    for step in range(count):
        column = pl.multiple_of((meta_ref[0] ^ step) * width, width)
        copies.append(
            pltpu.make_async_copy(sources[step], target.at[:, pl.ds(column, width)], sems.at[step])
        )
    for copy in copies:
        copy.start()
    for copy in copies:
        copy.wait()


def join_heads(meta, pieces):
    count = len(pieces)
    tokens, width = pieces[0].shape
    return pl.pallas_call(
        functools.partial(join_kernel, count),
        in_specs=[SMEM] + [VMEM] * count,
        out_specs=HBM,
        out_shape=jax.ShapeDtypeStruct((tokens, count * width), pieces[0].dtype),
        scratch_shapes=[pltpu.SemaphoreType.DMA((count,))],
        compiler_params=pltpu.CompilerParams(vmem_limit_bytes=4 * 2**20),
        name="join_heads",
    )(meta, *pieces)


def pack_kernel(first, second, target):
    target[0] = first[...]
    target[1] = second[...]


def pack(first, second):
    return pl.pallas_call(
        pack_kernel,
        in_specs=[VMEM] * 2,
        out_specs=VMEM,
        out_shape=jax.ShapeDtypeStruct((2,) + first.shape, first.dtype),
        compiler_params=pltpu.CompilerParams(vmem_limit_bytes=4 * 2**20),
        name="pack",
    )(first, second)


def assemble_kernel(places, members, head_size, meta_ref, *refs):
    arrays, targets = refs[:-2], refs[-2:]
    tokens = arrays[0].shape[-2]
    slab = head_size * tokens
    own = members * tokens
    for array, inner, step, halo in places:
        source = meta_ref[0] ^ step
        lane = (source % head_size) * tokens
        if halo:
            start = lane + jnp.where(source < head_size, slab + own, 0)
        else:
            start = slab + source * tokens
        rows = pl.ds(pl.multiple_of(start, 16), tokens)
        for part in range(2):
            ref = arrays[array]
            targets[part][rows] = ref[part] if inner is None else ref[inner, part]


def assemble(meta, pieces, members, head_size):
    arrays = [piece[0] for piece in pieces]
    places = [(i, inner, step, halo) for i, (_, inner, step, halo) in enumerate(pieces)]
    tokens, width = arrays[0].shape[-2:]
    window = (members + 2 * head_size) * tokens
    return pl.pallas_call(
        functools.partial(assemble_kernel, places, members, head_size),
        in_specs=[SMEM] + [VMEM] * len(arrays),
        out_specs=[VMEM] * 2,
        out_shape=[jax.ShapeDtypeStruct((window, width), arrays[0].dtype)] * 2,
        compiler_params=pltpu.CompilerParams(vmem_limit_bytes=24 * 2**20),
        name="assemble",
    )(meta, *arrays)


def fold(value, op):
    parts = [value[i * 8 : (i + 1) * 8] for i in range(value.shape[0] // 8)]
    while len(parts) > 1:
        rest = [parts[-1]] if len(parts) % 2 else []
        parts = [op(a, b) for a, b in zip(parts[::2], parts[1::2])] + rest
    return parts[0]


def rows_of(tile):
    return pl.ds(pl.multiple_of(tile * TILE, TILE), TILE)


def attend_kernel(parts, pieces, meta_ref, *refs):
    outputs = len(parts) * pieces
    plan_refs, q_refs = refs[: len(parts)], refs[len(parts) : len(parts) + outputs]
    keys, values = refs[len(parts) + outputs : len(parts) + outputs + 2]
    out_refs = refs[-9 - outputs : -9]
    item_tile, item_slot, item_key, q_part, out_part, raw, peaks, acc, totals = refs[-9:]
    tokens = q_refs[0].shape[0]
    block = pieces * tokens
    block_tiles = block // TILE
    tiles = len(parts) * block_tiles
    slab_tiles, slots = plan_refs[0].shape[0], plan_refs[0].shape[1] - 1
    me, base = meta_ref[0], meta_ref[1]
    factor = HD**-0.5 * LOG2E

    def piece_rows(index, step):
        row = index * block + ((me % pieces) ^ step) * tokens
        return pl.ds(pl.multiple_of(row, 16), tokens)

    for index in range(len(parts)):
        for step in range(pieces):
            q_part[piece_rows(index, step)] = q_refs[index * pieces + step][...]
    acc[...] = jnp.zeros_like(acc)
    totals[...] = jnp.zeros_like(totals)

    total = jnp.int32(0)
    for index, part in enumerate(parts):
        plan_ref = plan_refs[index]
        first_row = (((me // pieces) ^ part) * block_tiles) % slab_tiles
        for tile in range(block_tiles):
            for slot in range(slots):
                item_tile[total + slot] = jnp.int32(index * block_tiles + tile)
                item_slot[total + slot] = jnp.int32(slot)
                item_key[total + slot] = plan_ref[first_row + tile, slot] - base
            total = total + plan_ref[first_row + tile, slots]
    for extra in range(UNROLL):
        item_tile[total + extra] = jnp.int32(tiles)
        item_slot[total + extra] = jnp.int32(0)
        item_key[total + extra] = jnp.int32(0)

    def score(item, buffer):
        tile = jnp.minimum(item_tile[item], tiles - 1)
        scores = lax.dot_general(
            keys[rows_of(item_key[item])],
            q_part[rows_of(tile)],
            (((1,), (1,)), ((), ())),
            preferred_element_type=jnp.float32,
        )
        raw[buffer] = scores
        peaks[buffer] = fold(scores, jnp.maximum)

    def gather(item, buffer, highest, sums):
        tile = item_tile[item]
        before = jnp.where(item_slot[item] == 0, -1e30, highest)
        highest = jnp.maximum(before, jnp.max(peaks[buffer], axis=0, keepdims=True))
        kept = jnp.exp2((before - highest) * factor)
        raised = jnp.exp2((raw[buffer] - highest) * factor)
        sums = sums * kept + jnp.sum(fold(raised, jnp.add), axis=0, keepdims=True)
        update = lax.dot_general(
            values[rows_of(item_key[item])],
            raised.astype(jnp.bfloat16),
            (((0,), (0,)), ((), ())),
            preferred_element_type=jnp.float32,
        )
        acc[tile] = acc[tile] * kept + update
        totals[tile] = sums
        return highest, sums

    score(0, 0)

    def body(i, carry):
        for step in range(UNROLL):
            item = i * UNROLL + step
            score(item + 1, (step + 1) % 2)
            carry = gather(item, step % 2, *carry)
        return carry

    blank = jnp.zeros((1, TILE), jnp.float32)
    lax.fori_loop(0, (total + UNROLL - 1) // UNROLL, body, (blank, blank))
    for tile in range(tiles):
        out_part[tile * TILE : (tile + 1) * TILE] = jnp.transpose(acc[tile] / totals[tile]).astype(
            out_part.dtype
        )
    for index in range(len(parts)):
        for step in range(pieces):
            out_refs[index * pieces + step][...] = out_part[piece_rows(index, step)]


def attend(meta, plans, queries, keys, values, parts, pieces):
    tokens, width = queries[0].shape
    dtype = queries[0].dtype
    rows = len(parts) * pieces * tokens
    tiles = rows // TILE
    items = tiles * (plans[0].shape[1] - 1) + UNROLL + 8
    outputs = len(parts) * pieces
    return pl.pallas_call(
        functools.partial(attend_kernel, parts, pieces),
        in_specs=[SMEM] * (1 + len(parts)) + [VMEM] * (outputs + 2),
        out_specs=[VMEM] * outputs,
        out_shape=[jax.ShapeDtypeStruct((tokens, width), dtype)] * outputs,
        scratch_shapes=[pltpu.SMEM((items,), jnp.int32)] * 3
        + [pltpu.VMEM((rows, width), dtype)] * 2
        + [
            pltpu.VMEM((2, TILE, TILE), jnp.float32),
            pltpu.VMEM((2, 8, TILE), jnp.float32),
            pltpu.VMEM((tiles + 1, HD, TILE), jnp.float32),
            pltpu.VMEM((tiles + 1, 1, TILE), jnp.float32),
        ],
        compiler_params=pltpu.CompilerParams(vmem_limit_bytes=20 * 2**20),
        cost_estimate=pl.CostEstimate(
            flops=16 * rows * TILE * HD, bytes_accessed=4 * rows * width, transcendentals=0
        ),
        name="attend",
    )(meta, *plans, *queries, keys, values)


def pieces_of(tokens):
    pieces = 1
    while pieces * tokens % TILE:
        pieces *= 2
    return pieces


def shards(group_size, queries, keys, values, tile_list, tile_count):
    groups = lax.axis_size("group")
    head_size = lax.axis_size("head")
    members = group_size * head_size
    tokens = queries.shape[0]
    slab_tiles = tile_list.shape[0]
    pieces = pieces_of(tokens)
    meta = jnp.stack(
        [
            lax.axis_index("member") * head_size + lax.axis_index("head"),
            (lax.axis_index("group") * group_size - 1) * slab_tiles,
        ]
    ).astype(jnp.int32)

    def swap(piece, step):
        if step == 0:
            return piece
        pairs = [(g * members + i, g * members + (i ^ step)) for g in range(groups) for i in range(members)]
        return lax.ppermute(piece, AXES, pairs)

    def relay(piece, step):
        pairs = []
        for g in range(groups):
            for i in range(members):
                member = (i ^ step) // head_size
                if member == group_size - 1 and g + 1 < groups:
                    pairs.append((g * members + i, (g + 1) * members + i))
                if member == 0 and g > 0:
                    pairs.append((g * members + i, (g - 1) * members + i))
        return lax.ppermute(piece, AXES, pairs)

    own_plan = jnp.concatenate([tile_list, tile_count[:, None]], axis=1)
    plans = [swap(own_plan, step * head_size) for step in range(group_size)]

    layout = layout_of(members)
    kv_split = split_heads(meta, keys, values, layout, members)
    swapped = {s: swap(array, s) for (s,), array in zip(layout, kv_split)}
    pieces_kv = [(array, None, step, False) for step, array in swapped.items()]
    for step in range(members // 4, members):
        beyond = relay(swapped[step], step)
        pieces_kv.append((beyond, None, step, True))
    for step in range(0, members // 4, 2):
        pair = pack(swapped[step], swapped[step + 1])
        beyond = relay(pair, step)
        pieces_kv += [(beyond, inner, step + inner, True) for inner in range(2)]

    q_split = split_queries(meta, [queries], members)
    q_pieces = [swap(piece[0], step) for step, piece in enumerate(q_split)]
    window_keys, window_values = assemble(meta, pieces_kv, members, head_size)

    results = [None] * members
    for parts in calls_of(members // pieces):
        outputs = attend(
            meta,
            [plans[part * pieces // head_size] for part in parts],
            [q_pieces[part * pieces + step] for part in parts for step in range(pieces)],
            window_keys,
            window_values,
            parts,
            pieces,
        )
        steps = [part * pieces + step for part in parts for step in range(pieces)]
        for step, output in zip(steps, outputs):
            results[step] = swap(output, step)
    return join_heads(meta, results)


def calls_of(parts):
    return [(parts - 1,), tuple(range(parts - 2, 0, -1)), (0,)]


def layout_of(members):
    half = members // 2
    return [(s,) for s in [*range(members - 1, half - 1, -1), *range(half // 2, half), *range(half // 2)]]


def solution(mesh):
    tm_size, head_size = mesh.shape["tm"], mesh.shape["head"]

    def run(queries, keys, values, tile_list, tile_count):
        group_size = queries.shape[1] // HD // head_size
        members = group_size * head_size
        if group_size < 2 or tm_size % group_size or members & (members - 1):
            raise ValueError("unsupported mesh")
        fine = Mesh(mesh.devices.reshape(tm_size // group_size, group_size, head_size), AXES)
        tokens_spec = P(AXES, None)
        step = jax.shard_map(
            functools.partial(shards, group_size),
            mesh=fine,
            in_specs=(
                tokens_spec,
                tokens_spec,
                tokens_spec,
                P(("group", "member"), None),
                P(("group", "member")),
            ),
            out_specs=tokens_spec,
            check_vma=False,
        )
        return step(queries, keys, values, tile_list, tile_count)

    return run
```

profile of v0, /device:TPU:17, one launch (start us, length us, event | category | flops | bytes accessed | tf_op | source)
XLA Modules:
  0.0 104.0 jit_solution(13526965114885566177)
XLA Ops:
  0.0 0.1 pad_add_fusion.1.meta_ref
  0.1 1.3 %copy-done.2 = bf16[576,1024]{1,0:T(8,128)(2,1)S(1)} copy-done((bf16[576,1024]{1,0:T(8,128)(2,1)S(1)}, bf16[576,1024]{1,0:T(8,128)(2,1)}, u32[]{:S(2)}) %copy-start.2) | copy-done | bytes 1179672
  1.3 2.6 %split_queries.1 = (bf16[1,576,128]{2,1,0:T(8,128)(2,1)S(1)}, bf16[1,576,128]{2,1,0:T(8,128)(2,1)S(1)}, bf16[1,576,128]{2,1,0:T(8,128)(2,1)S(1)}, bf16[1,576,128...) custom-call(s32[2]{0:T(128)S(1)} %pad_add_fusion.1.meta_ref, ...), custom_call_target="tpu_custom_call" | custom-call | tf_op jit(solution)/shard_map/split_queries/pallas_call | solution.py:54
  4.0 2.2 %collective-permute-start.25 = (bf16[576,128]{1,0:T(8,128)(2,1)S(1)}, bf16[576,128]{1,0:T(8,128)(2,1)S(1)}, u32[]{:S(2)}, u32[]{:S(2)}) collective-permute-start(bf16[576,128]{1,0:T(8,128)(2,1)S(1)} %bitcast.18), channel_id=1, source_target_pairs={{0,6},{1,7},{2,4},{3,5},{4,2},{5,3},{6,0},{7,1},{8,14},{9,15},{10,... | collective-permute-start | bytes 442376 | tf_op jit(solution)/shard_map/ppermute | solution.py:346
  6.2 3.4 %split_heads.1 = (bf16[2,576,128]{2,1,0:T(8,128)(2,1)}, bf16[2,576,128]{2,1,0:T(8,128)(2,1)}, bf16[2,576,128]{2,1,0:T(8,128)(2,1)}, bf16[2,576,128]{2,1,0:T(8,12...) custom-call(s32[2]{0:T(128)} %copy-done.3, ...), custom_call_target="tpu_custom_call" | custom-call | tf_op jit(solution)/shard_map/split_heads/pallas_call | solution.py:101
  9.6 1.0 collective-permute-start.7
  10.6 0.3 collective-permute-start.4
  10.8 0.1 copy.6
  11.0 1.2 %collective-permute-start.16 = (s32[6,8]{1,0:T(8,128)S(1)}, s32[6,8]{1,0:T(8,128)S(1)}, u32[]{:S(2)}, u32[]{:S(2)}) collective-permute-start(s32[6,8]{1,0:T(8,128)S(1)} %pad_add_fusion.refs_0_.refs_1_), channel_id=1, source_target_pairs={{0,4},{1,5},{2,6},{3,7},{4,0},{5,1},{6,2},{7,3},{8,12},{9,13},{10,... | collective-permute-start | bytes 584 | tf_op jit(solution)/shard_map/ppermute | solution.py:346
  12.2 0.8 collective-permute-start.3
  13.0 6.4 %collective-permute-done.16.refs_0_ = s32[6,8]{1,0:T(8,128)S(1)} collective-permute-done((s32[6,8]{1,0:T(8,128)S(1)}, s32[6,8]{1,0:T(8,128)S(1)}, u32[]{:S(2)}, u32[]{:S(2)}) %collective-permute-start.16) | collective-permute-done | bytes 224 | tf_op jit(solution)/shard_map/ppermute | solution.py:346
  19.4 0.2 collective-permute-start.2
  19.6 3.8 %collective-permute-start.1 = (bf16[2,576,128]{2,1,0:T(8,128)(2,1)}, bf16[2,576,128]{2,1,0:T(8,128)(2,1)S(1)}, u32[]{:S(2)}, u32[]{:S(2)}) collective-permute-start(bf16[2,576,128]{2,1,0:T(8,128)(2,1)} %get-tuple-element.33), channel_id=1, source_target_pairs={{0,7},{1,6},{2,5},{3,4},{4,3},{5,2},{6,1},{7,0},{8,15},{9,14},{10,... | collective-permute-start | bytes 884744 | tf_op jit(solution)/shard_map/ppermute | solution.py:346
  23.4 0.2 collective-permute-start.5
  23.6 0.2 collective-permute-start.6
  23.8 3.0 %collective-permute-done.3.refs_2_ = bf16[2,576,128]{2,1,0:T(8,128)(2,1)S(1)} collective-permute-done((bf16[2,576,128]{2,1,0:T(8,128)(2,1)}, bf16[2,576,128]{2,1,0:T(8,128)(2,1)S(1)}, u32[]{:S(2)}, u32[]{:S(2)}) %collective-permute-start.3) | collective-permute-done | bytes 294944 | tf_op jit(solution)/shard_map/ppermute | solution.py:346
  26.8 3.2 %collective-permute-start.10 = (bf16[2,576,128]{2,1,0:T(8,128)(2,1)S(1)}, bf16[2,576,128]{2,1,0:T(8,128)(2,1)S(1)}, u32[]{:S(2)}, u32[]{:S(2)}) collective-permute-start(bf16[2,576,128]{2,1,0:T(8,128)(2,1)S(1)} %collective-permute-done.4.refs_3_), channel_id=1, source_target_pairs={{0,8},{1,9},{2,10},{3,11},{8,16},{9,17},{10,18},{11,19},{12,4},{13... | collective-permute-start | bytes 884744 | tf_op jit(solution)/shard_map/ppermute | solution.py:357
  30.0 2.0 %collective-permute-done.2.refs_1_ = bf16[2,576,128]{2,1,0:T(8,128)(2,1)S(1)} collective-permute-done((bf16[2,576,128]{2,1,0:T(8,128)(2,1)}, bf16[2,576,128]{2,1,0:T(8,128)(2,1)S(1)}, u32[]{:S(2)}, u32[]{:S(2)}) %collective-permute-start.2) | collective-permute-done | bytes 294944 | tf_op jit(solution)/shard_map/ppermute | solution.py:346
  32.0 3.2 %collective-permute-start.11 = (bf16[2,576,128]{2,1,0:T(8,128)(2,1)S(1)}, bf16[2,576,128]{2,1,0:T(8,128)(2,1)S(1)}, u32[]{:S(2)}, u32[]{:S(2)}) collective-permute-start(bf16[2,576,128]{2,1,0:T(8,128)(2,1)S(1)} %collective-permute-done.3.refs_2_), channel_id=1, source_target_pairs={{0,8},{1,9},{2,10},{3,11},{8,16},{9,17},{10,18},{11,19},{12,4},{13... | collective-permute-start | bytes 884744 | tf_op jit(solution)/shard_map/ppermute | solution.py:357
  35.2 1.0 copy-done
  36.2 2.4 %collective-permute-done.1.refs_0_ = bf16[2,576,128]{2,1,0:T(8,128)(2,1)S(1)} collective-permute-done((bf16[2,576,128]{2,1,0:T(8,128)(2,1)}, bf16[2,576,128]{2,1,0:T(8,128)(2,1)S(1)}, u32[]{:S(2)}, u32[]{:S(2)}) %collective-permute-start.1) | collective-permute-done | bytes 294944 | tf_op jit(solution)/shard_map/ppermute | solution.py:346
  38.6 2.1 %collective-permute-start.14 = (bf16[2,2,576,128]{3,2,1,0:T(8,128)(2,1)S(1)}, bf16[2,2,576,128]{3,2,1,0:T(8,128)(2,1)S(1)}, u32[]{:S(2)}, u32[]{:S(2)}) collective-permute-start(bf16[2,2,576,128]{3,2,1,0:T(8,128)(2,1)S(1)} %pack.1), channel_id=1, source_target_pairs={{4,12},{5,13},{6,14},{7,15},{8,0},{9,1},{10,2},{11,3},{12,20},{13,... | collective-permute-start | bytes 1769480 | tf_op jit(solution)/shard_map/ppermute | solution.py:357
  40.7 4.2 %collective-permute-done.5.refs_4_ = bf16[2,576,128]{2,1,0:T(8,128)(2,1)S(1)} collective-permute-done((bf16[2,576,128]{2,1,0:T(8,128)(2,1)}, bf16[2,576,128]{2,1,0:T(8,128)(2,1)S(1)}, u32[]{:S(2)}, u32[]{:S(2)}) %collective-permute-start.5) | collective-permute-done | bytes 294944 | tf_op jit(solution)/shard_map/ppermute | solution.py:346
  44.9 2.9 %collective-permute-start.12 = (bf16[2,576,128]{2,1,0:T(8,128)(2,1)S(1)}, bf16[2,576,128]{2,1,0:T(8,128)(2,1)S(1)}, u32[]{:S(2)}, u32[]{:S(2)}) collective-permute-start(bf16[2,576,128]{2,1,0:T(8,128)(2,1)S(1)} %collective-permute-done.2.refs_1_), channel_id=1, source_target_pairs={{0,8},{1,9},{2,10},{3,11},{8,16},{9,17},{10,18},{11,19},{12,4},{13... | collective-permute-start | bytes 884744 | tf_op jit(solution)/shard_map/ppermute | solution.py:357
  47.8 2.5 %collective-permute-done.6.refs_5_ = bf16[2,576,128]{2,1,0:T(8,128)(2,1)S(1)} collective-permute-done((bf16[2,576,128]{2,1,0:T(8,128)(2,1)}, bf16[2,576,128]{2,1,0:T(8,128)(2,1)S(1)}, u32[]{:S(2)}, u32[]{:S(2)}) %collective-permute-start.6) | collective-permute-done | bytes 294944 | tf_op jit(solution)/shard_map/ppermute | solution.py:346
  50.3 3.2 %collective-permute-start.13 = (bf16[2,576,128]{2,1,0:T(8,128)(2,1)S(1)}, bf16[2,576,128]{2,1,0:T(8,128)(2,1)S(1)}, u32[]{:S(2)}, u32[]{:S(2)}) collective-permute-start(bf16[2,576,128]{2,1,0:T(8,128)(2,1)S(1)} %collective-permute-done.1.refs_0_), channel_id=1, source_target_pairs={{0,8},{1,9},{2,10},{3,11},{8,16},{9,17},{10,18},{11,19},{12,4},{13... | collective-permute-start | bytes 884744 | tf_op jit(solution)/shard_map/ppermute | solution.py:357
  53.6 2.1 %collective-permute-start.8 = (bf16[2,576,128]{2,1,0:T(8,128)(2,1)S(1)}, bf16[2,576,128]{2,1,0:T(8,128)(2,1)S(1)}, u32[]{:S(2)}, u32[]{:S(2)}) collective-permute-start(bf16[2,576,128]{2,1,0:T(8,128)(2,1)S(1)} %collective-permute-done.5.refs_4_), channel_id=1, source_target_pairs={{4,12},{5,13},{6,14},{7,15},{8,0},{9,1},{10,2},{11,3},{12,20},{13,... | collective-permute-start | bytes 884744 | tf_op jit(solution)/shard_map/ppermute | solution.py:357
  55.6 2.1 %collective-permute-start.9 = (bf16[2,576,128]{2,1,0:T(8,128)(2,1)S(1)}, bf16[2,576,128]{2,1,0:T(8,128)(2,1)S(1)}, u32[]{:S(2)}, u32[]{:S(2)}) collective-permute-start(bf16[2,576,128]{2,1,0:T(8,128)(2,1)S(1)} %collective-permute-done.6.refs_5_), channel_id=1, source_target_pairs={{4,12},{5,13},{6,14},{7,15},{8,0},{9,1},{10,2},{11,3},{12,20},{13,... | collective-permute-start | bytes 884744 | tf_op jit(solution)/shard_map/ppermute | solution.py:357
  57.8 1.8 %collective-permute-start.26 = (bf16[576,128]{1,0:T(8,128)(2,1)S(1)}, bf16[576,128]{1,0:T(8,128)(2,1)S(1)}, u32[]{:S(2)}, u32[]{:S(2)}) collective-permute-start(bf16[576,128]{1,0:T(8,128)(2,1)S(1)} %bitcast.17), channel_id=1, source_target_pairs={{0,7},{1,6},{2,5},{3,4},{4,3},{5,2},{6,1},{7,0},{8,15},{9,14},{10,... | collective-permute-start | bytes 442376 | tf_op jit(solution)/shard_map/ppermute | solution.py:346
  59.5 2.1 %collective-permute-done.13.refs_13_ = bf16[2,576,128]{2,1,0:T(8,128)(2,1)S(1)} collective-permute-done((bf16[2,576,128]{2,1,0:T(8,128)(2,1)S(1)}, bf16[2,576,128]{2,1,0:T(8,128)(2,1)S(1)}, u32[]{:S(2)}, u32[]{:S(2)}) %collective-permute-start.13) | collective-permute-done | bytes 294944 | tf_op jit(solution)/shard_map/ppermute | solution.py:357
  61.6 0.2 collective-permute-start.17
  61.8 1.0 %collective-permute-done.8.refs_8_ = bf16[2,576,128]{2,1,0:T(8,128)(2,1)S(1)} collective-permute-done((bf16[2,576,128]{2,1,0:T(8,128)(2,1)S(1)}, bf16[2,576,128]{2,1,0:T(8,128)(2,1)S(1)}, u32[]{:S(2)}, u32[]{:S(2)}) %collective-permute-start.8) | collective-permute-done | bytes 294944 | tf_op jit(solution)/shard_map/ppermute | solution.py:357
  62.9 2.8 %collective-permute-start.18 = (bf16[576,128]{1,0:T(8,128)(2,1)S(1)}, bf16[576,128]{1,0:T(8,128)(2,1)S(1)}, u32[]{:S(2)}, u32[]{:S(2)}) collective-permute-start(bf16[576,128]{1,0:T(8,128)(2,1)S(1)} %bitcast.15), channel_id=1, source_target_pairs={{0,5},{1,4},{2,7},{3,6},{4,1},{5,0},{6,3},{7,2},{8,13},{9,12},{10,... | collective-permute-start | bytes 442376 | tf_op jit(solution)/shard_map/ppermute | solution.py:346
  65.6 3.6 %collective-permute-done.9.refs_9_ = bf16[2,576,128]{2,1,0:T(8,128)(2,1)S(1)} collective-permute-done((bf16[2,576,128]{2,1,0:T(8,128)(2,1)S(1)}, bf16[2,576,128]{2,1,0:T(8,128)(2,1)S(1)}, u32[]{:S(2)}, u32[]{:S(2)}) %collective-permute-start.9) | collective-permute-done | bytes 294944 | tf_op jit(solution)/shard_map/ppermute | solution.py:357
  69.2 0.4 collective-permute-start.19
  69.6 3.2 %collective-permute-start.20 = (bf16[576,128]{1,0:T(8,128)(2,1)S(1)}, bf16[576,128]{1,0:T(8,128)(2,1)S(1)}, u32[]{:S(2)}, u32[]{:S(2)}) collective-permute-start(bf16[576,128]{1,0:T(8,128)(2,1)S(1)} %bitcast.13), channel_id=1, source_target_pairs={{0,3},{1,2},{2,1},{3,0},{4,7},{5,6},{6,5},{7,4},{8,11},{9,10},{10,... | collective-permute-start | bytes 442376 | tf_op jit(solution)/shard_map/ppermute | solution.py:346
  72.8 0.9 assemble.1
  73.8 4.0 %attend.5 = (bf16[576,128]{1,0:T(8,128)(2,1)S(1)}, bf16[576,128]{1,0:T(8,128)(2,1)S(1)}) custom-call(s32[2]{0:T(128)S(1)} %copy-done.4, s32[6,8]{1,0:T(8,128)S(1)} %collective-permute-done.16.refs_0_, bf16[576,128]{1,0:T(8,128)(2,1)S(1)} %collective-permute-done.25.refs_1_, bf16[576,128]{1,0:T(8,128)(2,1)S(1)} %collective-permute-done.26.refs_2_, ...), custom_call_target="tpu_custom_call" | custom-call | flops 905969664 | bytes 589824 | tf_op jit(solution)/shard_map/attend/pallas_call | solution.py:300
  77.8 2.2 %collective-permute-start.27 = (bf16[576,128]{1,0:T(8,128)(2,1)S(1)}, bf16[576,128]{1,0:T(8,128)(2,1)S(1)}, u32[]{:S(2)}, u32[]{:S(2)}) collective-permute-start(bf16[576,128]{1,0:T(8,128)(2,1)S(1)} %get-tuple-element.55), channel_id=1, source_target_pairs={{0,6},{1,7},{2,4},{3,5},{4,2},{5,3},{6,0},{7,1},{8,14},{9,15},{10,... | collective-permute-start | bytes 442376 | tf_op jit(solution)/shard_map/ppermute | solution.py:346
  80.0 0.8 collective-permute-start.28
  80.8 6.9 %attend.4 = (bf16[576,128]{1,0:T(8,128)(2,1)S(1)}, bf16[576,128]{1,0:T(8,128)(2,1)S(1)}, bf16[576,128]{1,0:T(8,128)(2,1)S(1)}, bf16[576,128]{1,0:T(8,128)(2,1)S(1)}) custom-call(s32[2]{0:T(128)S(1)} %copy-done.4, s32[6,8]{1,0:T(8,128)S(1)} %collective-permute-done.16.refs_0_, s32[6,8]{1,0:T(8,128)S(1)} %pad_add_fusion.refs_0_.refs_1_, ...), custom_call_target="tpu_custom_call" | custom-call | flops 1811939328 | bytes 1179648 | tf_op jit(solution)/shard_map/attend/pallas_call | solution.py:300
  87.8 2.4 %collective-permute-start.21 = (bf16[576,128]{1,0:T(8,128)(2,1)S(1)}, bf16[576,128]{1,0:T(8,128)(2,1)S(1)}, u32[]{:S(2)}, u32[]{:S(2)}) collective-permute-start(bf16[576,128]{1,0:T(8,128)(2,1)S(1)} %get-tuple-element.49), channel_id=1, source_target_pairs={{0,2},{1,3},{2,0},{3,1},{4,6},{5,7},{6,4},{7,5},{8,10},{9,11},{10,... | collective-permute-start | bytes 442376 | tf_op jit(solution)/shard_map/ppermute | solution.py:346
  90.1 0.6 collective-permute-start.23
  90.7 5.8 %attend.3 = (bf16[576,128]{1,0:T(8,128)(2,1)S(1)}, bf16[576,128]{1,0:T(8,128)(2,1)S(1)}) custom-call(s32[2]{0:T(128)S(1)} %copy-done.4, s32[6,8]{1,0:T(8,128)S(1)} %pad_add_fusion.refs_0_.refs_1_, bf16[576,128]{1,0:T(8,128)(2,1)S(1)} %bitcast.11, bf16[576,128]{1,0:T(8,128)(2,1)S(1)} %collective-permute-done.refs_2_, ...), custom_call_target="tpu_custom_call" | custom-call | flops 905969664 | bytes 589824 | tf_op jit(solution)/shard_map/attend/pallas_call | solution.py:300
  96.5 0.6 collective-permute-start.24
  97.2 0.4 collective-permute-done.22.refs_3_
  97.6 4.8 %collective-permute-done.24.refs_5_ = bf16[576,128]{1,0:T(8,128)(2,1)S(1)} collective-permute-done((bf16[576,128]{1,0:T(8,128)(2,1)S(1)}, bf16[576,128]{1,0:T(8,128)(2,1)S(1)}, u32[]{:S(2)}, u32[]{:S(2)}) %collective-permute-start.24) | collective-permute-done | bytes 147488 | tf_op jit(solution)/shard_map/ppermute | solution.py:346
  102.3 1.6 %join_heads.1 = bf16[576,1024]{1,0:T(8,128)(2,1)} custom-call(s32[2]{0:T(128)S(1)} %copy-done.4, bf16[576,128]{1,0:T(8,128)(2,1)S(1)} %get-tuple-element.43.refs_0_, bf16[576,128]{1,0:T(8,128)(2,1)S(1)} %collective-permute-done.15.refs_1_, bf16[576,128]{1,0:T(8,128)(2,1)S(1)} %collective-permute-done.21.refs_2_, ...), custom_call_target="tpu_custom_call" | custom-call | tf_op jit(solution)/shard_map/join_heads/pallas_call | solution.py:134
  (35 shorter events, 0.3 us)
Async XLA Ops:
  0.1 1.3 %copy-start.2 = (bf16[576,1024]{1,0:T(8,128)(2,1)S(1)}, bf16[576,1024]{1,0:T(8,128)(2,1)}, u32[]{:S(2)}) copy-start(bf16[576,1024]{1,0:T(8,128)(2,1)} %refs_0_.2) | copy-start | bytes 3538948
  1.3 4.8 %copy-start.3 = (s32[2]{0:T(128)}, s32[2]{0:T(128)S(1)}, u32[]{:S(2)}) copy-start(s32[2]{0:T(128)S(1)} %pad_add_fusion.1.meta_ref) | copy-start | bytes 28
  3.9 6.9 %copy-start.6 = (s32[6]{0:T(128)S(1)}, s32[6]{0:T(128)}, u32[]{:S(2)}) copy-start(s32[6]{0:T(128)} %param.9) | copy-start | bytes 76
  3.9 7.0 %copy-start.5 = (s32[6,7]{1,0:T(8,128)S(1)}, s32[6,7]{1,0:T(8,128)}, u32[]{:S(2)}) copy-start(s32[6,7]{1,0:T(8,128)} %param.8) | copy-start | bytes 508
  4.0 15.6 %collective-permute-start.25 = (bf16[576,128]{1,0:T(8,128)(2,1)S(1)}, bf16[576,128]{1,0:T(8,128)(2,1)S(1)}, u32[]{:S(2)}, u32[]{:S(2)}) collective-permute-start(bf16[576,128]{1,0:T(8,128)(2,1)S(1)} %bitcast.18), channel_id=1, source_target_pairs={{0,6},{1,7},{2,4},{3,5},{4,2},{5,3},{6,0},{7,1},{8,14},{9,15},{10,... | collective-permute-start | bytes 442376 | tf_op jit(solution)/shard_map/ppermute | solution.py:346
  9.6 63.3 %copy-start.4 = (s32[2]{0:T(128)S(1)}, s32[2]{0:T(128)}, u32[]{:S(2)}) copy-start(s32[2]{0:T(128)} %copy-done.3) | copy-start | bytes 28
  9.6 13.8 %collective-permute-start.7 = (bf16[2,576,128]{2,1,0:T(8,128)(2,1)}, bf16[2,576,128]{2,1,0:T(8,128)(2,1)S(1)}, u32[]{:S(2)}, u32[]{:S(2)}) collective-permute-start(bf16[2,576,128]{2,1,0:T(8,128)(2,1)} %get-tuple-element.40), channel_id=1, source_target_pairs={{0,1},{1,0},{2,3},{3,2},{4,5},{5,4},{6,7},{7,6},{8,9},{9,8},{10,11... | collective-permute-start | bytes 884744 | tf_op jit(solution)/shard_map/ppermute | solution.py:346
  10.6 13.0 %collective-permute-start.4 = (bf16[2,576,128]{2,1,0:T(8,128)(2,1)}, bf16[2,576,128]{2,1,0:T(8,128)(2,1)S(1)}, u32[]{:S(2)}, u32[]{:S(2)}) collective-permute-start(bf16[2,576,128]{2,1,0:T(8,128)(2,1)} %get-tuple-element.36), channel_id=1, source_target_pairs={{0,4},{1,5},{2,6},{3,7},{4,0},{5,1},{6,2},{7,3},{8,12},{9,13},{10,... | collective-permute-start | bytes 884744 | tf_op jit(solution)/shard_map/ppermute | solution.py:346
  11.0 8.4 %collective-permute-start.16 = (s32[6,8]{1,0:T(8,128)S(1)}, s32[6,8]{1,0:T(8,128)S(1)}, u32[]{:S(2)}, u32[]{:S(2)}) collective-permute-start(s32[6,8]{1,0:T(8,128)S(1)} %pad_add_fusion.refs_0_.refs_1_), channel_id=1, source_target_pairs={{0,4},{1,5},{2,6},{3,7},{4,0},{5,1},{6,2},{7,3},{8,12},{9,13},{10,... | collective-permute-start | bytes 584 | tf_op jit(solution)/shard_map/ppermute | solution.py:346
  12.2 14.5 %collective-permute-start.3 = (bf16[2,576,128]{2,1,0:T(8,128)(2,1)}, bf16[2,576,128]{2,1,0:T(8,128)(2,1)S(1)}, u32[]{:S(2)}, u32[]{:S(2)}) collective-permute-start(bf16[2,576,128]{2,1,0:T(8,128)(2,1)} %get-tuple-element.35), channel_id=1, source_target_pairs={{0,5},{1,4},{2,7},{3,6},{4,1},{5,0},{6,3},{7,2},{8,13},{9,12},{10,... | collective-permute-start | bytes 884744 | tf_op jit(solution)/shard_map/ppermute | solution.py:346
  19.4 12.6 %collective-permute-start.2 = (bf16[2,576,128]{2,1,0:T(8,128)(2,1)}, bf16[2,576,128]{2,1,0:T(8,128)(2,1)S(1)}, u32[]{:S(2)}, u32[]{:S(2)}) collective-permute-start(bf16[2,576,128]{2,1,0:T(8,128)(2,1)} %get-tuple-element.34), channel_id=1, source_target_pairs={{0,6},{1,7},{2,4},{3,5},{4,2},{5,3},{6,0},{7,1},{8,14},{9,15},{10,... | collective-permute-start | bytes 884744 | tf_op jit(solution)/shard_map/ppermute | solution.py:346
  19.6 19.0 %collective-permute-start.1 = (bf16[2,576,128]{2,1,0:T(8,128)(2,1)}, bf16[2,576,128]{2,1,0:T(8,128)(2,1)S(1)}, u32[]{:S(2)}, u32[]{:S(2)}) collective-permute-start(bf16[2,576,128]{2,1,0:T(8,128)(2,1)} %get-tuple-element.33), channel_id=1, source_target_pairs={{0,7},{1,6},{2,5},{3,4},{4,3},{5,2},{6,1},{7,0},{8,15},{9,14},{10,... | collective-permute-start | bytes 884744 | tf_op jit(solution)/shard_map/ppermute | solution.py:346
  23.4 21.5 %collective-permute-start.5 = (bf16[2,576,128]{2,1,0:T(8,128)(2,1)}, bf16[2,576,128]{2,1,0:T(8,128)(2,1)S(1)}, u32[]{:S(2)}, u32[]{:S(2)}) collective-permute-start(bf16[2,576,128]{2,1,0:T(8,128)(2,1)} %get-tuple-element.37), channel_id=1, source_target_pairs={{0,2},{1,3},{2,0},{3,1},{4,6},{5,7},{6,4},{7,5},{8,10},{9,11},{10,... | collective-permute-start | bytes 884744 | tf_op jit(solution)/shard_map/ppermute | solution.py:346
  23.6 26.7 %collective-permute-start.6 = (bf16[2,576,128]{2,1,0:T(8,128)(2,1)}, bf16[2,576,128]{2,1,0:T(8,128)(2,1)S(1)}, u32[]{:S(2)}, u32[]{:S(2)}) collective-permute-start(bf16[2,576,128]{2,1,0:T(8,128)(2,1)} %get-tuple-element.38), channel_id=1, source_target_pairs={{0,3},{1,2},{2,1},{3,0},{4,7},{5,6},{6,5},{7,4},{8,11},{9,10},{10,... | collective-permute-start | bytes 884744 | tf_op jit(solution)/shard_map/ppermute | solution.py:346
  26.8 26.8 %collective-permute-start.10 = (bf16[2,576,128]{2,1,0:T(8,128)(2,1)S(1)}, bf16[2,576,128]{2,1,0:T(8,128)(2,1)S(1)}, u32[]{:S(2)}, u32[]{:S(2)}) collective-permute-start(bf16[2,576,128]{2,1,0:T(8,128)(2,1)S(1)} %collective-permute-done.4.refs_3_), channel_id=1, source_target_pairs={{0,8},{1,9},{2,10},{3,11},{8,16},{9,17},{10,18},{11,19},{12,4},{13... | collective-permute-start | bytes 884744 | tf_op jit(solution)/shard_map/ppermute | solution.py:357
  32.0 23.6 %collective-permute-start.11 = (bf16[2,576,128]{2,1,0:T(8,128)(2,1)S(1)}, bf16[2,576,128]{2,1,0:T(8,128)(2,1)S(1)}, u32[]{:S(2)}, u32[]{:S(2)}) collective-permute-start(bf16[2,576,128]{2,1,0:T(8,128)(2,1)S(1)} %collective-permute-done.3.refs_2_), channel_id=1, source_target_pairs={{0,8},{1,9},{2,10},{3,11},{8,16},{9,17},{10,18},{11,19},{12,4},{13... | collective-permute-start | bytes 884744 | tf_op jit(solution)/shard_map/ppermute | solution.py:357
  35.2 1.0 copy-start
  36.2 36.7 %copy-start.1 = (bf16[2,576,128]{2,1,0:T(8,128)(2,1)S(1)}, bf16[2,576,128]{2,1,0:T(8,128)(2,1)}, u32[]{:S(2)}) copy-start(bf16[2,576,128]{2,1,0:T(8,128)(2,1)} %get-tuple-element.39.first.refs_6_) | copy-start | bytes 884740
  38.6 31.0 %collective-permute-start.14 = (bf16[2,2,576,128]{3,2,1,0:T(8,128)(2,1)S(1)}, bf16[2,2,576,128]{3,2,1,0:T(8,128)(2,1)S(1)}, u32[]{:S(2)}, u32[]{:S(2)}) collective-permute-start(bf16[2,2,576,128]{3,2,1,0:T(8,128)(2,1)S(1)} %pack.1), channel_id=1, source_target_pairs={{4,12},{5,13},{6,14},{7,15},{8,0},{9,1},{10,2},{11,3},{12,20},{13,... | collective-permute-start | bytes 1769480 | tf_op jit(solution)/shard_map/ppermute | solution.py:357
  44.9 12.8 %collective-permute-start.12 = (bf16[2,576,128]{2,1,0:T(8,128)(2,1)S(1)}, bf16[2,576,128]{2,1,0:T(8,128)(2,1)S(1)}, u32[]{:S(2)}, u32[]{:S(2)}) collective-permute-start(bf16[2,576,128]{2,1,0:T(8,128)(2,1)S(1)} %collective-permute-done.2.refs_1_), channel_id=1, source_target_pairs={{0,8},{1,9},{2,10},{3,11},{8,16},{9,17},{10,18},{11,19},{12,4},{13... | collective-permute-start | bytes 884744 | tf_op jit(solution)/shard_map/ppermute | solution.py:357
  50.3 11.3 %collective-permute-start.13 = (bf16[2,576,128]{2,1,0:T(8,128)(2,1)S(1)}, bf16[2,576,128]{2,1,0:T(8,128)(2,1)S(1)}, u32[]{:S(2)}, u32[]{:S(2)}) collective-permute-start(bf16[2,576,128]{2,1,0:T(8,128)(2,1)S(1)} %collective-permute-done.1.refs_0_), channel_id=1, source_target_pairs={{0,8},{1,9},{2,10},{3,11},{8,16},{9,17},{10,18},{11,19},{12,4},{13... | collective-permute-start | bytes 884744 | tf_op jit(solution)/shard_map/ppermute | solution.py:357
  53.6 9.3 %collective-permute-start.8 = (bf16[2,576,128]{2,1,0:T(8,128)(2,1)S(1)}, bf16[2,576,128]{2,1,0:T(8,128)(2,1)S(1)}, u32[]{:S(2)}, u32[]{:S(2)}) collective-permute-start(bf16[2,576,128]{2,1,0:T(8,128)(2,1)S(1)} %collective-permute-done.5.refs_4_), channel_id=1, source_target_pairs={{4,12},{5,13},{6,14},{7,15},{8,0},{9,1},{10,2},{11,3},{12,20},{13,... | collective-permute-start | bytes 884744 | tf_op jit(solution)/shard_map/ppermute | solution.py:357
  55.6 13.6 %collective-permute-start.9 = (bf16[2,576,128]{2,1,0:T(8,128)(2,1)S(1)}, bf16[2,576,128]{2,1,0:T(8,128)(2,1)S(1)}, u32[]{:S(2)}, u32[]{:S(2)}) collective-permute-start(bf16[2,576,128]{2,1,0:T(8,128)(2,1)S(1)} %collective-permute-done.6.refs_5_), channel_id=1, source_target_pairs={{4,12},{5,13},{6,14},{7,15},{8,0},{9,1},{10,2},{11,3},{12,20},{13,... | collective-permute-start | bytes 884744 | tf_op jit(solution)/shard_map/ppermute | solution.py:357
  57.8 15.9 %collective-permute-start.26 = (bf16[576,128]{1,0:T(8,128)(2,1)S(1)}, bf16[576,128]{1,0:T(8,128)(2,1)S(1)}, u32[]{:S(2)}, u32[]{:S(2)}) collective-permute-start(bf16[576,128]{1,0:T(8,128)(2,1)S(1)} %bitcast.17), channel_id=1, source_target_pairs={{0,7},{1,6},{2,5},{3,4},{4,3},{5,2},{6,1},{7,0},{8,15},{9,14},{10,... | collective-permute-start | bytes 442376 | tf_op jit(solution)/shard_map/ppermute | solution.py:346
  61.6 16.1 %collective-permute-start.17 = (bf16[576,128]{1,0:T(8,128)(2,1)S(1)}, bf16[576,128]{1,0:T(8,128)(2,1)S(1)}, u32[]{:S(2)}, u32[]{:S(2)}) collective-permute-start(bf16[576,128]{1,0:T(8,128)(2,1)S(1)} %bitcast.16), channel_id=1, source_target_pairs={{0,4},{1,5},{2,6},{3,7},{4,0},{5,1},{6,2},{7,3},{8,12},{9,13},{10,... | collective-permute-start | bytes 442376 | tf_op jit(solution)/shard_map/ppermute | solution.py:346
  62.9 17.1 %collective-permute-start.18 = (bf16[576,128]{1,0:T(8,128)(2,1)S(1)}, bf16[576,128]{1,0:T(8,128)(2,1)S(1)}, u32[]{:S(2)}, u32[]{:S(2)}) collective-permute-start(bf16[576,128]{1,0:T(8,128)(2,1)S(1)} %bitcast.15), channel_id=1, source_target_pairs={{0,5},{1,4},{2,7},{3,6},{4,1},{5,0},{6,3},{7,2},{8,13},{9,12},{10,... | collective-permute-start | bytes 442376 | tf_op jit(solution)/shard_map/ppermute | solution.py:346
  69.2 11.6 %collective-permute-start.19 = (bf16[576,128]{1,0:T(8,128)(2,1)S(1)}, bf16[576,128]{1,0:T(8,128)(2,1)S(1)}, u32[]{:S(2)}, u32[]{:S(2)}) collective-permute-start(bf16[576,128]{1,0:T(8,128)(2,1)S(1)} %bitcast.14), channel_id=1, source_target_pairs={{0,2},{1,3},{2,0},{3,1},{4,6},{5,7},{6,4},{7,5},{8,10},{9,11},{10,... | collective-permute-start | bytes 442376 | tf_op jit(solution)/shard_map/ppermute | solution.py:346
  69.6 11.2 %collective-permute-start.20 = (bf16[576,128]{1,0:T(8,128)(2,1)S(1)}, bf16[576,128]{1,0:T(8,128)(2,1)S(1)}, u32[]{:S(2)}, u32[]{:S(2)}) collective-permute-start(bf16[576,128]{1,0:T(8,128)(2,1)S(1)} %bitcast.13), channel_id=1, source_target_pairs={{0,3},{1,2},{2,1},{3,0},{4,7},{5,6},{6,5},{7,4},{8,11},{9,10},{10,... | collective-permute-start | bytes 442376 | tf_op jit(solution)/shard_map/ppermute | solution.py:346
  73.7 16.4 %collective-permute-start = (bf16[576,128]{1,0:T(8,128)(2,1)S(1)}, bf16[576,128]{1,0:T(8,128)(2,1)S(1)}, u32[]{:S(2)}, u32[]{:S(2)}) collective-permute-start(bf16[576,128]{1,0:T(8,128)(2,1)S(1)} %bitcast.12), channel_id=1, source_target_pairs={{0,1},{1,0},{2,3},{3,2},{4,5},{5,4},{6,7},{7,6},{8,9},{9,8},{10,11... | collective-permute-start | bytes 442376 | tf_op jit(solution)/shard_map/ppermute | solution.py:346
  77.8 18.7 %collective-permute-start.27 = (bf16[576,128]{1,0:T(8,128)(2,1)S(1)}, bf16[576,128]{1,0:T(8,128)(2,1)S(1)}, u32[]{:S(2)}, u32[]{:S(2)}) collective-permute-start(bf16[576,128]{1,0:T(8,128)(2,1)S(1)} %get-tuple-element.55), channel_id=1, source_target_pairs={{0,6},{1,7},{2,4},{3,5},{4,2},{5,3},{6,0},{7,1},{8,14},{9,15},{10,... | collective-permute-start | bytes 442376 | tf_op jit(solution)/shard_map/ppermute | solution.py:346
  80.0 17.2 %collective-permute-start.28 = (bf16[576,128]{1,0:T(8,128)(2,1)S(1)}, bf16[576,128]{1,0:T(8,128)(2,1)S(1)}, u32[]{:S(2)}, u32[]{:S(2)}) collective-permute-start(bf16[576,128]{1,0:T(8,128)(2,1)S(1)} %get-tuple-element.56), channel_id=1, source_target_pairs={{0,7},{1,6},{2,5},{3,4},{4,3},{5,2},{6,1},{7,0},{8,15},{9,14},{10,... | collective-permute-start | bytes 442376 | tf_op jit(solution)/shard_map/ppermute | solution.py:346
  87.8 9.4 %collective-permute-start.21 = (bf16[576,128]{1,0:T(8,128)(2,1)S(1)}, bf16[576,128]{1,0:T(8,128)(2,1)S(1)}, u32[]{:S(2)}, u32[]{:S(2)}) collective-permute-start(bf16[576,128]{1,0:T(8,128)(2,1)S(1)} %get-tuple-element.49), channel_id=1, source_target_pairs={{0,2},{1,3},{2,0},{3,1},{4,6},{5,7},{6,4},{7,5},{8,10},{9,11},{10,... | collective-permute-start | bytes 442376 | tf_op jit(solution)/shard_map/ppermute | solution.py:346
  90.1 7.4 %collective-permute-start.22 = (bf16[576,128]{1,0:T(8,128)(2,1)S(1)}, bf16[576,128]{1,0:T(8,128)(2,1)S(1)}, u32[]{:S(2)}, u32[]{:S(2)}) collective-permute-start(bf16[576,128]{1,0:T(8,128)(2,1)S(1)} %get-tuple-element.50), channel_id=1, source_target_pairs={{0,3},{1,2},{2,1},{3,0},{4,7},{5,6},{6,5},{7,4},{8,11},{9,10},{10,... | collective-permute-start | bytes 442376 | tf_op jit(solution)/shard_map/ppermute | solution.py:346
  90.1 7.4 %collective-permute-start.23 = (bf16[576,128]{1,0:T(8,128)(2,1)S(1)}, bf16[576,128]{1,0:T(8,128)(2,1)S(1)}, u32[]{:S(2)}, u32[]{:S(2)}) collective-permute-start(bf16[576,128]{1,0:T(8,128)(2,1)S(1)} %get-tuple-element.51), channel_id=1, source_target_pairs={{0,4},{1,5},{2,6},{3,7},{4,0},{5,1},{6,2},{7,3},{8,12},{9,13},{10,... | collective-permute-start | bytes 442376 | tf_op jit(solution)/shard_map/ppermute | solution.py:346
  96.5 5.8 %collective-permute-start.24 = (bf16[576,128]{1,0:T(8,128)(2,1)S(1)}, bf16[576,128]{1,0:T(8,128)(2,1)S(1)}, u32[]{:S(2)}, u32[]{:S(2)}) collective-permute-start(bf16[576,128]{1,0:T(8,128)(2,1)S(1)} %get-tuple-element.52), channel_id=1, source_target_pairs={{0,5},{1,4},{2,7},{3,6},{4,1},{5,0},{6,3},{7,2},{8,13},{9,12},{10,... | collective-permute-start | bytes 442376 | tf_op jit(solution)/shard_map/ppermute | solution.py:346
  97.2 5.2 %collective-permute-start.15 = (bf16[576,128]{1,0:T(8,128)(2,1)S(1)}, bf16[576,128]{1,0:T(8,128)(2,1)S(1)}, u32[]{:S(2)}, u32[]{:S(2)}) collective-permute-start(bf16[576,128]{1,0:T(8,128)(2,1)S(1)} %get-tuple-element.44), channel_id=1, source_target_pairs={{0,1},{1,0},{2,3},{3,2},{4,5},{5,4},{6,7},{7,6},{8,9},{9,8},{10,11... | collective-permute-start | bytes 442376 | tf_op jit(solution)/shard_map/ppermute | solution.py:346
where the time goes:
time: 104 us
  starting transfers between devices  43.6 us (42%)
  waiting for transfers between devices  32.5 us (31%)
  Pallas kernels  25.1 us (24%)
  local copies, waits for them, and re-layouts  2.34 us (2%)
    ppermute x22, waiting for transfers between devices, swap(): return lax.ppermute(piece, AXES, pairs)  25.7 us
    ppermute x22, starting transfers between devices, swap(): return lax.ppermute(piece, AXES, pairs)  24.9 us
    ppermute x7, starting transfers between devices, relay(): return lax.ppermute(piece, AXES, pairs)  18.7 us
    pallas_call x3, Pallas kernels, attend(): pl.pallas_call(functools.partial(attend_kernel, parts, pieces), in_specs=...  16.7 us
    ppermute x7, waiting for transfers between devices, relay(): return lax.ppermute(piece, AXES, pairs)  6.72 us
    pallas_call x1, Pallas kernels, split_heads(): pl.pallas_call(functools.partial(split_kernel, layout), in_specs=[SMEM] +...  3.36 us
    pallas_call x1, Pallas kernels, split_queries(): pl.pallas_call(functools.partial(split_kernel_q, count, arrays), in_specs...  2.57 us
    unnamed x14, local copies, waits for them, and re-layouts  2.25 us
  transfers between devices with their start and end apart: 29, of which 11 were waited for; matrix products, arithmetic and copies ran while one was open for 0% of the time, Pallas kernels for 20%

commit v1 on v0

--- a/solution.py
+++ b/solution.py
@@ -10,7 +10,7 @@
 
 HD = 128
 TILE = 384
-UNROLL = 4
+UNROLL = 6
 LOG2E = 1.4426950408889634
 SPLIT_VMEM = 61 * 2**20
 AXES = ("group", "member", "head")
@@ -21,58 +21,62 @@
 VMEM = pl.BlockSpec(memory_space=pltpu.VMEM)
 
 
-def split_kernel_q(count, arrays, meta_ref, *refs):
-    sources, targets = refs[:arrays], refs[arrays : arrays + count]
-    stage, in_sems, out_sems = refs[arrays + count :]
+def own_index():
+    return lax.axis_index("member") * lax.axis_size("head") + lax.axis_index("head")
+
+
+def split_kernel_q(members, source, *refs):
+    pairs = members // 2
+    targets = refs[:pairs]
+    stage, in_sems, out_sems = refs[pairs:]
     width = stage.shape[-1]
 
-    def read(step, array):
-        column = pl.multiple_of((meta_ref[0] ^ step) * width, width)
+    def read(step):
+        column = pl.multiple_of((own_index() ^ step) * width, width)
         return pltpu.make_async_copy(
-            sources[array].at[:, pl.ds(column, width)], stage.at[step, array], in_sems.at[step, array]
-        )
-
-    def write(step):
-        return pltpu.make_async_copy(stage.at[step], targets[step], out_sems.at[step])
-
-    order = list(range(count - 1, -1, -1))
-    for step in order:
-        for array in range(arrays):
-            read(step, array).start()
-    for step in order:
-        for array in range(arrays):
-            read(step, array).wait()
-        write(step).start()
-    for step in order:
-        write(step).wait()
-
-
-def split_queries(meta, sources, count):
-    tokens, row_width = sources[0].shape
-    arrays = len(sources)
-    piece = (arrays, tokens, row_width // count)
-    return pl.pallas_call(
-        functools.partial(split_kernel_q, count, arrays),
-        in_specs=[SMEM] + [HBM] * arrays,
-        out_specs=[ANY] * count,
-        out_shape=[jax.ShapeDtypeStruct(piece, sources[0].dtype)] * count,
+            source.at[:, pl.ds(column, width)], stage.at[step], in_sems.at[step]
+        )
+
+    def write(pair):
+        return pltpu.make_async_copy(
+            stage.at[pl.ds(2 * pair, 2)], targets[pair], out_sems.at[pair]
+        )
+
+    for step in range(members):
+        read(step).start()
+    for pair in range(pairs):
+        read(2 * pair).wait()
+        read(2 * pair + 1).wait()
+        write(pair).start()
+    for pair in range(pairs):
+        write(pair).wait()
+
+
+def split_queries(source, members):
+    tokens, row_width = source.shape
+    piece = (tokens, row_width // members)
+    return pl.pallas_call(
+        functools.partial(split_kernel_q, members),
+        in_specs=[HBM],
+        out_specs=[ANY] * (members // 2),
+        out_shape=[jax.ShapeDtypeStruct((2,) + piece, source.dtype)] * (members // 2),
         scratch_shapes=[
-            pltpu.VMEM((count,) + piece, sources[0].dtype),
-            pltpu.SemaphoreType.DMA((count, arrays)),
-            pltpu.SemaphoreType.DMA((count,)),
+            pltpu.VMEM((members,) + piece, source.dtype),
+            pltpu.SemaphoreType.DMA((members,)),
+            pltpu.SemaphoreType.DMA((members // 2,)),
         ],
         compiler_params=pltpu.CompilerParams(vmem_limit_bytes=8 * 2**20),
         name="split_queries",
-    )(meta, *sources)
-
-
-def split_kernel(layout, meta_ref, *refs):
+    )(source)
+
+
+def split_kernel(layout, *refs):
     sources, targets = refs[:2], refs[2 : 2 + len(layout)]
     stage, in_sems, out_sems = refs[2 + len(layout) :]
     width = stage.shape[-1]
 
     def read(slot, step, array):
-        column = pl.multiple_of((meta_ref[0] ^ step) * width, width)
+        column = pl.multiple_of((own_index() ^ step) * width, width)
         return pltpu.make_async_copy(
             sources[array].at[:, pl.ds(column, width)], stage.at[slot, array], in_sems.at[slot, array]
         )
@@ -94,13 +98,13 @@
         write.wait()
 
 
-def split_heads(meta, keys, values, layout, members):
+def split_heads(keys, values, layout, members):
     tokens, row_width = keys.shape
     piece = (2, tokens, row_width // members)
     shapes = [piece if len(steps) == 1 else (len(steps),) + piece for steps in layout]
     return pl.pallas_call(
         functools.partial(split_kernel, layout),
-        in_specs=[SMEM] + [HBM] * 2,
+        in_specs=[HBM] * 2,
         out_specs=[ANY] * len(layout),
         out_shape=[jax.ShapeDtypeStruct(shape, keys.dtype) for shape in shapes],
         scratch_shapes=[
@@ -110,15 +114,15 @@
         ],
         compiler_params=pltpu.CompilerParams(vmem_limit_bytes=SPLIT_VMEM),
         name="split_heads",
-    )(meta, keys, values)
-
-
-def join_kernel(count, meta_ref, *refs):
+    )(keys, values)
+
+
+def join_kernel(count, *refs):
     sources, target, sems = refs[:count], refs[count], refs[count + 1]
     width = sources[0].shape[-1]
     copies = []
     for step in range(count):
-        column = pl.multiple_of((meta_ref[0] ^ step) * width, width)
+        column = pl.multiple_of((own_index() ^ step) * width, width)
         copies.append(
             pltpu.make_async_copy(sources[step], target.at[:, pl.ds(column, width)], sems.at[step])
         )
@@ -128,18 +132,18 @@
         copy.wait()
 
 
-def join_heads(meta, pieces):
+def join_heads(pieces):
     count = len(pieces)
     tokens, width = pieces[0].shape
     return pl.pallas_call(
         functools.partial(join_kernel, count),
-        in_specs=[SMEM] + [VMEM] * count,
+        in_specs=[VMEM] * count,
         out_specs=HBM,
         out_shape=jax.ShapeDtypeStruct((tokens, count * width), pieces[0].dtype),
         scratch_shapes=[pltpu.SemaphoreType.DMA((count,))],
         compiler_params=pltpu.CompilerParams(vmem_limit_bytes=4 * 2**20),
         name="join_heads",
-    )(meta, *pieces)
+    )(*pieces)
 
 
 def pack_kernel(first, second, target):
@@ -158,13 +162,13 @@
     )(first, second)
 
 
-def assemble_kernel(places, members, head_size, meta_ref, *refs):
+def assemble_kernel(places, members, head_size, *refs):
     arrays, targets = refs[:-2], refs[-2:]
     tokens = arrays[0].shape[-2]
     slab = head_size * tokens
     own = members * tokens
     for array, inner, step, halo in places:
-        source = meta_ref[0] ^ step
+        source = own_index() ^ step
         lane = (source % head_size) * tokens
         if halo:
             start = lane + jnp.where(source < head_size, slab + own, 0)
@@ -176,19 +180,19 @@
             targets[part][rows] = ref[part] if inner is None else ref[inner, part]
 
 
-def assemble(meta, pieces, members, head_size):
+def assemble(pieces, members, head_size):
     arrays = [piece[0] for piece in pieces]
     places = [(i, inner, step, halo) for i, (_, inner, step, halo) in enumerate(pieces)]
     tokens, width = arrays[0].shape[-2:]
     window = (members + 2 * head_size) * tokens
     return pl.pallas_call(
         functools.partial(assemble_kernel, places, members, head_size),
-        in_specs=[SMEM] + [VMEM] * len(arrays),
+        in_specs=[VMEM] * len(arrays),
         out_specs=[VMEM] * 2,
         out_shape=[jax.ShapeDtypeStruct((window, width), arrays[0].dtype)] * 2,
         compiler_params=pltpu.CompilerParams(vmem_limit_bytes=24 * 2**20),
         name="assemble",
-    )(meta, *arrays)
+    )(*arrays)
 
 
 def fold(value, op):
@@ -203,18 +207,24 @@
     return pl.ds(pl.multiple_of(tile * TILE, TILE), TILE)
 
 
-def attend_kernel(parts, pieces, meta_ref, *refs):
+def attend_kernel(parts, pieces, *refs):
     outputs = len(parts) * pieces
-    plan_refs, q_refs = refs[: len(parts)], refs[len(parts) : len(parts) + outputs]
+    plan_in, q_refs = refs[: len(parts)], refs[len(parts) : len(parts) + outputs]
     keys, values = refs[len(parts) + outputs : len(parts) + outputs + 2]
-    out_refs = refs[-9 - outputs : -9]
-    item_tile, item_slot, item_key, q_part, out_part, raw, peaks, acc, totals = refs[-9:]
-    tokens = q_refs[0].shape[0]
+    out_refs = refs[-11 - outputs : -11]
+    plans, sems, item_tile, item_slot, item_key, q_part, out_part, raw, peaks, acc, totals = refs[-11:]
+    tokens = q_refs[0].shape[1]
     block = pieces * tokens
     block_tiles = block // TILE
     tiles = len(parts) * block_tiles
-    slab_tiles, slots = plan_refs[0].shape[0], plan_refs[0].shape[1] - 1
-    me, base = meta_ref[0], meta_ref[1]
+    slab_tiles, slots = plan_in[0].shape[0], plan_in[0].shape[1] - 1
+    copies = [
+        pltpu.make_async_copy(plan, plans.at[i], sems.at[i]) for i, plan in enumerate(plan_in)
+    ]
+    for copy in copies:
+        copy.start()
+    me = own_index()
+    base = (lax.axis_index("group") * lax.axis_size("member") - 1) * slab_tiles
     factor = HD**-0.5 * LOG2E
 
     def piece_rows(index, step):
@@ -223,20 +233,21 @@
 
     for index in range(len(parts)):
         for step in range(pieces):
-            q_part[piece_rows(index, step)] = q_refs[index * pieces + step][...]
+            q_part[piece_rows(index, step)] = q_refs[index * pieces + step][step % 2]
     acc[...] = jnp.zeros_like(acc)
     totals[...] = jnp.zeros_like(totals)
 
+    for copy in copies:
+        copy.wait()
     total = jnp.int32(0)
     for index, part in enumerate(parts):
-        plan_ref = plan_refs[index]
         first_row = (((me // pieces) ^ part) * block_tiles) % slab_tiles
         for tile in range(block_tiles):
             for slot in range(slots):
                 item_tile[total + slot] = jnp.int32(index * block_tiles + tile)
                 item_slot[total + slot] = jnp.int32(slot)
-                item_key[total + slot] = plan_ref[first_row + tile, slot] - base
-            total = total + plan_ref[first_row + tile, slots]
+                item_key[total + slot] = plans[index, first_row + tile, slot] - base
+            total = total + plans[index, first_row + tile, slots]
     for extra in range(UNROLL):
         item_tile[total + extra] = jnp.int32(tiles)
         item_slot[total + extra] = jnp.int32(0)
@@ -272,15 +283,21 @@
 
     score(0, 0)
 
-    def body(i, carry):
-        for step in range(UNROLL):
-            item = i * UNROLL + step
-            score(item + 1, (step + 1) % 2)
-            carry = gather(item, step % 2, *carry)
-        return carry
+    def chunk(size, start):
+        def body(i, carry):
+            for step in range(size):
+                item = start + i * size + step
+                score(item + 1, (step + 1) % 2)
+                carry = gather(item, step % 2, *carry)
+            return carry
+
+        return body
 
     blank = jnp.zeros((1, TILE), jnp.float32)
-    lax.fori_loop(0, (total + UNROLL - 1) // UNROLL, body, (blank, blank))
+    whole = total // UNROLL
+    carry = lax.fori_loop(0, whole, chunk(UNROLL, 0), (blank, blank))
+    rest = total - whole * UNROLL
+    lax.fori_loop(0, (rest + 1) // 2, chunk(2, whole * UNROLL), carry)
     for tile in range(tiles):
         out_part[tile * TILE : (tile + 1) * TILE] = jnp.transpose(acc[tile] / totals[tile]).astype(
             out_part.dtype
@@ -290,8 +307,8 @@
             out_refs[index * pieces + step][...] = out_part[piece_rows(index, step)]
 
 
-def attend(meta, plans, queries, keys, values, parts, pieces):
-    tokens, width = queries[0].shape
+def attend(plans, queries, keys, values, parts, pieces):
+    _, tokens, width = queries[0].shape
     dtype = queries[0].dtype
     rows = len(parts) * pieces * tokens
     tiles = rows // TILE
@@ -299,10 +316,14 @@
     outputs = len(parts) * pieces
     return pl.pallas_call(
         functools.partial(attend_kernel, parts, pieces),
-        in_specs=[SMEM] * (1 + len(parts)) + [VMEM] * (outputs + 2),
+        in_specs=[VMEM] * (len(parts) + outputs + 2),
         out_specs=[VMEM] * outputs,
         out_shape=[jax.ShapeDtypeStruct((tokens, width), dtype)] * outputs,
-        scratch_shapes=[pltpu.SMEM((items,), jnp.int32)] * 3
+        scratch_shapes=[
+            pltpu.SMEM((len(parts),) + plans[0].shape, jnp.int32),
+            pltpu.SemaphoreType.DMA((len(parts),)),
+        ]
+        + [pltpu.SMEM((items,), jnp.int32)] * 3
         + [pltpu.VMEM((rows, width), dtype)] * 2
         + [
             pltpu.VMEM((2, TILE, TILE), jnp.float32),
@@ -315,7 +336,7 @@
             flops=16 * rows * TILE * HD, bytes_accessed=4 * rows * width, transcendentals=0
         ),
         name="attend",
-    )(meta, *plans, *queries, keys, values)
+    )(*plans, *queries, keys, values)
 
 
 def pieces_of(tokens):
@@ -330,14 +351,7 @@
     head_size = lax.axis_size("head")
     members = group_size * head_size
     tokens = queries.shape[0]
-    slab_tiles = tile_list.shape[0]
     pieces = pieces_of(tokens)
-    meta = jnp.stack(
-        [
-            lax.axis_index("member") * head_size + lax.axis_index("head"),
-            (lax.axis_index("group") * group_size - 1) * slab_tiles,
-        ]
-    ).astype(jnp.int32)
 
     def swap(piece, step):
         if step == 0:
@@ -360,7 +374,7 @@
     plans = [swap(own_plan, step * head_size) for step in range(group_size)]
 
     layout = layout_of(members)
-    kv_split = split_heads(meta, keys, values, layout, members)
+    kv_split = split_heads(keys, values, layout, members)
     swapped = {s: swap(array, s) for (s,), array in zip(layout, kv_split)}
     pieces_kv = [(array, None, step, False) for step, array in swapped.items()]
     for step in range(members // 4, members):
@@ -371,14 +385,16 @@
         beyond = relay(pair, step)
         pieces_kv += [(beyond, inner, step + inner, True) for inner in range(2)]
 
-    q_split = split_queries(meta, [queries], members)
-    q_pieces = [swap(piece[0], step) for step, piece in enumerate(q_split)]
-    window_keys, window_values = assemble(meta, pieces_kv, members, head_size)
+    q_split = split_queries(queries, members)
+    q_pieces = []
+    for pair, piece in enumerate(q_split):
+        piece = swap(piece, 2 * pair)
+        q_pieces += [piece, swap(piece, 1)]
+    window_keys, window_values = assemble(pieces_kv, members, head_size)
 
     results = [None] * members
     for parts in calls_of(members // pieces):
         outputs = attend(
-            meta,
             [plans[part * pieces // head_size] for part in parts],
             [q_pieces[part * pieces + step] for part in parts for step in range(pieces)],
             window_keys,
@@ -389,7 +405,7 @@
         steps = [part * pieces + step for part in parts for step in range(pieces)]
         for step, output in zip(steps, outputs):
             results[step] = swap(output, step)
-    return join_heads(meta, results)
+    return join_heads(results)
 
 
 def calls_of(parts):
@@ -407,7 +423,7 @@
     def run(queries, keys, values, tile_list, tile_count):
         group_size = queries.shape[1] // HD // head_size
         members = group_size * head_size
-        if group_size < 2 or tm_size % group_size or members & (members - 1):
+        if group_size < 2 or members < 8 or tm_size % group_size or members & (members - 1):
             raise ValueError("unsupported mesh")
         fine = Mesh(mesh.devices.reshape(tm_size // group_size, group_size, head_size), AXES)
         tokens_spec = P(AXES, None)

time: 104 us -> 118 us (1.13)
  local copies, waits for them, and re-layouts: 2.34 us -> 11.4 us
  waiting for transfers between devices: 32.5 us -> 40.7 us
  Pallas kernels: 25.1 us -> 22.6 us
    unnamed x14 -> x40, local copies, waits for them, and re-layouts: 2.25 us -> 11.3 us
    ppermute x7, waiting for transfers between devices: 6.72 us -> 11.3 us  [relay(): return lax.ppermute(piece, AXES, pairs)]
    ppermute x22, waiting for transfers between devices: 25.7 us -> 29.5 us  [swap(): return lax.ppermute(piece, AXES, pairs)]
    pallas_call x3, Pallas kernels: 7.54 us -> 4.55 us  [the longest x1 2.79 us: split_heads(): pl.pallas_call(functools.partial(split_kernel, layout), in_specs=[HBM] *...]
    ppermute x22, starting transfers between devices: 24.9 us -> 23.7 us  [swap(): return lax.ppermute(piece, AXES, pairs)]
  transfers between devices with their start and end apart: 29 -> 29, of which waited for: 11 -> 10; matrix products, arithmetic and copies ran while one was open for 0% -> 0% of each run, Pallas kernels for 20% -> 16%
where the time goes in v1:
time: 118 us
  starting transfers between devices  42.7 us (36%)
  waiting for transfers between devices  40.7 us (34%)
  Pallas kernels  22.6 us (19%)
  local copies, waits for them, and re-layouts  11.4 us (10%)
    ppermute x22, waiting for transfers between devices, swap(): return lax.ppermute(piece, AXES, pairs)  29.5 us
    ppermute x22, starting transfers between devices, swap(): return lax.ppermute(piece, AXES, pairs)  23.7 us
    ppermute x7, starting transfers between devices, relay(): return lax.ppermute(piece, AXES, pairs)  19 us
    pallas_call x3, Pallas kernels, attend(): pl.pallas_call(functools.partial(attend_kernel, parts, pieces), in_specs=...  16.6 us
    unnamed x40, local copies, waits for them, and re-layouts  11.3 us
    ppermute x7, waiting for transfers between devices, relay(): return lax.ppermute(piece, AXES, pairs)  11.3 us
    pallas_call x1, Pallas kernels, split_heads(): pl.pallas_call(functools.partial(split_kernel, layout), in_specs=[HBM] *...  2.79 us
  transfers between devices with their start and end apart: 29, of which 10 were waited for; matrix products, arithmetic and copies ran while one was open for 0% of the time, Pallas kernels for 16%

profile of v1, /device:TPU:17, one launch (start us, length us, event | category | flops | bytes accessed | tf_op | source)
XLA Modules:
  0.0 117.7 jit_solution(1754313394076222454)
XLA Ops:
  0.0 2.8 %split_heads.1 = (bf16[2,576,128]{2,1,0:T(8,128)(2,1)}, bf16[2,576,128]{2,1,0:T(8,128)(2,1)}, bf16[2,576,128]{2,1,0:T(8,128)(2,1)}, bf16[2,576,128]{2,1,0:T(8,12...) custom-call(bf16[576,1024]{1,0:T(8,128)(2,1)} %refs_0_.1, ...), custom_call_target="tpu_custom_call" | custom-call | tf_op jit(solution)/shard_map/split_heads/pallas_call | solution.py:105
  2.8 0.7 collective-permute-start.7
  3.6 1.2 %collective-permute-start.4 = (bf16[2,576,128]{2,1,0:T(8,128)(2,1)}, bf16[2,576,128]{2,1,0:T(8,128)(2,1)S(1)}, u32[]{:S(2)}, u32[]{:S(2)}) collective-permute-start(bf16[2,576,128]{2,1,0:T(8,128)(2,1)} %get-tuple-element.31), channel_id=1, source_target_pairs={{0,4},{1,5},{2,6},{3,7},{4,0},{5,1},{6,2},{7,3},{8,12},{9,13},{10,... | collective-permute-start | bytes 884744 | tf_op jit(solution)/shard_map/ppermute | solution.py:360
  5.3 2.2 %collective-permute-start.2 = (bf16[2,576,128]{2,1,0:T(8,128)(2,1)}, bf16[2,576,128]{2,1,0:T(8,128)(2,1)S(1)}, u32[]{:S(2)}, u32[]{:S(2)}) collective-permute-start(bf16[2,576,128]{2,1,0:T(8,128)(2,1)} %get-tuple-element.29), channel_id=1, source_target_pairs={{0,6},{1,7},{2,4},{3,5},{4,2},{5,3},{6,0},{7,1},{8,14},{9,15},{10,... | collective-permute-start | bytes 884744 | tf_op jit(solution)/shard_map/ppermute | solution.py:360
  7.9 1.2 %collective-permute-start.5 = (bf16[2,576,128]{2,1,0:T(8,128)(2,1)}, bf16[2,576,128]{2,1,0:T(8,128)(2,1)S(1)}, u32[]{:S(2)}, u32[]{:S(2)}) collective-permute-start(bf16[2,576,128]{2,1,0:T(8,128)(2,1)} %get-tuple-element.32), channel_id=1, source_target_pairs={{0,2},{1,3},{2,0},{3,1},{4,6},{5,7},{6,4},{7,5},{8,10},{9,11},{10,... | collective-permute-start | bytes 884744 | tf_op jit(solution)/shard_map/ppermute | solution.py:360
  9.2 3.1 %collective-permute-done.4.refs_3_ = bf16[2,576,128]{2,1,0:T(8,128)(2,1)S(1)} collective-permute-done((bf16[2,576,128]{2,1,0:T(8,128)(2,1)}, bf16[2,576,128]{2,1,0:T(8,128)(2,1)S(1)}, u32[]{:S(2)}, u32[]{:S(2)}) %collective-permute-start.4) | collective-permute-done | bytes 294944 | tf_op jit(solution)/shard_map/ppermute | solution.py:360
  12.3 2.6 %collective-permute-start.6 = (bf16[2,576,128]{2,1,0:T(8,128)(2,1)}, bf16[2,576,128]{2,1,0:T(8,128)(2,1)}, u32[]{:S(2)}, u32[]{:S(2)}) collective-permute-start(bf16[2,576,128]{2,1,0:T(8,128)(2,1)} %get-tuple-element.33), channel_id=1, source_target_pairs={{0,3},{1,2},{2,1},{3,0},{4,7},{5,6},{6,5},{7,4},{8,11},{9,10},{10,... | collective-permute-start | bytes 884744 | tf_op jit(solution)/shard_map/ppermute | solution.py:360
  15.5 4.2 %collective-permute-done.3.refs_2_ = bf16[2,576,128]{2,1,0:T(8,128)(2,1)S(1)} collective-permute-done((bf16[2,576,128]{2,1,0:T(8,128)(2,1)}, bf16[2,576,128]{2,1,0:T(8,128)(2,1)S(1)}, u32[]{:S(2)}, u32[]{:S(2)}) %collective-permute-start.3) | collective-permute-done | bytes 294944 | tf_op jit(solution)/shard_map/ppermute | solution.py:360
  19.8 2.2 %collective-permute-start.25 = (bf16[2,576,128]{2,1,0:T(8,128)(2,1)S(1)}, bf16[2,576,128]{2,1,0:T(8,128)(2,1)S(1)}, u32[]{:S(2)}, u32[]{:S(2)}) collective-permute-start(bf16[2,576,128]{2,1,0:T(8,128)(2,1)S(1)} %get-tuple-element.46), channel_id=1, source_target_pairs={{0,6},{1,7},{2,4},{3,5},{4,2},{5,3},{6,0},{7,1},{8,14},{9,15},{10,... | collective-permute-start | bytes 884744 | tf_op jit(solution)/shard_map/ppermute | solution.py:360
  21.9 4.0 %collective-permute-done.2.refs_1_ = bf16[2,576,128]{2,1,0:T(8,128)(2,1)S(1)} collective-permute-done((bf16[2,576,128]{2,1,0:T(8,128)(2,1)}, bf16[2,576,128]{2,1,0:T(8,128)(2,1)S(1)}, u32[]{:S(2)}, u32[]{:S(2)}) %collective-permute-start.2) | collective-permute-done | bytes 294944 | tf_op jit(solution)/shard_map/ppermute | solution.py:360
  25.9 1.2 %collective-permute-start.17 = (bf16[2,576,128]{2,1,0:T(8,128)(2,1)S(1)}, bf16[2,576,128]{2,1,0:T(8,128)(2,1)}, u32[]{:S(2)}, u32[]{:S(2)}) collective-permute-start(bf16[2,576,128]{2,1,0:T(8,128)(2,1)S(1)} %get-tuple-element.40), channel_id=1, source_target_pairs={{0,4},{1,5},{2,6},{3,7},{4,0},{5,1},{6,2},{7,3},{8,12},{9,13},{10,... | collective-permute-start | bytes 884744 | tf_op jit(solution)/shard_map/ppermute | solution.py:360
  27.1 5.9 %collective-permute-done.1.refs_0_ = bf16[2,576,128]{2,1,0:T(8,128)(2,1)S(1)} collective-permute-done((bf16[2,576,128]{2,1,0:T(8,128)(2,1)}, bf16[2,576,128]{2,1,0:T(8,128)(2,1)S(1)}, u32[]{:S(2)}, u32[]{:S(2)}) %collective-permute-start.1) | collective-permute-done | bytes 294944 | tf_op jit(solution)/shard_map/ppermute | solution.py:360
  33.3 3.2 %collective-permute-start.10 = (bf16[2,576,128]{2,1,0:T(8,128)(2,1)S(1)}, bf16[2,576,128]{2,1,0:T(8,128)(2,1)S(1)}, u32[]{:S(2)}, u32[]{:S(2)}) collective-permute-start(bf16[2,576,128]{2,1,0:T(8,128)(2,1)S(1)} %collective-permute-done.4.refs_3_), channel_id=1, source_target_pairs={{0,8},{1,9},{2,10},{3,11},{8,16},{9,17},{10,18},{11,19},{12,4},{13... | collective-permute-start | bytes 884744 | tf_op jit(solution)/shard_map/ppermute | solution.py:371
  36.5 6.6 %collective-permute-done.6.refs_5_ = bf16[2,576,128]{2,1,0:T(8,128)(2,1)} collective-permute-done((bf16[2,576,128]{2,1,0:T(8,128)(2,1)}, bf16[2,576,128]{2,1,0:T(8,128)(2,1)}, u32[]{:S(2)}, u32[]{:S(2)}) %collective-permute-start.6) | collective-permute-done | bytes 294944 | tf_op jit(solution)/shard_map/ppermute | solution.py:360
  43.1 3.2 %collective-permute-start.11 = (bf16[2,576,128]{2,1,0:T(8,128)(2,1)S(1)}, bf16[2,576,128]{2,1,0:T(8,128)(2,1)S(1)}, u32[]{:S(2)}, u32[]{:S(2)}) collective-permute-start(bf16[2,576,128]{2,1,0:T(8,128)(2,1)S(1)} %collective-permute-done.3.refs_2_), channel_id=1, source_target_pairs={{0,8},{1,9},{2,10},{3,11},{8,16},{9,17},{10,18},{11,19},{12,4},{13... | collective-permute-start | bytes 884744 | tf_op jit(solution)/shard_map/ppermute | solution.py:371
  46.4 2.1 %collective-permute-start.14 = (bf16[2,2,576,128]{3,2,1,0:T(8,128)(2,1)S(1)}, bf16[2,2,576,128]{3,2,1,0:T(8,128)(2,1)S(1)}, u32[]{:S(2)}, u32[]{:S(2)}) collective-permute-start(bf16[2,2,576,128]{3,2,1,0:T(8,128)(2,1)S(1)} %pack.1), channel_id=1, source_target_pairs={{4,12},{5,13},{6,14},{7,15},{8,0},{9,1},{10,2},{11,3},{12,20},{13,... | collective-permute-start | bytes 1769480 | tf_op jit(solution)/shard_map/ppermute | solution.py:371
  48.5 3.2 %collective-permute-start.12 = (bf16[2,576,128]{2,1,0:T(8,128)(2,1)S(1)}, bf16[2,576,128]{2,1,0:T(8,128)(2,1)S(1)}, u32[]{:S(2)}, u32[]{:S(2)}) collective-permute-start(bf16[2,576,128]{2,1,0:T(8,128)(2,1)S(1)} %collective-permute-done.2.refs_1_), channel_id=1, source_target_pairs={{0,8},{1,9},{2,10},{3,11},{8,16},{9,17},{10,18},{11,19},{12,4},{13... | collective-permute-start | bytes 884744 | tf_op jit(solution)/shard_map/ppermute | solution.py:371
  51.7 1.9 %collective-permute-start.13 = (bf16[2,576,128]{2,1,0:T(8,128)(2,1)S(1)}, bf16[2,576,128]{2,1,0:T(8,128)(2,1)S(1)}, u32[]{:S(2)}, u32[]{:S(2)}) collective-permute-start(bf16[2,576,128]{2,1,0:T(8,128)(2,1)S(1)} %collective-permute-done.1.refs_0_), channel_id=1, source_target_pairs={{0,8},{1,9},{2,10},{3,11},{8,16},{9,17},{10,18},{11,19},{12,4},{13... | collective-permute-start | bytes 884744 | tf_op jit(solution)/shard_map/ppermute | solution.py:371
  53.7 0.7 copy-done.8
  54.4 3.4 %collective-permute-start.8 = (bf16[2,576,128]{2,1,0:T(8,128)(2,1)S(1)}, bf16[2,576,128]{2,1,0:T(8,128)(2,1)S(1)}, u32[]{:S(2)}, u32[]{:S(2)}) collective-permute-start(bf16[2,576,128]{2,1,0:T(8,128)(2,1)S(1)} %collective-permute-done.5.refs_4_), channel_id=1, source_target_pairs={{4,12},{5,13},{6,14},{7,15},{8,0},{9,1},{10,2},{11,3},{12,20},{13,... | collective-permute-start | bytes 884744 | tf_op jit(solution)/shard_map/ppermute | solution.py:371
  57.8 0.7 copy-done.10
  58.5 2.0 %collective-permute-start.9 = (bf16[2,576,128]{2,1,0:T(8,128)(2,1)}, bf16[2,576,128]{2,1,0:T(8,128)(2,1)}, u32[]{:S(2)}, u32[]{:S(2)}) collective-permute-start(bf16[2,576,128]{2,1,0:T(8,128)(2,1)} %collective-permute-done.6.refs_5_), channel_id=1, source_target_pairs={{4,12},{5,13},{6,14},{7,15},{8,0},{9,1},{10,2},{11,3},{12,20},{13,... | collective-permute-start | bytes 884744 | tf_op jit(solution)/shard_map/ppermute | solution.py:371
  60.6 0.7 copy-done.12
  61.3 1.1 collective-permute-start.26
  62.4 4.1 %collective-permute-done.13.refs_13_ = bf16[2,576,128]{2,1,0:T(8,128)(2,1)S(1)} collective-permute-done((bf16[2,576,128]{2,1,0:T(8,128)(2,1)S(1)}, bf16[2,576,128]{2,1,0:T(8,128)(2,1)S(1)}, u32[]{:S(2)}, u32[]{:S(2)}) %collective-permute-start.13) | collective-permute-done | bytes 294944 | tf_op jit(solution)/shard_map/ppermute | solution.py:371
  66.6 0.7 copy-done.14
  67.5 2.2 %collective-permute-done.8.refs_8_ = bf16[2,576,128]{2,1,0:T(8,128)(2,1)S(1)} collective-permute-done((bf16[2,576,128]{2,1,0:T(8,128)(2,1)S(1)}, bf16[2,576,128]{2,1,0:T(8,128)(2,1)S(1)}, u32[]{:S(2)}, u32[]{:S(2)}) %collective-permute-start.8) | collective-permute-done | bytes 294944 | tf_op jit(solution)/shard_map/ppermute | solution.py:371
  69.8 0.7 copy-done.16
  70.5 0.7 collective-permute-start.20
  71.3 4.9 %collective-permute-done.9.refs_9_ = bf16[2,576,128]{2,1,0:T(8,128)(2,1)} collective-permute-done((bf16[2,576,128]{2,1,0:T(8,128)(2,1)}, bf16[2,576,128]{2,1,0:T(8,128)(2,1)}, u32[]{:S(2)}, u32[]{:S(2)}) %collective-permute-start.9) | collective-permute-done | bytes 294944 | tf_op jit(solution)/shard_map/ppermute | solution.py:371
  76.9 1.0 copy-done.3
  77.9 1.0 copy-done.5
  78.9 1.0 copy-done.7
  79.8 1.0 copy-done.9
  80.8 1.0 copy-done.11
  81.8 1.0 copy-done.13
  82.7 1.0 copy-done.15
  83.7 1.0 copy-done.17
  84.6 1.4 %assemble.1 = (bf16[9216,128]{1,0:T(8,128)(2,1)S(1)}, bf16[9216,128]{1,0:T(8,128)(2,1)S(1)}) custom-call(bf16[2,576,128]{2,1,0:T(8,128)(2,1)S(1)} %copy-done.5, bf16[2,576,128]{2,1,0:T(8,128)(2,1)S(1)} %copy-done.3, bf16[2,576,128]{2,1,0:T(8,128)(2,1)S(1)} %collective-permute-done.3.refs_2_, bf16[2,576,128]{2,1,0:T(8,128)(2,1)S(1)} %collective-permute-done.4.refs_3_, ...), custom_call_target="tpu_custom_call" | custom-call | tf_op jit(solution)/shard_map/assemble/pallas_call | solution.py:188
  86.1 3.5 %attend.5 = (bf16[576,128]{1,0:T(8,128)(2,1)S(1)}, bf16[576,128]{1,0:T(8,128)(2,1)S(1)}) custom-call(s32[6,8]{1,0:T(8,128)S(1)} %collective-permute-done.16.refs_0_, bf16[2,576,128]{2,1,0:T(8,128)(2,1)S(1)} %collective-permute-done.25.refs_1_, bf16[2,576,128]{2,1,0:T(8,128)(2,1)S(1)} %collective-permute-done.26.refs_2_, ...), custom_call_target="tpu_custom_call" | custom-call | flops 905969664 | bytes 589824 | tf_op jit(solution)/shard_map/attend/pallas_call | solution.py:317
  89.6 4.2 %collective-permute-start.27 = (bf16[576,128]{1,0:T(8,128)(2,1)S(1)}, bf16[576,128]{1,0:T(8,128)(2,1)S(1)}, u32[]{:S(2)}, u32[]{:S(2)}) collective-permute-start(bf16[576,128]{1,0:T(8,128)(2,1)S(1)} %get-tuple-element.47), channel_id=1, source_target_pairs={{0,6},{1,7},{2,4},{3,5},{4,2},{5,3},{6,0},{7,1},{8,14},{9,15},{10,... | collective-permute-start | bytes 442376 | tf_op jit(solution)/shard_map/ppermute | solution.py:360
  94.1 7.7 %attend.4 = (bf16[576,128]{1,0:T(8,128)(2,1)S(1)}, bf16[576,128]{1,0:T(8,128)(2,1)S(1)}, bf16[576,128]{1,0:T(8,128)(2,1)S(1)}, bf16[576,128]{1,0:T(8,128)(2,1)S(1)}) custom-call(s32[6,8]{1,0:T(8,128)S(1)} %collective-permute-done.16.refs_0_, s32[6,8]{1,0:T(8,128)S(1)} %pad_add_fusion.refs_0_.refs_1_, bf16[2,576,128]{2,1,0:T(8,128)(2,1)} %collective-permute-done.17.refs_2_, ...), custom_call_target="tpu_custom_call" | custom-call | flops 1811939328 | bytes 1179648 | tf_op jit(solution)/shard_map/attend/pallas_call | solution.py:317
  101.8 2.1 %collective-permute-start.21 = (bf16[576,128]{1,0:T(8,128)(2,1)S(1)}, bf16[576,128]{1,0:T(8,128)(2,1)S(1)}, u32[]{:S(2)}, u32[]{:S(2)}) collective-permute-start(bf16[576,128]{1,0:T(8,128)(2,1)S(1)} %get-tuple-element.42), channel_id=1, source_target_pairs={{0,2},{1,3},{2,0},{3,1},{4,6},{5,7},{6,4},{7,5},{8,10},{9,11},{10,... | collective-permute-start | bytes 442376 | tf_op jit(solution)/shard_map/ppermute | solution.py:360
  103.9 0.8 collective-permute-start.23
  104.7 5.4 %attend.3 = (bf16[576,128]{1,0:T(8,128)(2,1)S(1)}, bf16[576,128]{1,0:T(8,128)(2,1)S(1)}) custom-call(s32[6,8]{1,0:T(8,128)S(1)} %pad_add_fusion.refs_0_.refs_1_, bf16[2,576,128]{2,1,0:T(8,128)(2,1)S(1)} %get-tuple-element.27.refs_1_, bf16[2,576,128]{2,1,0:T(8,128)(2,1)S(1)} %collective-permute-done.refs_2_, ...), custom_call_target="tpu_custom_call" | custom-call | flops 905969664 | bytes 589824 | tf_op jit(solution)/shard_map/attend/pallas_call | solution.py:317
  110.2 0.7 collective-permute-start.24
  111.3 5.4 %collective-permute-done.24.refs_5_ = bf16[576,128]{1,0:T(8,128)(2,1)S(1)} collective-permute-done((bf16[576,128]{1,0:T(8,128)(2,1)S(1)}, bf16[576,128]{1,0:T(8,128)(2,1)S(1)}, u32[]{:S(2)}, u32[]{:S(2)}) %collective-permute-start.24) | collective-permute-done | bytes 147488 | tf_op jit(solution)/shard_map/ppermute | solution.py:360
  116.6 1.1 join_heads.1
  (60 shorter events, 3.8 us)
Async XLA Ops:
  0.0 14.9 %copy-start = (bf16[576,1024]{1,0:T(8,128)(2,1)S(1)}, bf16[576,1024]{1,0:T(8,128)(2,1)}, u32[]{:S(2)}) copy-start(bf16[576,1024]{1,0:T(8,128)(2,1)} %source.1) | copy-start | bytes 3538948
  2.8 43.5 %copy-start.1 = (bf16[2,576,128]{2,1,0:T(8,128)(2,1)S(1)}, bf16[2,576,128]{2,1,0:T(8,128)(2,1)}, u32[]{:S(2)}) copy-start(bf16[2,576,128]{2,1,0:T(8,128)(2,1)} %get-tuple-element.34.first.refs_6_) | copy-start | bytes 884740
  2.8 5.1 %collective-permute-start.7 = (bf16[2,576,128]{2,1,0:T(8,128)(2,1)}, bf16[2,576,128]{2,1,0:T(8,128)(2,1)S(1)}, u32[]{:S(2)}, u32[]{:S(2)}) collective-permute-start(bf16[2,576,128]{2,1,0:T(8,128)(2,1)} %get-tuple-element.35), channel_id=1, source_target_pairs={{0,1},{1,0},{2,3},{3,2},{4,5},{5,4},{6,7},{7,6},{8,9},{9,8},{10,11... | collective-permute-start | bytes 884744 | tf_op jit(solution)/shard_map/ppermute | solution.py:360
  3.6 8.7 %collective-permute-start.4 = (bf16[2,576,128]{2,1,0:T(8,128)(2,1)}, bf16[2,576,128]{2,1,0:T(8,128)(2,1)S(1)}, u32[]{:S(2)}, u32[]{:S(2)}) collective-permute-start(bf16[2,576,128]{2,1,0:T(8,128)(2,1)} %get-tuple-element.31), channel_id=1, source_target_pairs={{0,4},{1,5},{2,6},{3,7},{4,0},{5,1},{6,2},{7,3},{8,12},{9,13},{10,... | collective-permute-start | bytes 884744 | tf_op jit(solution)/shard_map/ppermute | solution.py:360
  4.8 15.0 %collective-permute-start.3 = (bf16[2,576,128]{2,1,0:T(8,128)(2,1)}, bf16[2,576,128]{2,1,0:T(8,128)(2,1)S(1)}, u32[]{:S(2)}, u32[]{:S(2)}) collective-permute-start(bf16[2,576,128]{2,1,0:T(8,128)(2,1)} %get-tuple-element.30), channel_id=1, source_target_pairs={{0,5},{1,4},{2,7},{3,6},{4,1},{5,0},{6,3},{7,2},{8,13},{9,12},{10,... | collective-permute-start | bytes 884744 | tf_op jit(solution)/shard_map/ppermute | solution.py:360
  5.3 20.6 %collective-permute-start.2 = (bf16[2,576,128]{2,1,0:T(8,128)(2,1)}, bf16[2,576,128]{2,1,0:T(8,128)(2,1)S(1)}, u32[]{:S(2)}, u32[]{:S(2)}) collective-permute-start(bf16[2,576,128]{2,1,0:T(8,128)(2,1)} %get-tuple-element.29), channel_id=1, source_target_pairs={{0,6},{1,7},{2,4},{3,5},{4,2},{5,3},{6,0},{7,1},{8,14},{9,15},{10,... | collective-permute-start | bytes 884744 | tf_op jit(solution)/shard_map/ppermute | solution.py:360
  7.4 25.6 %collective-permute-start.1 = (bf16[2,576,128]{2,1,0:T(8,128)(2,1)}, bf16[2,576,128]{2,1,0:T(8,128)(2,1)S(1)}, u32[]{:S(2)}, u32[]{:S(2)}) collective-permute-start(bf16[2,576,128]{2,1,0:T(8,128)(2,1)} %get-tuple-element.28), channel_id=1, source_target_pairs={{0,7},{1,6},{2,5},{3,4},{4,3},{5,2},{6,1},{7,0},{8,15},{9,14},{10,... | collective-permute-start | bytes 884744 | tf_op jit(solution)/shard_map/ppermute | solution.py:360
  7.9 25.3 %collective-permute-start.5 = (bf16[2,576,128]{2,1,0:T(8,128)(2,1)}, bf16[2,576,128]{2,1,0:T(8,128)(2,1)S(1)}, u32[]{:S(2)}, u32[]{:S(2)}) collective-permute-start(bf16[2,576,128]{2,1,0:T(8,128)(2,1)} %get-tuple-element.32), channel_id=1, source_target_pairs={{0,2},{1,3},{2,0},{3,1},{4,6},{5,7},{6,4},{7,5},{8,10},{9,11},{10,... | collective-permute-start | bytes 884744 | tf_op jit(solution)/shard_map/ppermute | solution.py:360
  12.2 59.0 %copy-start.19 = (s32[6]{0:T(128)S(1)}, s32[6]{0:T(128)}, u32[]{:S(2)}) copy-start(s32[6]{0:T(128)} %param.9) | copy-start | bytes 76
  12.3 64.5 %copy-start.18 = (s32[6,7]{1,0:T(8,128)S(1)}, s32[6,7]{1,0:T(8,128)}, u32[]{:S(2)}) copy-start(s32[6,7]{1,0:T(8,128)} %param.8) | copy-start | bytes 508
  12.3 30.9 %collective-permute-start.6 = (bf16[2,576,128]{2,1,0:T(8,128)(2,1)}, bf16[2,576,128]{2,1,0:T(8,128)(2,1)}, u32[]{:S(2)}, u32[]{:S(2)}) collective-permute-start(bf16[2,576,128]{2,1,0:T(8,128)(2,1)} %get-tuple-element.33), channel_id=1, source_target_pairs={{0,3},{1,2},{2,1},{3,0},{4,7},{5,6},{6,5},{7,4},{8,11},{9,10},{10,... | collective-permute-start | bytes 884744 | tf_op jit(solution)/shard_map/ppermute | solution.py:360
  19.8 26.6 %collective-permute-start.25 = (bf16[2,576,128]{2,1,0:T(8,128)(2,1)S(1)}, bf16[2,576,128]{2,1,0:T(8,128)(2,1)S(1)}, u32[]{:S(2)}, u32[]{:S(2)}) collective-permute-start(bf16[2,576,128]{2,1,0:T(8,128)(2,1)S(1)} %get-tuple-element.46), channel_id=1, source_target_pairs={{0,6},{1,7},{2,4},{3,5},{4,2},{5,3},{6,0},{7,1},{8,14},{9,15},{10,... | collective-permute-start | bytes 884744 | tf_op jit(solution)/shard_map/ppermute | solution.py:360
  25.9 34.6 %copy-start.2 = (bf16[2,576,128]{2,1,0:T(8,128)(2,1)}, bf16[2,576,128]{2,1,0:T(8,128)(2,1)S(1)}, u32[]{:S(2)}) copy-start(bf16[2,576,128]{2,1,0:T(8,128)(2,1)S(1)} %collective-permute-done.2.refs_1_) | copy-start | bytes 884740
  25.9 22.6 %collective-permute-start.17 = (bf16[2,576,128]{2,1,0:T(8,128)(2,1)S(1)}, bf16[2,576,128]{2,1,0:T(8,128)(2,1)}, u32[]{:S(2)}, u32[]{:S(2)}) collective-permute-start(bf16[2,576,128]{2,1,0:T(8,128)(2,1)S(1)} %get-tuple-element.40), channel_id=1, source_target_pairs={{0,4},{1,5},{2,6},{3,7},{4,0},{5,1},{6,2},{7,3},{8,12},{9,13},{10,... | collective-permute-start | bytes 884744 | tf_op jit(solution)/shard_map/ppermute | solution.py:360
  33.0 27.5 %copy-start.4 = (bf16[2,576,128]{2,1,0:T(8,128)(2,1)}, bf16[2,576,128]{2,1,0:T(8,128)(2,1)S(1)}, u32[]{:S(2)}) copy-start(bf16[2,576,128]{2,1,0:T(8,128)(2,1)S(1)} %collective-permute-done.1.refs_0_) | copy-start | bytes 884740
  33.1 18.7 %collective-permute-start.19 = (bf16[2,576,128]{2,1,0:T(8,128)(2,1)S(1)}, bf16[2,576,128]{2,1,0:T(8,128)(2,1)}, u32[]{:S(2)}, u32[]{:S(2)}) collective-permute-start(bf16[2,576,128]{2,1,0:T(8,128)(2,1)S(1)} %get-tuple-element.41), channel_id=1, source_target_pairs={{0,2},{1,3},{2,0},{3,1},{4,6},{5,7},{6,4},{7,5},{8,10},{9,11},{10,... | collective-permute-start | bytes 884744 | tf_op jit(solution)/shard_map/ppermute | solution.py:360
  33.3 33.3 %copy-start.6 = (bf16[2,576,128]{2,1,0:T(8,128)(2,1)}, bf16[2,576,128]{2,1,0:T(8,128)(2,1)S(1)}, u32[]{:S(2)}) copy-start(bf16[2,576,128]{2,1,0:T(8,128)(2,1)S(1)} %collective-permute-done.5.refs_4_) | copy-start | bytes 884740
  33.3 20.4 %collective-permute-start.10 = (bf16[2,576,128]{2,1,0:T(8,128)(2,1)S(1)}, bf16[2,576,128]{2,1,0:T(8,128)(2,1)S(1)}, u32[]{:S(2)}, u32[]{:S(2)}) collective-permute-start(bf16[2,576,128]{2,1,0:T(8,128)(2,1)S(1)} %collective-permute-done.4.refs_3_), channel_id=1, source_target_pairs={{0,8},{1,9},{2,10},{3,11},{8,16},{9,17},{10,18},{11,19},{12,4},{13... | collective-permute-start | bytes 884744 | tf_op jit(solution)/shard_map/ppermute | solution.py:371
  43.1 14.6 %collective-permute-start.11 = (bf16[2,576,128]{2,1,0:T(8,128)(2,1)S(1)}, bf16[2,576,128]{2,1,0:T(8,128)(2,1)S(1)}, u32[]{:S(2)}, u32[]{:S(2)}) collective-permute-start(bf16[2,576,128]{2,1,0:T(8,128)(2,1)S(1)} %collective-permute-done.3.refs_2_), channel_id=1, source_target_pairs={{0,8},{1,9},{2,10},{3,11},{8,16},{9,17},{10,18},{11,19},{12,4},{13... | collective-permute-start | bytes 884744 | tf_op jit(solution)/shard_map/ppermute | solution.py:371
  46.4 30.5 %collective-permute-start.14 = (bf16[2,2,576,128]{3,2,1,0:T(8,128)(2,1)S(1)}, bf16[2,2,576,128]{3,2,1,0:T(8,128)(2,1)S(1)}, u32[]{:S(2)}, u32[]{:S(2)}) collective-permute-start(bf16[2,2,576,128]{3,2,1,0:T(8,128)(2,1)S(1)} %pack.1), channel_id=1, source_target_pairs={{4,12},{5,13},{6,14},{7,15},{8,0},{9,1},{10,2},{11,3},{12,20},{13,... | collective-permute-start | bytes 1769480 | tf_op jit(solution)/shard_map/ppermute | solution.py:371
  48.5 12.1 %collective-permute-start.12 = (bf16[2,576,128]{2,1,0:T(8,128)(2,1)S(1)}, bf16[2,576,128]{2,1,0:T(8,128)(2,1)S(1)}, u32[]{:S(2)}, u32[]{:S(2)}) collective-permute-start(bf16[2,576,128]{2,1,0:T(8,128)(2,1)S(1)} %collective-permute-done.2.refs_1_), channel_id=1, source_target_pairs={{0,8},{1,9},{2,10},{3,11},{8,16},{9,17},{10,18},{11,19},{12,4},{13... | collective-permute-start | bytes 884744 | tf_op jit(solution)/shard_map/ppermute | solution.py:371
  51.7 14.8 %collective-permute-start.13 = (bf16[2,576,128]{2,1,0:T(8,128)(2,1)S(1)}, bf16[2,576,128]{2,1,0:T(8,128)(2,1)S(1)}, u32[]{:S(2)}, u32[]{:S(2)}) collective-permute-start(bf16[2,576,128]{2,1,0:T(8,128)(2,1)S(1)} %collective-permute-done.1.refs_0_), channel_id=1, source_target_pairs={{0,8},{1,9},{2,10},{3,11},{8,16},{9,17},{10,18},{11,19},{12,4},{13... | collective-permute-start | bytes 884744 | tf_op jit(solution)/shard_map/ppermute | solution.py:371
  53.7 0.7 copy-start.8
  54.4 15.4 %collective-permute-start.8 = (bf16[2,576,128]{2,1,0:T(8,128)(2,1)S(1)}, bf16[2,576,128]{2,1,0:T(8,128)(2,1)S(1)}, u32[]{:S(2)}, u32[]{:S(2)}) collective-permute-start(bf16[2,576,128]{2,1,0:T(8,128)(2,1)S(1)} %collective-permute-done.5.refs_4_), channel_id=1, source_target_pairs={{4,12},{5,13},{6,14},{7,15},{8,0},{9,1},{10,2},{11,3},{12,20},{13,... | collective-permute-start | bytes 884744 | tf_op jit(solution)/shard_map/ppermute | solution.py:371
  57.8 0.7 copy-start.10
  58.5 17.7 %collective-permute-start.9 = (bf16[2,576,128]{2,1,0:T(8,128)(2,1)}, bf16[2,576,128]{2,1,0:T(8,128)(2,1)}, u32[]{:S(2)}, u32[]{:S(2)}) collective-permute-start(bf16[2,576,128]{2,1,0:T(8,128)(2,1)} %collective-permute-done.6.refs_5_), channel_id=1, source_target_pairs={{4,12},{5,13},{6,14},{7,15},{8,0},{9,1},{10,2},{11,3},{12,20},{13,... | collective-permute-start | bytes 884744 | tf_op jit(solution)/shard_map/ppermute | solution.py:371
  60.6 0.7 copy-start.12
  61.3 24.7 %collective-permute-start.26 = (bf16[2,576,128]{2,1,0:T(8,128)(2,1)S(1)}, bf16[2,576,128]{2,1,0:T(8,128)(2,1)S(1)}, u32[]{:S(2)}, u32[]{:S(2)}) collective-permute-start(bf16[2,576,128]{2,1,0:T(8,128)(2,1)S(1)} %collective-permute-done.25.refs_1_), channel_id=1, source_target_pairs={{0,1},{1,0},{2,3},{3,2},{4,5},{5,4},{6,7},{7,6},{8,9},{9,8},{10,11... | collective-permute-start | bytes 884744 | tf_op jit(solution)/shard_map/ppermute | solution.py:360
  67.3 26.9 %collective-permute-start.18 = (bf16[2,576,128]{2,1,0:T(8,128)(2,1)}, bf16[2,576,128]{2,1,0:T(8,128)(2,1)}, u32[]{:S(2)}, u32[]{:S(2)}) collective-permute-start(bf16[2,576,128]{2,1,0:T(8,128)(2,1)} %collective-permute-done.17.refs_2_), channel_id=1, source_target_pairs={{0,1},{1,0},{2,3},{3,2},{4,5},{5,4},{6,7},{7,6},{8,9},{9,8},{10,11... | collective-permute-start | bytes 884744 | tf_op jit(solution)/shard_map/ppermute | solution.py:360
  69.8 0.7 copy-start.16
  70.5 23.6 %collective-permute-start.20 = (bf16[2,576,128]{2,1,0:T(8,128)(2,1)}, bf16[2,576,128]{2,1,0:T(8,128)(2,1)}, u32[]{:S(2)}, u32[]{:S(2)}) collective-permute-start(bf16[2,576,128]{2,1,0:T(8,128)(2,1)} %collective-permute-done.19.refs_4_), channel_id=1, source_target_pairs={{0,1},{1,0},{2,3},{3,2},{4,5},{5,4},{6,7},{7,6},{8,9},{9,8},{10,11... | collective-permute-start | bytes 884744 | tf_op jit(solution)/shard_map/ppermute | solution.py:360
  76.2 27.7 %collective-permute-start = (bf16[2,576,128]{2,1,0:T(8,128)(2,1)S(1)}, bf16[2,576,128]{2,1,0:T(8,128)(2,1)S(1)}, u32[]{:S(2)}, u32[]{:S(2)}) collective-permute-start(bf16[2,576,128]{2,1,0:T(8,128)(2,1)S(1)} %get-tuple-element.27.refs_1_), channel_id=1, source_target_pairs={{0,1},{1,0},{2,3},{3,2},{4,5},{5,4},{6,7},{7,6},{8,9},{9,8},{10,11... | collective-permute-start | bytes 884744 | tf_op jit(solution)/shard_map/ppermute | solution.py:360
  76.8 9.2 %collective-permute-start.16 = (s32[6,8]{1,0:T(8,128)S(1)}, s32[6,8]{1,0:T(8,128)S(1)}, u32[]{:S(2)}, u32[]{:S(2)}) collective-permute-start(s32[6,8]{1,0:T(8,128)S(1)} %pad_add_fusion.refs_0_.refs_1_), channel_id=1, source_target_pairs={{0,4},{1,5},{2,6},{3,7},{4,0},{5,1},{6,2},{7,3},{8,12},{9,13},{10,... | collective-permute-start | bytes 584 | tf_op jit(solution)/shard_map/ppermute | solution.py:360
  76.9 1.0 copy-start.3
  77.9 1.0 copy-start.5
  78.9 1.0 copy-start.7
  79.8 1.0 copy-start.9
  80.8 1.0 copy-start.11
  81.7 1.0 copy-start.13
  82.7 1.0 copy-start.15
  83.7 1.0 copy-start.17
  89.6 20.5 %collective-permute-start.27 = (bf16[576,128]{1,0:T(8,128)(2,1)S(1)}, bf16[576,128]{1,0:T(8,128)(2,1)S(1)}, u32[]{:S(2)}, u32[]{:S(2)}) collective-permute-start(bf16[576,128]{1,0:T(8,128)(2,1)S(1)} %get-tuple-element.47), channel_id=1, source_target_pairs={{0,6},{1,7},{2,4},{3,5},{4,2},{5,3},{6,0},{7,1},{8,14},{9,15},{10,... | collective-permute-start | bytes 442376 | tf_op jit(solution)/shard_map/ppermute | solution.py:360
  93.8 17.1 %collective-permute-start.28 = (bf16[576,128]{1,0:T(8,128)(2,1)S(1)}, bf16[576,128]{1,0:T(8,128)(2,1)S(1)}, u32[]{:S(2)}, u32[]{:S(2)}) collective-permute-start(bf16[576,128]{1,0:T(8,128)(2,1)S(1)} %get-tuple-element.48), channel_id=1, source_target_pairs={{0,7},{1,6},{2,5},{3,4},{4,3},{5,2},{6,1},{7,0},{8,15},{9,14},{10,... | collective-permute-start | bytes 442376 | tf_op jit(solution)/shard_map/ppermute | solution.py:360
  101.8 9.2 %collective-permute-start.21 = (bf16[576,128]{1,0:T(8,128)(2,1)S(1)}, bf16[576,128]{1,0:T(8,128)(2,1)S(1)}, u32[]{:S(2)}, u32[]{:S(2)}) collective-permute-start(bf16[576,128]{1,0:T(8,128)(2,1)S(1)} %get-tuple-element.42), channel_id=1, source_target_pairs={{0,2},{1,3},{2,0},{3,1},{4,6},{5,7},{6,4},{7,5},{8,10},{9,11},{10,... | collective-permute-start | bytes 442376 | tf_op jit(solution)/shard_map/ppermute | solution.py:360
  103.9 7.4 %collective-permute-start.22 = (bf16[576,128]{1,0:T(8,128)(2,1)S(1)}, bf16[576,128]{1,0:T(8,128)(2,1)S(1)}, u32[]{:S(2)}, u32[]{:S(2)}) collective-permute-start(bf16[576,128]{1,0:T(8,128)(2,1)S(1)} %get-tuple-element.43), channel_id=1, source_target_pairs={{0,3},{1,2},{2,1},{3,0},{4,7},{5,6},{6,5},{7,4},{8,11},{9,10},{10,... | collective-permute-start | bytes 442376 | tf_op jit(solution)/shard_map/ppermute | solution.py:360
  103.9 7.4 %collective-permute-start.23 = (bf16[576,128]{1,0:T(8,128)(2,1)S(1)}, bf16[576,128]{1,0:T(8,128)(2,1)S(1)}, u32[]{:S(2)}, u32[]{:S(2)}) collective-permute-start(bf16[576,128]{1,0:T(8,128)(2,1)S(1)} %get-tuple-element.44), channel_id=1, source_target_pairs={{0,4},{1,5},{2,6},{3,7},{4,0},{5,1},{6,2},{7,3},{8,12},{9,13},{10,... | collective-permute-start | bytes 442376 | tf_op jit(solution)/shard_map/ppermute | solution.py:360
  110.2 6.5 %collective-permute-start.24 = (bf16[576,128]{1,0:T(8,128)(2,1)S(1)}, bf16[576,128]{1,0:T(8,128)(2,1)S(1)}, u32[]{:S(2)}, u32[]{:S(2)}) collective-permute-start(bf16[576,128]{1,0:T(8,128)(2,1)S(1)} %get-tuple-element.45), channel_id=1, source_target_pairs={{0,5},{1,4},{2,7},{3,6},{4,1},{5,0},{6,3},{7,2},{8,13},{9,12},{10,... | collective-permute-start | bytes 442376 | tf_op jit(solution)/shard_map/ppermute | solution.py:360
  110.9 5.7 %collective-permute-start.15 = (bf16[576,128]{1,0:T(8,128)(2,1)S(1)}, bf16[576,128]{1,0:T(8,128)(2,1)S(1)}, u32[]{:S(2)}, u32[]{:S(2)}) collective-permute-start(bf16[576,128]{1,0:T(8,128)(2,1)S(1)} %get-tuple-element.39), channel_id=1, source_target_pairs={{0,1},{1,0},{2,3},{3,2},{4,5},{5,4},{6,7},{7,6},{8,9},{9,8},{10,11... | collective-permute-start | bytes 442376 | tf_op jit(solution)/shard_map/ppermute | solution.py:360
  (1 other events, 0.7 us)

commit v2 on v1

--- a/solution.py
+++ b/solution.py
@@ -25,10 +25,9 @@
     return lax.axis_index("member") * lax.axis_size("head") + lax.axis_index("head")
 
 
-def split_kernel_q(members, source, *refs):
-    pairs = members // 2
-    targets = refs[:pairs]
-    stage, in_sems, out_sems = refs[pairs:]
+def split_kernel_q(layout, source, *refs):
+    targets = refs[: len(layout)]
+    stage, in_sems, out_sems = refs[len(layout) :]
     width = stage.shape[-1]
 
     def read(step):
@@ -37,33 +36,35 @@
             source.at[:, pl.ds(column, width)], stage.at[step], in_sems.at[step]
         )
 
-    def write(pair):
-        return pltpu.make_async_copy(
-            stage.at[pl.ds(2 * pair, 2)], targets[pair], out_sems.at[pair]
-        )
-
-    for step in range(members):
-        read(step).start()
-    for pair in range(pairs):
-        read(2 * pair).wait()
-        read(2 * pair + 1).wait()
-        write(pair).start()
-    for pair in range(pairs):
-        write(pair).wait()
-
-
-def split_queries(source, members):
+    def write(index):
+        first, size = layout[index][0], len(layout[index])
+        block = stage.at[first] if size == 1 else stage.at[pl.ds(first, size)]
+        return pltpu.make_async_copy(block, targets[index], out_sems.at[index])
+
+    for steps in layout:
+        for step in steps:
+            read(step).start()
+    for index, steps in enumerate(layout):
+        for step in steps:
+            read(step).wait()
+        write(index).start()
+    for index in range(len(layout)):
+        write(index).wait()
+
+
+def split_queries(source, layout, members):
     tokens, row_width = source.shape
     piece = (tokens, row_width // members)
-    return pl.pallas_call(
-        functools.partial(split_kernel_q, members),
+    shapes = [piece if len(steps) == 1 else (len(steps),) + piece for steps in layout]
+    return pl.pallas_call(
+        functools.partial(split_kernel_q, layout),
         in_specs=[HBM],
-        out_specs=[ANY] * (members // 2),
-        out_shape=[jax.ShapeDtypeStruct((2,) + piece, source.dtype)] * (members // 2),
+        out_specs=[ANY] * len(layout),
+        out_shape=[jax.ShapeDtypeStruct(shape, source.dtype) for shape in shapes],
         scratch_shapes=[
             pltpu.VMEM((members,) + piece, source.dtype),
             pltpu.SemaphoreType.DMA((members,)),
-            pltpu.SemaphoreType.DMA((members // 2,)),
+            pltpu.SemaphoreType.DMA((len(layout),)),
         ],
         compiler_params=pltpu.CompilerParams(vmem_limit_bytes=8 * 2**20),
         name="split_queries",
@@ -117,14 +118,16 @@
     )(keys, values)
 
 
-def join_kernel(count, *refs):
+def join_kernel(inner, *refs):
+    count = len(inner)
     sources, target, sems = refs[:count], refs[count], refs[count + 1]
     width = sources[0].shape[-1]
     copies = []
-    for step in range(count):
+    for step, (source, index) in enumerate(zip(sources, inner)):
         column = pl.multiple_of((own_index() ^ step) * width, width)
+        source = source if index is None else source.at[index]
         copies.append(
-            pltpu.make_async_copy(sources[step], target.at[:, pl.ds(column, width)], sems.at[step])
+            pltpu.make_async_copy(source, target.at[:, pl.ds(column, width)], sems.at[step])
         )
     for copy in copies:
         copy.start()
@@ -133,17 +136,18 @@
 
 
 def join_heads(pieces):
-    count = len(pieces)
-    tokens, width = pieces[0].shape
-    return pl.pallas_call(
-        functools.partial(join_kernel, count),
+    arrays, inner = [piece[0] for piece in pieces], [piece[1] for piece in pieces]
+    count = len(arrays)
+    tokens, width = arrays[0].shape[-2:]
+    return pl.pallas_call(
+        functools.partial(join_kernel, inner),
         in_specs=[VMEM] * count,
         out_specs=HBM,
-        out_shape=jax.ShapeDtypeStruct((tokens, count * width), pieces[0].dtype),
+        out_shape=jax.ShapeDtypeStruct((tokens, count * width), arrays[0].dtype),
         scratch_shapes=[pltpu.SemaphoreType.DMA((count,))],
-        compiler_params=pltpu.CompilerParams(vmem_limit_bytes=4 * 2**20),
+        compiler_params=pltpu.CompilerParams(vmem_limit_bytes=8 * 2**20),
         name="join_heads",
-    )(*pieces)
+    )(*arrays)
 
 
 def pack_kernel(first, second, target):
@@ -207,13 +211,13 @@
     return pl.ds(pl.multiple_of(tile * TILE, TILE), TILE)
 
 
-def attend_kernel(parts, pieces, *refs):
+def attend_kernel(parts, pieces, inner, paired, *refs):
     outputs = len(parts) * pieces
     plan_in, q_refs = refs[: len(parts)], refs[len(parts) : len(parts) + outputs]
     keys, values = refs[len(parts) + outputs : len(parts) + outputs + 2]
-    out_refs = refs[-11 - outputs : -11]
+    out_refs = refs[-11 - (outputs // 2 if paired else outputs) : -11]
     plans, sems, item_tile, item_slot, item_key, q_part, out_part, raw, peaks, acc, totals = refs[-11:]
-    tokens = q_refs[0].shape[1]
+    tokens = q_refs[0].shape[-2]
     block = pieces * tokens
     block_tiles = block // TILE
     tiles = len(parts) * block_tiles
@@ -233,7 +237,11 @@
 
     for index in range(len(parts)):
         for step in range(pieces):
-            q_part[piece_rows(index, step)] = q_refs[index * pieces + step][step % 2]
+            place = index * pieces + step
+            ref = q_refs[place]
+            q_part[piece_rows(index, step)] = (
+                ref[...] if inner[place] is None else ref[inner[place]]
+            )
     acc[...] = jnp.zeros_like(acc)
     totals[...] = jnp.zeros_like(totals)
 
@@ -304,21 +312,28 @@
         )
     for index in range(len(parts)):
         for step in range(pieces):
-            out_refs[index * pieces + step][...] = out_part[piece_rows(index, step)]
-
-
-def attend(plans, queries, keys, values, parts, pieces):
-    _, tokens, width = queries[0].shape
+            place = index * pieces + step
+            if paired:
+                out_refs[place // 2][place % 2] = out_part[piece_rows(index, step)]
+            else:
+                out_refs[place][...] = out_part[piece_rows(index, step)]
+
+
+def attend(plans, queries, keys, values, parts, pieces, paired):
+    queries, inner = [q[0] for q in queries], [q[1] for q in queries]
+    tokens, width = queries[0].shape[-2:]
     dtype = queries[0].dtype
     rows = len(parts) * pieces * tokens
     tiles = rows // TILE
     items = tiles * (plans[0].shape[1] - 1) + UNROLL + 8
     outputs = len(parts) * pieces
     return pl.pallas_call(
-        functools.partial(attend_kernel, parts, pieces),
+        functools.partial(attend_kernel, parts, pieces, inner, paired),
         in_specs=[VMEM] * (len(parts) + outputs + 2),
-        out_specs=[VMEM] * outputs,
-        out_shape=[jax.ShapeDtypeStruct((tokens, width), dtype)] * outputs,
+        out_specs=[VMEM] * (outputs // 2 if paired else outputs),
+        out_shape=[jax.ShapeDtypeStruct((2, tokens, width), dtype)] * (outputs // 2)
+        if paired
+        else [jax.ShapeDtypeStruct((tokens, width), dtype)] * outputs,
         scratch_shapes=[
             pltpu.SMEM((len(parts),) + plans[0].shape, jnp.int32),
             pltpu.SemaphoreType.DMA((len(parts),)),
@@ -385,26 +400,41 @@
         beyond = relay(pair, step)
         pieces_kv += [(beyond, inner, step + inner, True) for inner in range(2)]
 
-    q_split = split_queries(queries, members)
-    q_pieces = []
-    for pair, piece in enumerate(q_split):
-        piece = swap(piece, 2 * pair)
-        q_pieces += [piece, swap(piece, 1)]
+    quarter = members // 4
+    paired_steps = [*range(0, quarter, 2), *range(3 * quarter, members, 2)]
+    q_layout = [(s, s + 1) for s in paired_steps] + [(s,) for s in range(quarter, 3 * quarter)]
+    q_pieces = {}
+    for steps, piece in zip(q_layout, split_queries(queries, q_layout, members)):
+        first = steps[0]
+        piece = swap(piece, first)
+        if len(steps) == 1:
+            q_pieces[first] = (piece, None)
+        else:
+            q_pieces[first] = (piece, 0)
+            q_pieces[first + 1] = (swap(piece, 1), 1)
     window_keys, window_values = assemble(pieces_kv, members, head_size)
 
     results = [None] * members
     for parts in calls_of(members // pieces):
+        paired = parts[0] == members // pieces - 1
+        steps = [part * pieces + step for part in parts for step in range(pieces)]
         outputs = attend(
             [plans[part * pieces // head_size] for part in parts],
-            [q_pieces[part * pieces + step] for part in parts for step in range(pieces)],
+            [q_pieces[step] for step in steps],
             window_keys,
             window_values,
             parts,
             pieces,
-        )
-        steps = [part * pieces + step for part in parts for step in range(pieces)]
-        for step, output in zip(steps, outputs):
-            results[step] = swap(output, step)
+            paired,
+        )
+        if paired:
+            for step, output in zip(steps[::2], outputs):
+                output = swap(output, step)
+                results[step] = (output, 0)
+                results[step + 1] = (swap(output, 1), 1)
+        else:
+            for step, output in zip(steps, outputs):
+                results[step] = (swap(output, step), None)
     return join_heads(results)
 
 

time: 118 us -> 102 us (0.86)
  the two profiles are of different devices: /device:TPU:17 before, /device:TPU:0 now
where the time goes in v2:
time: 102 us; the launch traced here: 101 us
  starting transfers between devices  38.3 us (38%)
  waiting for transfers between devices  36.7 us (36%)
  Pallas kernels  19.9 us (20%)
  local copies, waits for them, and re-layouts  6.12 us (6%)
    ppermute x22, waiting for transfers between devices, swap(): return lax.ppermute(piece, AXES, pairs)  25.9 us
    ppermute x22, starting transfers between devices, swap(): return lax.ppermute(piece, AXES, pairs)  19.5 us
    ppermute x7, starting transfers between devices, relay(): return lax.ppermute(piece, AXES, pairs)  18.8 us
    pallas_call x3, Pallas kernels, attend(): pl.pallas_call(functools.partial(attend_kernel, parts, pieces, inner, pai...  12.9 us
    ppermute x7, waiting for transfers between devices, relay(): return lax.ppermute(piece, AXES, pairs)  10.8 us
    unnamed x34, local copies, waits for them, and re-layouts  6.02 us
    pallas_call x1, Pallas kernels, split_heads(): pl.pallas_call(functools.partial(split_kernel, layout), in_specs=[HBM] *...  2.77 us
  transfers between devices with their start and end apart: 29, of which 12 were waited for; matrix products, arithmetic and copies ran while one was open for 0% of the time, Pallas kernels for 16%

profile of v2, /device:TPU:0, one launch (start us, length us, event | category | flops | bytes accessed | tf_op | source)
XLA Modules:
  0.0 101.5 jit_solution(6164804181594150237)
XLA Ops:
  0.0 2.8 %split_heads.1 = (bf16[2,576,128]{2,1,0:T(8,128)(2,1)}, bf16[2,576,128]{2,1,0:T(8,128)(2,1)}, bf16[2,576,128]{2,1,0:T(8,128)(2,1)}, bf16[2,576,128]{2,1,0:T(8,12...) custom-call(bf16[576,1024]{1,0:T(8,128)(2,1)} %refs_0_.1, ...), custom_call_target="tpu_custom_call" | custom-call | tf_op jit(solution)/shard_map/split_heads/pallas_call | solution.py:106
  2.8 0.6 collective-permute-start.7
  3.4 2.6 %collective-permute-start.4 = (bf16[2,576,128]{2,1,0:T(8,128)(2,1)}, bf16[2,576,128]{2,1,0:T(8,128)(2,1)S(1)}, u32[]{:S(2)}, u32[]{:S(2)}) collective-permute-start(bf16[2,576,128]{2,1,0:T(8,128)(2,1)} %get-tuple-element.31), channel_id=1, source_target_pairs={{0,4},{1,5},{2,6},{3,7},{4,0},{5,1},{6,2},{7,3},{8,12},{9,13},{10,... | collective-permute-start | bytes 884744 | tf_op jit(solution)/shard_map/ppermute | solution.py:375
  5.9 2.7 %collective-permute-start.2 = (bf16[2,576,128]{2,1,0:T(8,128)(2,1)}, bf16[2,576,128]{2,1,0:T(8,128)(2,1)S(1)}, u32[]{:S(2)}, u32[]{:S(2)}) collective-permute-start(bf16[2,576,128]{2,1,0:T(8,128)(2,1)} %get-tuple-element.29), channel_id=1, source_target_pairs={{0,6},{1,7},{2,4},{3,5},{4,2},{5,3},{6,0},{7,1},{8,14},{9,15},{10,... | collective-permute-start | bytes 884744 | tf_op jit(solution)/shard_map/ppermute | solution.py:375
  8.7 1.7 %collective-permute-start.5 = (bf16[2,576,128]{2,1,0:T(8,128)(2,1)}, bf16[2,576,128]{2,1,0:T(8,128)(2,1)}, u32[]{:S(2)}, u32[]{:S(2)}) collective-permute-start(bf16[2,576,128]{2,1,0:T(8,128)(2,1)} %get-tuple-element.32), channel_id=1, source_target_pairs={{0,2},{1,3},{2,0},{3,1},{4,6},{5,7},{6,4},{7,5},{8,10},{9,11},{10,... | collective-permute-start | bytes 884744 | tf_op jit(solution)/shard_map/ppermute | solution.py:375
  10.3 3.6 %collective-permute-done.4.refs_3_ = bf16[2,576,128]{2,1,0:T(8,128)(2,1)S(1)} collective-permute-done((bf16[2,576,128]{2,1,0:T(8,128)(2,1)}, bf16[2,576,128]{2,1,0:T(8,128)(2,1)S(1)}, u32[]{:S(2)}, u32[]{:S(2)}) %collective-permute-start.4) | collective-permute-done | bytes 294944 | tf_op jit(solution)/shard_map/ppermute | solution.py:375
  14.0 0.8 collective-permute-start.6
  14.8 1.3 %split_queries.1 = (bf16[2,576,128]{2,1,0:T(8,128)(2,1)S(1)}, bf16[2,576,128]{2,1,0:T(8,128)(2,1)S(1)}, bf16[576,128]{1,0:T(8,128)(2,1)S(1)}, bf16[576,128]{1,0:...) custom-call(bf16[576,1024]{1,0:T(8,128)(2,1)S(1)} %copy-done), custom_call_target="tpu_custom_call" | custom-call | tf_op jit(solution)/shard_map/split_queries/pallas_call | solution.py:59
  16.2 3.8 %collective-permute-done.3.refs_2_ = bf16[2,576,128]{2,1,0:T(8,128)(2,1)S(1)} collective-permute-done((bf16[2,576,128]{2,1,0:T(8,128)(2,1)}, bf16[2,576,128]{2,1,0:T(8,128)(2,1)S(1)}, u32[]{:S(2)}, u32[]{:S(2)}) %collective-permute-start.3) | collective-permute-done | bytes 294944 | tf_op jit(solution)/shard_map/ppermute | solution.py:375
  19.9 2.3 %collective-permute-start.25 = (bf16[2,576,128]{2,1,0:T(8,128)(2,1)S(1)}, bf16[2,576,128]{2,1,0:T(8,128)(2,1)S(1)}, u32[]{:S(2)}, u32[]{:S(2)}) collective-permute-start(bf16[2,576,128]{2,1,0:T(8,128)(2,1)S(1)} %get-tuple-element.48), channel_id=1, source_target_pairs={{0,6},{1,7},{2,4},{3,5},{4,2},{5,3},{6,0},{7,1},{8,14},{9,15},{10,... | collective-permute-start | bytes 884744 | tf_op jit(solution)/shard_map/ppermute | solution.py:375
  22.2 6.0 %collective-permute-done.2.refs_1_ = bf16[2,576,128]{2,1,0:T(8,128)(2,1)S(1)} collective-permute-done((bf16[2,576,128]{2,1,0:T(8,128)(2,1)}, bf16[2,576,128]{2,1,0:T(8,128)(2,1)S(1)}, u32[]{:S(2)}, u32[]{:S(2)}) %collective-permute-start.2) | collective-permute-done | bytes 294944 | tf_op jit(solution)/shard_map/ppermute | solution.py:375
  28.2 3.5 %collective-permute-start.10 = (bf16[2,576,128]{2,1,0:T(8,128)(2,1)S(1)}, bf16[2,576,128]{2,1,0:T(8,128)(2,1)S(1)}, u32[]{:S(2)}, u32[]{:S(2)}) collective-permute-start(bf16[2,576,128]{2,1,0:T(8,128)(2,1)S(1)} %collective-permute-done.4.refs_3_), channel_id=1, source_target_pairs={{0,8},{1,9},{2,10},{3,11},{8,16},{9,17},{10,18},{11,19},{12,4},{13... | collective-permute-start | bytes 884744 | tf_op jit(solution)/shard_map/ppermute | solution.py:386
  31.7 1.8 %collective-permute-done.1.refs_0_ = bf16[2,576,128]{2,1,0:T(8,128)(2,1)} collective-permute-done((bf16[2,576,128]{2,1,0:T(8,128)(2,1)}, bf16[2,576,128]{2,1,0:T(8,128)(2,1)}, u32[]{:S(2)}, u32[]{:S(2)}) %collective-permute-start.1) | collective-permute-done | bytes 294944 | tf_op jit(solution)/shard_map/ppermute | solution.py:375
  33.5 3.5 %collective-permute-start.11 = (bf16[2,576,128]{2,1,0:T(8,128)(2,1)S(1)}, bf16[2,576,128]{2,1,0:T(8,128)(2,1)S(1)}, u32[]{:S(2)}, u32[]{:S(2)}) collective-permute-start(bf16[2,576,128]{2,1,0:T(8,128)(2,1)S(1)} %collective-permute-done.3.refs_2_), channel_id=1, source_target_pairs={{0,8},{1,9},{2,10},{3,11},{8,16},{9,17},{10,18},{11,19},{12,4},{13... | collective-permute-start | bytes 884744 | tf_op jit(solution)/shard_map/ppermute | solution.py:386
  37.1 1.3 %collective-permute-start.14 = (bf16[2,2,576,128]{3,2,1,0:T(8,128)(2,1)S(1)}, bf16[2,2,576,128]{3,2,1,0:T(8,128)(2,1)S(1)}, u32[]{:S(2)}, u32[]{:S(2)}) collective-permute-start(bf16[2,2,576,128]{3,2,1,0:T(8,128)(2,1)S(1)} %pack.1), channel_id=1, source_target_pairs={{4,12},{5,13},{6,14},{7,15},{8,0},{9,1},{10,2},{11,3},{12,20},{13,... | collective-permute-start | bytes 1769480 | tf_op jit(solution)/shard_map/ppermute | solution.py:386
  38.4 4.5 %collective-permute-done.6.refs_5_ = bf16[2,576,128]{2,1,0:T(8,128)(2,1)} collective-permute-done((bf16[2,576,128]{2,1,0:T(8,128)(2,1)}, bf16[2,576,128]{2,1,0:T(8,128)(2,1)}, u32[]{:S(2)}, u32[]{:S(2)}) %collective-permute-start.6) | collective-permute-done | bytes 294944 | tf_op jit(solution)/shard_map/ppermute | solution.py:375
  42.9 3.8 %collective-permute-start.12 = (bf16[2,576,128]{2,1,0:T(8,128)(2,1)S(1)}, bf16[2,576,128]{2,1,0:T(8,128)(2,1)S(1)}, u32[]{:S(2)}, u32[]{:S(2)}) collective-permute-start(bf16[2,576,128]{2,1,0:T(8,128)(2,1)S(1)} %collective-permute-done.2.refs_1_), channel_id=1, source_target_pairs={{0,8},{1,9},{2,10},{3,11},{8,16},{9,17},{10,18},{11,19},{12,4},{13... | collective-permute-start | bytes 884744 | tf_op jit(solution)/shard_map/ppermute | solution.py:386
  46.7 4.2 %collective-permute-start.13 = (bf16[2,576,128]{2,1,0:T(8,128)(2,1)}, bf16[2,576,128]{2,1,0:T(8,128)(2,1)}, u32[]{:S(2)}, u32[]{:S(2)}) collective-permute-start(bf16[2,576,128]{2,1,0:T(8,128)(2,1)} %collective-permute-done.1.refs_0_), channel_id=1, source_target_pairs={{0,8},{1,9},{2,10},{3,11},{8,16},{9,17},{10,18},{11,19},{12,4},{13... | collective-permute-start | bytes 884744 | tf_op jit(solution)/shard_map/ppermute | solution.py:386
  50.9 0.7 copy-done.4
  51.6 1.3 %collective-permute-start.8 = (bf16[2,576,128]{2,1,0:T(8,128)(2,1)}, bf16[2,576,128]{2,1,0:T(8,128)(2,1)}, u32[]{:S(2)}, u32[]{:S(2)}) collective-permute-start(bf16[2,576,128]{2,1,0:T(8,128)(2,1)} %collective-permute-done.5.refs_4_), channel_id=1, source_target_pairs={{4,12},{5,13},{6,14},{7,15},{8,0},{9,1},{10,2},{11,3},{12,20},{13,... | collective-permute-start | bytes 884744 | tf_op jit(solution)/shard_map/ppermute | solution.py:386
  53.0 0.7 copy-done.6
  53.7 1.3 %collective-permute-start.9 = (bf16[2,576,128]{2,1,0:T(8,128)(2,1)}, bf16[2,576,128]{2,1,0:T(8,128)(2,1)}, u32[]{:S(2)}, u32[]{:S(2)}) collective-permute-start(bf16[2,576,128]{2,1,0:T(8,128)(2,1)} %collective-permute-done.6.refs_5_), channel_id=1, source_target_pairs={{4,12},{5,13},{6,14},{7,15},{8,0},{9,1},{10,2},{11,3},{12,20},{13,... | collective-permute-start | bytes 884744 | tf_op jit(solution)/shard_map/ppermute | solution.py:386
  55.0 0.7 copy-done.8
  55.7 0.1 copy.6
  55.9 4.2 %collective-permute-done.13.refs_13_ = bf16[2,576,128]{2,1,0:T(8,128)(2,1)} collective-permute-done((bf16[2,576,128]{2,1,0:T(8,128)(2,1)}, bf16[2,576,128]{2,1,0:T(8,128)(2,1)}, u32[]{:S(2)}, u32[]{:S(2)}) %collective-permute-start.13) | collective-permute-done | bytes 294944 | tf_op jit(solution)/shard_map/ppermute | solution.py:386
  60.1 2.4 %collective-permute-start.16 = (s32[6,8]{1,0:T(8,128)S(1)}, s32[6,8]{1,0:T(8,128)S(1)}, u32[]{:S(2)}, u32[]{:S(2)}) collective-permute-start(s32[6,8]{1,0:T(8,128)S(1)} %pad_add_fusion.refs_0_.refs_1_), channel_id=1, source_target_pairs={{0,4},{1,5},{2,6},{3,7},{4,0},{5,1},{6,2},{7,3},{8,12},{9,13},{10,... | collective-permute-start | bytes 584 | tf_op jit(solution)/shard_map/ppermute | solution.py:375
  62.5 1.3 %collective-permute-done.8.refs_8_ = bf16[2,576,128]{2,1,0:T(8,128)(2,1)} collective-permute-done((bf16[2,576,128]{2,1,0:T(8,128)(2,1)}, bf16[2,576,128]{2,1,0:T(8,128)(2,1)}, u32[]{:S(2)}, u32[]{:S(2)}) %collective-permute-start.8) | collective-permute-done | bytes 294944 | tf_op jit(solution)/shard_map/ppermute | solution.py:386
  63.7 5.3 %collective-permute-done.9.refs_9_ = bf16[2,576,128]{2,1,0:T(8,128)(2,1)} collective-permute-done((bf16[2,576,128]{2,1,0:T(8,128)(2,1)}, bf16[2,576,128]{2,1,0:T(8,128)(2,1)}, u32[]{:S(2)}, u32[]{:S(2)}) %collective-permute-start.9) | collective-permute-done | bytes 294944 | tf_op jit(solution)/shard_map/ppermute | solution.py:386
  69.1 1.5 %collective-permute-start.19 = (bf16[576,128]{1,0:T(8,128)(2,1)}, bf16[576,128]{1,0:T(8,128)(2,1)S(1)}, u32[]{:S(2)}, u32[]{:S(2)}) collective-permute-start(bf16[576,128]{1,0:T(8,128)(2,1)} %copy-done.12), channel_id=1, source_target_pairs={{0,2},{1,3},{2,0},{3,1},{4,6},{5,7},{6,4},{7,5},{8,10},{9,11},{10,... | collective-permute-start | bytes 442376 | tf_op jit(solution)/shard_map/ppermute | solution.py:375
  70.6 1.0 copy-done.3
  71.6 1.0 copy-done.5
  72.5 1.0 copy-done.7
  73.5 1.0 copy-done.9
  74.5 1.8 %assemble.1 = (bf16[9216,128]{1,0:T(8,128)(2,1)S(1)}, bf16[9216,128]{1,0:T(8,128)(2,1)S(1)}) custom-call(bf16[2,576,128]{2,1,0:T(8,128)(2,1)} %collective-permute-done.1.refs_0_, bf16[2,576,128]{2,1,0:T(8,128)(2,1)S(1)} %copy-done.3, bf16[2,576,128]{2,1,0:T(8,128)(2,1)S(1)} %collective-permute-done.3.refs_2_, ...), custom_call_target="tpu_custom_call" | custom-call | tf_op jit(solution)/shard_map/assemble/pallas_call | solution.py:192
  76.4 4.2 %attend.5 = bf16[2,576,128]{2,1,0:T(8,128)(2,1)S(1)} custom-call(s32[6,8]{1,0:T(8,128)S(1)} %collective-permute-done.16.refs_0_, bf16[2,576,128]{2,1,0:T(8,128)(2,1)S(1)} %collective-permute-done.25.refs_1_, bf16[2,576,128]{2,1,0:T(8,128)(2,1)S(1)} %collective-permute-done.26.refs_2_, bf16[9216,128]{1,0:T(8,128)(2,1)S(1)} %get-tuple-element.36.refs_3_.refs_6_, ...), custom_call_target="tpu_custom_call" | custom-call | flops 905969664 | bytes 589824 | tf_op jit(solution)/shard_map/attend/pallas_call | solution.py:330
  80.6 1.7 %collective-permute-start.27 = (bf16[2,576,128]{2,1,0:T(8,128)(2,1)S(1)}, bf16[2,576,128]{2,1,0:T(8,128)(2,1)S(1)}, u32[]{:S(2)}, u32[]{:S(2)}) collective-permute-start(bf16[2,576,128]{2,1,0:T(8,128)(2,1)S(1)} %attend.5), channel_id=1, source_target_pairs={{0,6},{1,7},{2,4},{3,5},{4,2},{5,3},{6,0},{7,1},{8,14},{9,15},{10,... | collective-permute-start | bytes 884744 | tf_op jit(solution)/shard_map/ppermute | solution.py:375
  82.3 5.7 %attend.4 = (bf16[576,128]{1,0:T(8,128)(2,1)S(1)}, bf16[576,128]{1,0:T(8,128)(2,1)S(1)}, bf16[576,128]{1,0:T(8,128)(2,1)S(1)}, bf16[576,128]{1,0:T(8,128)(2,1)S(1)}) custom-call(s32[6,8]{1,0:T(8,128)S(1)} %collective-permute-done.16.refs_0_, s32[6,8]{1,0:T(8,128)S(1)} %pad_add_fusion.refs_0_.refs_1_, bf16[576,128]{1,0:T(8,128)(2,1)S(1)} %collective-permute-done.17.refs_2_, ...), custom_call_target="tpu_custom_call" | custom-call | flops 1811939328 | bytes 1179648 | tf_op jit(solution)/shard_map/attend/pallas_call | solution.py:330
  88.1 0.7 collective-permute-start.21
  88.8 2.4 %collective-permute-done.27.refs_6_ = bf16[2,576,128]{2,1,0:T(8,128)(2,1)S(1)} collective-permute-done((bf16[2,576,128]{2,1,0:T(8,128)(2,1)S(1)}, bf16[2,576,128]{2,1,0:T(8,128)(2,1)S(1)}, u32[]{:S(2)}, u32[]{:S(2)}) %collective-permute-start.27) | collective-permute-done | bytes 294944 | tf_op jit(solution)/shard_map/ppermute | solution.py:375
  91.1 0.3 collective-permute-start.22
  91.4 0.8 collective-permute-start.23
  92.2 1.0 %collective-permute-start.24 = (bf16[576,128]{1,0:T(8,128)(2,1)S(1)}, bf16[576,128]{1,0:T(8,128)(2,1)S(1)}, u32[]{:S(2)}, u32[]{:S(2)}) collective-permute-start(bf16[576,128]{1,0:T(8,128)(2,1)S(1)} %get-tuple-element.47), channel_id=1, source_target_pairs={{0,5},{1,4},{2,7},{3,6},{4,1},{5,0},{6,3},{7,2},{8,13},{9,12},{10,... | collective-permute-start | bytes 442376 | tf_op jit(solution)/shard_map/ppermute | solution.py:375
  93.3 3.0 %attend.3 = (bf16[576,128]{1,0:T(8,128)(2,1)S(1)}, bf16[576,128]{1,0:T(8,128)(2,1)S(1)}) custom-call(s32[6,8]{1,0:T(8,128)S(1)} %pad_add_fusion.refs_0_.refs_1_, bf16[2,576,128]{2,1,0:T(8,128)(2,1)S(1)} %get-tuple-element.27.refs_1_, bf16[2,576,128]{2,1,0:T(8,128)(2,1)S(1)} %collective-permute-done.refs_2_, ...), custom_call_target="tpu_custom_call" | custom-call | flops 905969664 | bytes 589824 | tf_op jit(solution)/shard_map/attend/pallas_call | solution.py:330
  96.3 0.4 collective-permute-start.15
  96.6 0.5 collective-permute-done.22.refs_3_
  97.1 1.0 collective-permute-done.23.refs_4_
  98.1 2.2 %collective-permute-done.24.refs_5_ = bf16[576,128]{1,0:T(8,128)(2,1)S(1)} collective-permute-done((bf16[576,128]{1,0:T(8,128)(2,1)S(1)}, bf16[576,128]{1,0:T(8,128)(2,1)S(1)}, u32[]{:S(2)}, u32[]{:S(2)}) %collective-permute-start.24) | collective-permute-done | bytes 147488 | tf_op jit(solution)/shard_map/ppermute | solution.py:375
  100.4 1.1 %join_heads.1 = bf16[576,1024]{1,0:T(8,128)(2,1)} custom-call(bf16[576,128]{1,0:T(8,128)(2,1)S(1)} %get-tuple-element.38.refs_0_, bf16[576,128]{1,0:T(8,128)(2,1)S(1)} %collective-permute-done.15.refs_1_, bf16[576,128]{1,0:T(8,128)(2,1)S(1)} %collective-permute-done.21.refs_2_, bf16[576,128]{1,0:T(8,128)(2,1)S(1)} %collective-permute-done.22.refs_3_, ...), custom_call_target="tpu_custom_call" | custom-call | tf_op jit(solution)/shard_map/join_heads/pallas_call | solution.py:142
  (54 shorter events, 0.3 us)
Async XLA Ops:
  0.0 14.8 %copy-start = (bf16[576,1024]{1,0:T(8,128)(2,1)S(1)}, bf16[576,1024]{1,0:T(8,128)(2,1)}, u32[]{:S(2)}) copy-start(bf16[576,1024]{1,0:T(8,128)(2,1)} %source.1) | copy-start | bytes 3538948
  2.8 34.3 %copy-start.1 = (bf16[2,576,128]{2,1,0:T(8,128)(2,1)S(1)}, bf16[2,576,128]{2,1,0:T(8,128)(2,1)}, u32[]{:S(2)}) copy-start(bf16[2,576,128]{2,1,0:T(8,128)(2,1)} %get-tuple-element.34.first.refs_6_) | copy-start | bytes 884740
  2.8 5.9 %collective-permute-start.7 = (bf16[2,576,128]{2,1,0:T(8,128)(2,1)}, bf16[2,576,128]{2,1,0:T(8,128)(2,1)S(1)}, u32[]{:S(2)}, u32[]{:S(2)}) collective-permute-start(bf16[2,576,128]{2,1,0:T(8,128)(2,1)} %get-tuple-element.35), channel_id=1, source_target_pairs={{0,1},{1,0},{2,3},{3,2},{4,5},{5,4},{6,7},{7,6},{8,9},{9,8},{10,11... | collective-permute-start | bytes 884744 | tf_op jit(solution)/shard_map/ppermute | solution.py:375
  3.4 10.6 %collective-permute-start.4 = (bf16[2,576,128]{2,1,0:T(8,128)(2,1)}, bf16[2,576,128]{2,1,0:T(8,128)(2,1)S(1)}, u32[]{:S(2)}, u32[]{:S(2)}) collective-permute-start(bf16[2,576,128]{2,1,0:T(8,128)(2,1)} %get-tuple-element.31), channel_id=1, source_target_pairs={{0,4},{1,5},{2,6},{3,7},{4,0},{5,1},{6,2},{7,3},{8,12},{9,13},{10,... | collective-permute-start | bytes 884744 | tf_op jit(solution)/shard_map/ppermute | solution.py:375
  5.9 14.0 %collective-permute-start.3 = (bf16[2,576,128]{2,1,0:T(8,128)(2,1)}, bf16[2,576,128]{2,1,0:T(8,128)(2,1)S(1)}, u32[]{:S(2)}, u32[]{:S(2)}) collective-permute-start(bf16[2,576,128]{2,1,0:T(8,128)(2,1)} %get-tuple-element.30), channel_id=1, source_target_pairs={{0,5},{1,4},{2,7},{3,6},{4,1},{5,0},{6,3},{7,2},{8,13},{9,12},{10,... | collective-permute-start | bytes 884744 | tf_op jit(solution)/shard_map/ppermute | solution.py:375
  5.9 22.3 %collective-permute-start.2 = (bf16[2,576,128]{2,1,0:T(8,128)(2,1)}, bf16[2,576,128]{2,1,0:T(8,128)(2,1)S(1)}, u32[]{:S(2)}, u32[]{:S(2)}) collective-permute-start(bf16[2,576,128]{2,1,0:T(8,128)(2,1)} %get-tuple-element.29), channel_id=1, source_target_pairs={{0,6},{1,7},{2,4},{3,5},{4,2},{5,3},{6,0},{7,1},{8,14},{9,15},{10,... | collective-permute-start | bytes 884744 | tf_op jit(solution)/shard_map/ppermute | solution.py:375
  8.6 24.9 %collective-permute-start.1 = (bf16[2,576,128]{2,1,0:T(8,128)(2,1)}, bf16[2,576,128]{2,1,0:T(8,128)(2,1)}, u32[]{:S(2)}, u32[]{:S(2)}) collective-permute-start(bf16[2,576,128]{2,1,0:T(8,128)(2,1)} %get-tuple-element.28), channel_id=1, source_target_pairs={{0,7},{1,6},{2,5},{3,4},{4,3},{5,2},{6,1},{7,0},{8,15},{9,14},{10,... | collective-permute-start | bytes 884744 | tf_op jit(solution)/shard_map/ppermute | solution.py:375
  8.7 28.5 %collective-permute-start.5 = (bf16[2,576,128]{2,1,0:T(8,128)(2,1)}, bf16[2,576,128]{2,1,0:T(8,128)(2,1)}, u32[]{:S(2)}, u32[]{:S(2)}) collective-permute-start(bf16[2,576,128]{2,1,0:T(8,128)(2,1)} %get-tuple-element.32), channel_id=1, source_target_pairs={{0,2},{1,3},{2,0},{3,1},{4,6},{5,7},{6,4},{7,5},{8,10},{9,11},{10,... | collective-permute-start | bytes 884744 | tf_op jit(solution)/shard_map/ppermute | solution.py:375
  14.0 41.8 %copy-start.16 = (s32[6]{0:T(128)S(1)}, s32[6]{0:T(128)}, u32[]{:S(2)}) copy-start(s32[6]{0:T(128)} %param.9) | copy-start | bytes 76
  14.0 41.9 %copy-start.15 = (s32[6,7]{1,0:T(8,128)S(1)}, s32[6,7]{1,0:T(8,128)}, u32[]{:S(2)}) copy-start(s32[6,7]{1,0:T(8,128)} %param.8) | copy-start | bytes 508
  14.0 28.9 %collective-permute-start.6 = (bf16[2,576,128]{2,1,0:T(8,128)(2,1)}, bf16[2,576,128]{2,1,0:T(8,128)(2,1)}, u32[]{:S(2)}, u32[]{:S(2)}) collective-permute-start(bf16[2,576,128]{2,1,0:T(8,128)(2,1)} %get-tuple-element.33), channel_id=1, source_target_pairs={{0,3},{1,2},{2,1},{3,0},{4,7},{5,6},{6,5},{7,4},{8,11},{9,10},{10,... | collective-permute-start | bytes 884744 | tf_op jit(solution)/shard_map/ppermute | solution.py:375
  16.1 38.9 %copy-start.10 = (bf16[576,128]{1,0:T(8,128)(2,1)}, bf16[576,128]{1,0:T(8,128)(2,1)S(1)}, u32[]{:S(2)}) copy-start(bf16[576,128]{1,0:T(8,128)(2,1)S(1)} %get-tuple-element.43) | copy-start | bytes 442372
  16.1 39.6 %copy-start.12 = (bf16[576,128]{1,0:T(8,128)(2,1)}, bf16[576,128]{1,0:T(8,128)(2,1)S(1)}, u32[]{:S(2)}) copy-start(bf16[576,128]{1,0:T(8,128)(2,1)S(1)} %get-tuple-element.42) | copy-start | bytes 442372
  16.1 39.6 %copy-start.13 = (bf16[576,128]{1,0:T(8,128)(2,1)}, bf16[576,128]{1,0:T(8,128)(2,1)S(1)}, u32[]{:S(2)}) copy-start(bf16[576,128]{1,0:T(8,128)(2,1)S(1)} %get-tuple-element.41) | copy-start | bytes 442372
  16.2 39.6 %copy-start.14 = (bf16[576,128]{1,0:T(8,128)(2,1)}, bf16[576,128]{1,0:T(8,128)(2,1)S(1)}, u32[]{:S(2)}) copy-start(bf16[576,128]{1,0:T(8,128)(2,1)S(1)} %get-tuple-element.40) | copy-start | bytes 442372
  19.9 26.8 %collective-permute-start.25 = (bf16[2,576,128]{2,1,0:T(8,128)(2,1)S(1)}, bf16[2,576,128]{2,1,0:T(8,128)(2,1)S(1)}, u32[]{:S(2)}, u32[]{:S(2)}) collective-permute-start(bf16[2,576,128]{2,1,0:T(8,128)(2,1)S(1)} %get-tuple-element.48), channel_id=1, source_target_pairs={{0,6},{1,7},{2,4},{3,5},{4,2},{5,3},{6,0},{7,1},{8,14},{9,15},{10,... | collective-permute-start | bytes 884744 | tf_op jit(solution)/shard_map/ppermute | solution.py:375
  28.2 26.8 %copy-start.2 = (bf16[2,576,128]{2,1,0:T(8,128)(2,1)}, bf16[2,576,128]{2,1,0:T(8,128)(2,1)S(1)}, u32[]{:S(2)}) copy-start(bf16[2,576,128]{2,1,0:T(8,128)(2,1)S(1)} %collective-permute-done.2.refs_1_) | copy-start | bytes 884740
  28.2 22.7 %collective-permute-start.10 = (bf16[2,576,128]{2,1,0:T(8,128)(2,1)S(1)}, bf16[2,576,128]{2,1,0:T(8,128)(2,1)S(1)}, u32[]{:S(2)}, u32[]{:S(2)}) collective-permute-start(bf16[2,576,128]{2,1,0:T(8,128)(2,1)S(1)} %collective-permute-done.4.refs_3_), channel_id=1, source_target_pairs={{0,8},{1,9},{2,10},{3,11},{8,16},{9,17},{10,18},{11,19},{12,4},{13... | collective-permute-start | bytes 884744 | tf_op jit(solution)/shard_map/ppermute | solution.py:386
  33.5 19.4 %collective-permute-start.11 = (bf16[2,576,128]{2,1,0:T(8,128)(2,1)S(1)}, bf16[2,576,128]{2,1,0:T(8,128)(2,1)S(1)}, u32[]{:S(2)}, u32[]{:S(2)}) collective-permute-start(bf16[2,576,128]{2,1,0:T(8,128)(2,1)S(1)} %collective-permute-done.3.refs_2_), channel_id=1, source_target_pairs={{0,8},{1,9},{2,10},{3,11},{8,16},{9,17},{10,18},{11,19},{12,4},{13... | collective-permute-start | bytes 884744 | tf_op jit(solution)/shard_map/ppermute | solution.py:386
  37.1 32.0 %collective-permute-start.14 = (bf16[2,2,576,128]{3,2,1,0:T(8,128)(2,1)S(1)}, bf16[2,2,576,128]{3,2,1,0:T(8,128)(2,1)S(1)}, u32[]{:S(2)}, u32[]{:S(2)}) collective-permute-start(bf16[2,2,576,128]{3,2,1,0:T(8,128)(2,1)S(1)} %pack.1), channel_id=1, source_target_pairs={{4,12},{5,13},{6,14},{7,15},{8,0},{9,1},{10,2},{11,3},{12,20},{13,... | collective-permute-start | bytes 1769480 | tf_op jit(solution)/shard_map/ppermute | solution.py:386
  42.9 12.1 %collective-permute-start.12 = (bf16[2,576,128]{2,1,0:T(8,128)(2,1)S(1)}, bf16[2,576,128]{2,1,0:T(8,128)(2,1)S(1)}, u32[]{:S(2)}, u32[]{:S(2)}) collective-permute-start(bf16[2,576,128]{2,1,0:T(8,128)(2,1)S(1)} %collective-permute-done.2.refs_1_), channel_id=1, source_target_pairs={{0,8},{1,9},{2,10},{3,11},{8,16},{9,17},{10,18},{11,19},{12,4},{13... | collective-permute-start | bytes 884744 | tf_op jit(solution)/shard_map/ppermute | solution.py:386
  46.7 13.4 %collective-permute-start.13 = (bf16[2,576,128]{2,1,0:T(8,128)(2,1)}, bf16[2,576,128]{2,1,0:T(8,128)(2,1)}, u32[]{:S(2)}, u32[]{:S(2)}) collective-permute-start(bf16[2,576,128]{2,1,0:T(8,128)(2,1)} %collective-permute-done.1.refs_0_), channel_id=1, source_target_pairs={{0,8},{1,9},{2,10},{3,11},{8,16},{9,17},{10,18},{11,19},{12,4},{13... | collective-permute-start | bytes 884744 | tf_op jit(solution)/shard_map/ppermute | solution.py:386
  50.9 0.7 copy-start.4
  51.6 12.1 %collective-permute-start.8 = (bf16[2,576,128]{2,1,0:T(8,128)(2,1)}, bf16[2,576,128]{2,1,0:T(8,128)(2,1)}, u32[]{:S(2)}, u32[]{:S(2)}) collective-permute-start(bf16[2,576,128]{2,1,0:T(8,128)(2,1)} %collective-permute-done.5.refs_4_), channel_id=1, source_target_pairs={{4,12},{5,13},{6,14},{7,15},{8,0},{9,1},{10,2},{11,3},{12,20},{13,... | collective-permute-start | bytes 884744 | tf_op jit(solution)/shard_map/ppermute | solution.py:386
  52.9 0.7 copy-start.6
  53.7 15.4 %collective-permute-start.9 = (bf16[2,576,128]{2,1,0:T(8,128)(2,1)}, bf16[2,576,128]{2,1,0:T(8,128)(2,1)}, u32[]{:S(2)}, u32[]{:S(2)}) collective-permute-start(bf16[2,576,128]{2,1,0:T(8,128)(2,1)} %collective-permute-done.6.refs_5_), channel_id=1, source_target_pairs={{4,12},{5,13},{6,14},{7,15},{8,0},{9,1},{10,2},{11,3},{12,20},{13,... | collective-permute-start | bytes 884744 | tf_op jit(solution)/shard_map/ppermute | solution.py:386
  55.0 0.7 copy-start.8
  55.7 20.6 %collective-permute-start.26 = (bf16[2,576,128]{2,1,0:T(8,128)(2,1)S(1)}, bf16[2,576,128]{2,1,0:T(8,128)(2,1)S(1)}, u32[]{:S(2)}, u32[]{:S(2)}) collective-permute-start(bf16[2,576,128]{2,1,0:T(8,128)(2,1)S(1)} %collective-permute-done.25.refs_1_), channel_id=1, source_target_pairs={{0,1},{1,0},{2,3},{3,2},{4,5},{5,4},{6,7},{7,6},{8,9},{9,8},{10,11... | collective-permute-start | bytes 884744 | tf_op jit(solution)/shard_map/ppermute | solution.py:375
  60.1 16.2 %collective-permute-start.16 = (s32[6,8]{1,0:T(8,128)S(1)}, s32[6,8]{1,0:T(8,128)S(1)}, u32[]{:S(2)}, u32[]{:S(2)}) collective-permute-start(s32[6,8]{1,0:T(8,128)S(1)} %pad_add_fusion.refs_0_.refs_1_), channel_id=1, source_target_pairs={{0,4},{1,5},{2,6},{3,7},{4,0},{5,1},{6,2},{7,3},{8,12},{9,13},{10,... | collective-permute-start | bytes 584 | tf_op jit(solution)/shard_map/ppermute | solution.py:375
  63.7 18.6 %collective-permute-start.17 = (bf16[576,128]{1,0:T(8,128)(2,1)}, bf16[576,128]{1,0:T(8,128)(2,1)S(1)}, u32[]{:S(2)}, u32[]{:S(2)}) collective-permute-start(bf16[576,128]{1,0:T(8,128)(2,1)} %copy-done.14), channel_id=1, source_target_pairs={{0,4},{1,5},{2,6},{3,7},{4,0},{5,1},{6,2},{7,3},{8,12},{9,13},{10,... | collective-permute-start | bytes 442376 | tf_op jit(solution)/shard_map/ppermute | solution.py:375
  69.1 13.2 %collective-permute-start.18 = (bf16[576,128]{1,0:T(8,128)(2,1)}, bf16[576,128]{1,0:T(8,128)(2,1)S(1)}, u32[]{:S(2)}, u32[]{:S(2)}) collective-permute-start(bf16[576,128]{1,0:T(8,128)(2,1)} %copy-done.13), channel_id=1, source_target_pairs={{0,5},{1,4},{2,7},{3,6},{4,1},{5,0},{6,3},{7,2},{8,13},{9,12},{10,... | collective-permute-start | bytes 442376 | tf_op jit(solution)/shard_map/ppermute | solution.py:375
  69.1 13.2 %collective-permute-start.19 = (bf16[576,128]{1,0:T(8,128)(2,1)}, bf16[576,128]{1,0:T(8,128)(2,1)S(1)}, u32[]{:S(2)}, u32[]{:S(2)}) collective-permute-start(bf16[576,128]{1,0:T(8,128)(2,1)} %copy-done.12), channel_id=1, source_target_pairs={{0,2},{1,3},{2,0},{3,1},{4,6},{5,7},{6,4},{7,5},{8,10},{9,11},{10,... | collective-permute-start | bytes 442376 | tf_op jit(solution)/shard_map/ppermute | solution.py:375
  70.6 1.0 copy-start.3
  71.6 1.0 copy-start.5
  72.5 1.0 copy-start.7
  73.5 1.0 copy-start.9
  74.4 1.8 %copy-start.11 = (bf16[576,128]{1,0:T(8,128)(2,1)S(1)}, bf16[576,128]{1,0:T(8,128)(2,1)}, u32[]{:S(2)}) copy-start(bf16[576,128]{1,0:T(8,128)(2,1)} %copy-done.10) | copy-start | bytes 442372
  76.3 6.1 %collective-permute-start.20 = (bf16[576,128]{1,0:T(8,128)(2,1)S(1)}, bf16[576,128]{1,0:T(8,128)(2,1)S(1)}, u32[]{:S(2)}, u32[]{:S(2)}) collective-permute-start(bf16[576,128]{1,0:T(8,128)(2,1)S(1)} %copy-done.11), channel_id=1, source_target_pairs={{0,3},{1,2},{2,1},{3,0},{4,7},{5,6},{6,5},{7,4},{8,11},{9,10},{10,... | collective-permute-start | bytes 442376 | tf_op jit(solution)/shard_map/ppermute | solution.py:375
  80.6 10.5 %collective-permute-start.27 = (bf16[2,576,128]{2,1,0:T(8,128)(2,1)S(1)}, bf16[2,576,128]{2,1,0:T(8,128)(2,1)S(1)}, u32[]{:S(2)}, u32[]{:S(2)}) collective-permute-start(bf16[2,576,128]{2,1,0:T(8,128)(2,1)S(1)} %attend.5), channel_id=1, source_target_pairs={{0,6},{1,7},{2,4},{3,5},{4,2},{5,3},{6,0},{7,1},{8,14},{9,15},{10,... | collective-permute-start | bytes 884744 | tf_op jit(solution)/shard_map/ppermute | solution.py:375
  82.3 9.9 %collective-permute-start = (bf16[2,576,128]{2,1,0:T(8,128)(2,1)S(1)}, bf16[2,576,128]{2,1,0:T(8,128)(2,1)S(1)}, u32[]{:S(2)}, u32[]{:S(2)}) collective-permute-start(bf16[2,576,128]{2,1,0:T(8,128)(2,1)S(1)} %get-tuple-element.27.refs_1_), channel_id=1, source_target_pairs={{0,1},{1,0},{2,3},{3,2},{4,5},{5,4},{6,7},{7,6},{8,9},{9,8},{10,11... | collective-permute-start | bytes 884744 | tf_op jit(solution)/shard_map/ppermute | solution.py:375
  88.1 8.2 %collective-permute-start.21 = (bf16[576,128]{1,0:T(8,128)(2,1)S(1)}, bf16[576,128]{1,0:T(8,128)(2,1)S(1)}, u32[]{:S(2)}, u32[]{:S(2)}) collective-permute-start(bf16[576,128]{1,0:T(8,128)(2,1)S(1)} %get-tuple-element.44), channel_id=1, source_target_pairs={{0,2},{1,3},{2,0},{3,1},{4,6},{5,7},{6,4},{7,5},{8,10},{9,11},{10,... | collective-permute-start | bytes 442376 | tf_op jit(solution)/shard_map/ppermute | solution.py:375
  91.1 9.2 %collective-permute-start.28 = (bf16[2,576,128]{2,1,0:T(8,128)(2,1)S(1)}, bf16[2,576,128]{2,1,0:T(8,128)(2,1)S(1)}, u32[]{:S(2)}, u32[]{:S(2)}) collective-permute-start(bf16[2,576,128]{2,1,0:T(8,128)(2,1)S(1)} %collective-permute-done.27.refs_6_), channel_id=1, source_target_pairs={{0,1},{1,0},{2,3},{3,2},{4,5},{5,4},{6,7},{7,6},{8,9},{9,8},{10,11... | collective-permute-start | bytes 884744 | tf_op jit(solution)/shard_map/ppermute | solution.py:375
  91.1 6.0 %collective-permute-start.22 = (bf16[576,128]{1,0:T(8,128)(2,1)S(1)}, bf16[576,128]{1,0:T(8,128)(2,1)S(1)}, u32[]{:S(2)}, u32[]{:S(2)}) collective-permute-start(bf16[576,128]{1,0:T(8,128)(2,1)S(1)} %get-tuple-element.45), channel_id=1, source_target_pairs={{0,3},{1,2},{2,1},{3,0},{4,7},{5,6},{6,5},{7,4},{8,11},{9,10},{10,... | collective-permute-start | bytes 442376 | tf_op jit(solution)/shard_map/ppermute | solution.py:375
  91.4 6.7 %collective-permute-start.23 = (bf16[576,128]{1,0:T(8,128)(2,1)S(1)}, bf16[576,128]{1,0:T(8,128)(2,1)S(1)}, u32[]{:S(2)}, u32[]{:S(2)}) collective-permute-start(bf16[576,128]{1,0:T(8,128)(2,1)S(1)} %get-tuple-element.46), channel_id=1, source_target_pairs={{0,4},{1,5},{2,6},{3,7},{4,0},{5,1},{6,2},{7,3},{8,12},{9,13},{10,... | collective-permute-start | bytes 442376 | tf_op jit(solution)/shard_map/ppermute | solution.py:375
  92.2 8.1 %collective-permute-start.24 = (bf16[576,128]{1,0:T(8,128)(2,1)S(1)}, bf16[576,128]{1,0:T(8,128)(2,1)S(1)}, u32[]{:S(2)}, u32[]{:S(2)}) collective-permute-start(bf16[576,128]{1,0:T(8,128)(2,1)S(1)} %get-tuple-element.47), channel_id=1, source_target_pairs={{0,5},{1,4},{2,7},{3,6},{4,1},{5,0},{6,3},{7,2},{8,13},{9,12},{10,... | collective-permute-start | bytes 442376 | tf_op jit(solution)/shard_map/ppermute | solution.py:375
  96.3 4.1 %collective-permute-start.15 = (bf16[576,128]{1,0:T(8,128)(2,1)S(1)}, bf16[576,128]{1,0:T(8,128)(2,1)S(1)}, u32[]{:S(2)}, u32[]{:S(2)}) collective-permute-start(bf16[576,128]{1,0:T(8,128)(2,1)S(1)} %get-tuple-element.39), channel_id=1, source_target_pairs={{0,1},{1,0},{2,3},{3,2},{4,5},{5,4},{6,7},{7,6},{8,9},{9,8},{10,11... | collective-permute-start | bytes 442376 | tf_op jit(solution)/shard_map/ppermute | solution.py:375

commit v3 on v2

--- a/solution.py
+++ b/solution.py
@@ -215,7 +215,7 @@
     outputs = len(parts) * pieces
     plan_in, q_refs = refs[: len(parts)], refs[len(parts) : len(parts) + outputs]
     keys, values = refs[len(parts) + outputs : len(parts) + outputs + 2]
-    out_refs = refs[-11 - (outputs // 2 if paired else outputs) : -11]
+    out_refs = list(refs[-11 - sum(pieces // 2 if p else pieces for p in paired) : -11])
     plans, sems, item_tile, item_slot, item_key, q_part, out_part, raw, peaks, acc, totals = refs[-11:]
     tokens = q_refs[0].shape[-2]
     block = pieces * tokens
@@ -312,11 +312,13 @@
         )
     for index in range(len(parts)):
         for step in range(pieces):
-            place = index * pieces + step
-            if paired:
-                out_refs[place // 2][place % 2] = out_part[piece_rows(index, step)]
+            value = out_part[piece_rows(index, step)]
+            if not paired[index]:
+                out_refs.pop(0)[...] = value
+            elif step % 2 == 0:
+                out_refs[0][0] = value
             else:
-                out_refs[place][...] = out_part[piece_rows(index, step)]
+                out_refs.pop(0)[1] = value
 
 
 def attend(plans, queries, keys, values, parts, pieces, paired):
@@ -327,13 +329,14 @@
     tiles = rows // TILE
     items = tiles * (plans[0].shape[1] - 1) + UNROLL + 8
     outputs = len(parts) * pieces
+    shapes = []
+    for pair in paired:
+        shapes += [(2, tokens, width)] * (pieces // 2) if pair else [(tokens, width)] * pieces
     return pl.pallas_call(
         functools.partial(attend_kernel, parts, pieces, inner, paired),
         in_specs=[VMEM] * (len(parts) + outputs + 2),
-        out_specs=[VMEM] * (outputs // 2 if paired else outputs),
-        out_shape=[jax.ShapeDtypeStruct((2, tokens, width), dtype)] * (outputs // 2)
-        if paired
-        else [jax.ShapeDtypeStruct((tokens, width), dtype)] * outputs,
+        out_specs=[VMEM] * len(shapes),
+        out_shape=[jax.ShapeDtypeStruct(shape, dtype) for shape in shapes],
         scratch_shapes=[
             pltpu.SMEM((len(parts),) + plans[0].shape, jnp.int32),
             pltpu.SemaphoreType.DMA((len(parts),)),
@@ -416,7 +419,7 @@
 
     results = [None] * members
     for parts in calls_of(members // pieces):
-        paired = parts[0] == members // pieces - 1
+        paired = [part >= members // pieces // 2 for part in parts]
         steps = [part * pieces + step for part in parts for step in range(pieces)]
         outputs = attend(
             [plans[part * pieces // head_size] for part in parts],
@@ -427,14 +430,14 @@
             pieces,
             paired,
         )
-        if paired:
-            for step, output in zip(steps[::2], outputs):
-                output = swap(output, step)
+        outputs = list(outputs)
+        for step in steps:
+            if not paired[parts.index(step // pieces)]:
+                results[step] = (swap(outputs.pop(0), step), None)
+            elif step % 2 == 0:
+                output = swap(outputs.pop(0), step)
                 results[step] = (output, 0)
                 results[step + 1] = (swap(output, 1), 1)
-        else:
-            for step, output in zip(steps, outputs):
-                results[step] = (swap(output, step), None)
     return join_heads(results)
 
 

time: 102 us -> 110 us (1.078)
  the two profiles are of different devices: /device:TPU:0 before, /device:TPU:17 now
where the time goes in v3:
time: 110 us
  starting transfers between devices  44.8 us (41%)
  waiting for transfers between devices  43.9 us (40%)
  Pallas kernels  21.1 us (19%)
    ppermute x22, waiting for transfers between devices, swap(): return lax.ppermute(piece, AXES, pairs)  36.7 us
    ppermute x22, starting transfers between devices, swap(): return lax.ppermute(piece, AXES, pairs)  25.8 us
    ppermute x7, starting transfers between devices, relay(): return lax.ppermute(piece, AXES, pairs)  19 us
    pallas_call x3, Pallas kernels, attend(): pl.pallas_call(functools.partial(attend_kernel, parts, pieces, inner, pai...  15.4 us
    ppermute x7, waiting for transfers between devices, relay(): return lax.ppermute(piece, AXES, pairs)  7.18 us
    pallas_call x1, Pallas kernels, split_heads(): pl.pallas_call(functools.partial(split_kernel, layout), in_specs=[HBM] *...  2.78 us
  transfers between devices with their start and end apart: 29, of which 9 were waited for; matrix products, arithmetic and copies ran while one was open for 0% of the time, Pallas kernels for 16%

profile of v3, /device:TPU:17, one launch (start us, length us, event | category | flops | bytes accessed | tf_op | source)
XLA Modules:
  0.0 110.1 jit_solution(15095988998357011468)
XLA Ops:
  0.0 2.8 %split_heads.1 = (bf16[2,576,128]{2,1,0:T(8,128)(2,1)}, bf16[2,576,128]{2,1,0:T(8,128)(2,1)}, bf16[2,576,128]{2,1,0:T(8,128)(2,1)}, bf16[2,576,128]{2,1,0:T(8,12...) custom-call(bf16[576,1024]{1,0:T(8,128)(2,1)} %refs_0_.1, ...), custom_call_target="tpu_custom_call" | custom-call | tf_op jit(solution)/shard_map/split_heads/pallas_call | solution.py:106
  2.8 0.7 collective-permute-start.7
  3.6 1.2 %collective-permute-start.4 = (bf16[2,576,128]{2,1,0:T(8,128)(2,1)}, bf16[2,576,128]{2,1,0:T(8,128)(2,1)S(1)}, u32[]{:S(2)}, u32[]{:S(2)}) collective-permute-start(bf16[2,576,128]{2,1,0:T(8,128)(2,1)} %get-tuple-element.30), channel_id=1, source_target_pairs={{0,4},{1,5},{2,6},{3,7},{4,0},{5,1},{6,2},{7,3},{8,12},{9,13},{10,... | collective-permute-start | bytes 884744 | tf_op jit(solution)/shard_map/ppermute | solution.py:378
  4.8 0.5 collective-permute-start.3
  5.3 0.1 copy.6
  5.4 0.1 pad_add_fusion.refs_0_.refs_1_
  5.4 1.2 %collective-permute-start.16 = (s32[6,8]{1,0:T(8,128)S(1)}, s32[6,8]{1,0:T(8,128)S(1)}, u32[]{:S(2)}, u32[]{:S(2)}) collective-permute-start(s32[6,8]{1,0:T(8,128)S(1)} %pad_add_fusion.refs_0_.refs_1_), channel_id=1, source_target_pairs={{0,4},{1,5},{2,6},{3,7},{4,0},{5,1},{6,2},{7,3},{8,12},{9,13},{10,... | collective-permute-start | bytes 584 | tf_op jit(solution)/shard_map/ppermute | solution.py:378
  6.6 1.2 %collective-permute-start.2 = (bf16[2,576,128]{2,1,0:T(8,128)(2,1)}, bf16[2,576,128]{2,1,0:T(8,128)(2,1)S(1)}, u32[]{:S(2)}, u32[]{:S(2)}) collective-permute-start(bf16[2,576,128]{2,1,0:T(8,128)(2,1)} %get-tuple-element.28), channel_id=1, source_target_pairs={{0,6},{1,7},{2,4},{3,5},{4,2},{5,3},{6,0},{7,1},{8,14},{9,15},{10,... | collective-permute-start | bytes 884744 | tf_op jit(solution)/shard_map/ppermute | solution.py:378
  7.9 10.7 %collective-permute-done.16.refs_0_ = s32[6,8]{1,0:T(8,128)S(1)} collective-permute-done((s32[6,8]{1,0:T(8,128)S(1)}, s32[6,8]{1,0:T(8,128)S(1)}, u32[]{:S(2)}, u32[]{:S(2)}) %collective-permute-start.16) | collective-permute-done | bytes 224 | tf_op jit(solution)/shard_map/ppermute | solution.py:378
  18.6 3.6 %collective-permute-start.1 = (bf16[2,576,128]{2,1,0:T(8,128)(2,1)}, bf16[2,576,128]{2,1,0:T(8,128)(2,1)S(1)}, u32[]{:S(2)}, u32[]{:S(2)}) collective-permute-start(bf16[2,576,128]{2,1,0:T(8,128)(2,1)} %get-tuple-element.27), channel_id=1, source_target_pairs={{0,7},{1,6},{2,5},{3,4},{4,3},{5,2},{6,1},{7,0},{8,15},{9,14},{10,... | collective-permute-start | bytes 884744 | tf_op jit(solution)/shard_map/ppermute | solution.py:378
  22.2 0.0 collective-permute-done.7.second.refs_7_
  22.2 0.2 collective-permute-start.5
  22.4 0.0 collective-permute-done.4.refs_3_
  22.4 0.4 collective-permute-start.6
  22.8 1.3 %split_queries.1 = (bf16[2,576,128]{2,1,0:T(8,128)(2,1)S(1)}, bf16[2,576,128]{2,1,0:T(8,128)(2,1)S(1)}, bf16[576,128]{1,0:T(8,128)(2,1)S(1)}, bf16[576,128]{1,0:...) custom-call(bf16[576,1024]{1,0:T(8,128)(2,1)S(1)} %copy-done), custom_call_target="tpu_custom_call" | custom-call | tf_op jit(solution)/shard_map/split_queries/pallas_call | solution.py:59
  24.1 1.2 %collective-permute-start.25 = (bf16[2,576,128]{2,1,0:T(8,128)(2,1)S(1)}, bf16[2,576,128]{2,1,0:T(8,128)(2,1)S(1)}, u32[]{:S(2)}, u32[]{:S(2)}) collective-permute-start(bf16[2,576,128]{2,1,0:T(8,128)(2,1)S(1)} %get-tuple-element.46), channel_id=1, source_target_pairs={{0,6},{1,7},{2,4},{3,5},{4,2},{5,3},{6,0},{7,1},{8,14},{9,15},{10,... | collective-permute-start | bytes 884744 | tf_op jit(solution)/shard_map/ppermute | solution.py:378
  25.4 0.6 collective-permute-done.2.refs_1_
  25.9 3.2 %collective-permute-start.10 = (bf16[2,576,128]{2,1,0:T(8,128)(2,1)S(1)}, bf16[2,576,128]{2,1,0:T(8,128)(2,1)S(1)}, u32[]{:S(2)}, u32[]{:S(2)}) collective-permute-start(bf16[2,576,128]{2,1,0:T(8,128)(2,1)S(1)} %collective-permute-done.4.refs_3_), channel_id=1, source_target_pairs={{0,8},{1,9},{2,10},{3,11},{8,16},{9,17},{10,18},{11,19},{12,4},{13... | collective-permute-start | bytes 884744 | tf_op jit(solution)/shard_map/ppermute | solution.py:389
  29.1 4.0 %collective-permute-done.1.refs_0_ = bf16[2,576,128]{2,1,0:T(8,128)(2,1)S(1)} collective-permute-done((bf16[2,576,128]{2,1,0:T(8,128)(2,1)}, bf16[2,576,128]{2,1,0:T(8,128)(2,1)S(1)}, u32[]{:S(2)}, u32[]{:S(2)}) %collective-permute-start.1) | collective-permute-done | bytes 294944 | tf_op jit(solution)/shard_map/ppermute | solution.py:378
  33.1 3.2 %collective-permute-start.11 = (bf16[2,576,128]{2,1,0:T(8,128)(2,1)S(1)}, bf16[2,576,128]{2,1,0:T(8,128)(2,1)S(1)}, u32[]{:S(2)}, u32[]{:S(2)}) collective-permute-start(bf16[2,576,128]{2,1,0:T(8,128)(2,1)S(1)} %collective-permute-done.3.refs_2_), channel_id=1, source_target_pairs={{0,8},{1,9},{2,10},{3,11},{8,16},{9,17},{10,18},{11,19},{12,4},{13... | collective-permute-start | bytes 884744 | tf_op jit(solution)/shard_map/ppermute | solution.py:389
  36.4 9.0 %collective-permute-done.5.refs_4_ = bf16[2,576,128]{2,1,0:T(8,128)(2,1)S(1)} collective-permute-done((bf16[2,576,128]{2,1,0:T(8,128)(2,1)}, bf16[2,576,128]{2,1,0:T(8,128)(2,1)S(1)}, u32[]{:S(2)}, u32[]{:S(2)}) %collective-permute-start.5) | collective-permute-done | bytes 294944 | tf_op jit(solution)/shard_map/ppermute | solution.py:378
  45.4 2.1 %collective-permute-start.14 = (bf16[2,2,576,128]{3,2,1,0:T(8,128)(2,1)S(1)}, bf16[2,2,576,128]{3,2,1,0:T(8,128)(2,1)S(1)}, u32[]{:S(2)}, u32[]{:S(2)}) collective-permute-start(bf16[2,2,576,128]{3,2,1,0:T(8,128)(2,1)S(1)} %pack.1), channel_id=1, source_target_pairs={{4,12},{5,13},{6,14},{7,15},{8,0},{9,1},{10,2},{11,3},{12,20},{13,... | collective-permute-start | bytes 1769480 | tf_op jit(solution)/shard_map/ppermute | solution.py:389
  47.5 4.2 %collective-permute-done.6.refs_5_ = bf16[2,576,128]{2,1,0:T(8,128)(2,1)S(1)} collective-permute-done((bf16[2,576,128]{2,1,0:T(8,128)(2,1)}, bf16[2,576,128]{2,1,0:T(8,128)(2,1)S(1)}, u32[]{:S(2)}, u32[]{:S(2)}) %collective-permute-start.6) | collective-permute-done | bytes 294944 | tf_op jit(solution)/shard_map/ppermute | solution.py:378
  51.7 3.2 %collective-permute-start.12 = (bf16[2,576,128]{2,1,0:T(8,128)(2,1)S(1)}, bf16[2,576,128]{2,1,0:T(8,128)(2,1)S(1)}, u32[]{:S(2)}, u32[]{:S(2)}) collective-permute-start(bf16[2,576,128]{2,1,0:T(8,128)(2,1)S(1)} %collective-permute-done.2.refs_1_), channel_id=1, source_target_pairs={{0,8},{1,9},{2,10},{3,11},{8,16},{9,17},{10,18},{11,19},{12,4},{13... | collective-permute-start | bytes 884744 | tf_op jit(solution)/shard_map/ppermute | solution.py:389
  54.9 1.9 %collective-permute-start.13 = (bf16[2,576,128]{2,1,0:T(8,128)(2,1)S(1)}, bf16[2,576,128]{2,1,0:T(8,128)(2,1)S(1)}, u32[]{:S(2)}, u32[]{:S(2)}) collective-permute-start(bf16[2,576,128]{2,1,0:T(8,128)(2,1)S(1)} %collective-permute-done.1.refs_0_), channel_id=1, source_target_pairs={{0,8},{1,9},{2,10},{3,11},{8,16},{9,17},{10,18},{11,19},{12,4},{13... | collective-permute-start | bytes 884744 | tf_op jit(solution)/shard_map/ppermute | solution.py:389
  56.9 3.4 %collective-permute-start.8 = (bf16[2,576,128]{2,1,0:T(8,128)(2,1)S(1)}, bf16[2,576,128]{2,1,0:T(8,128)(2,1)S(1)}, u32[]{:S(2)}, u32[]{:S(2)}) collective-permute-start(bf16[2,576,128]{2,1,0:T(8,128)(2,1)S(1)} %collective-permute-done.5.refs_4_), channel_id=1, source_target_pairs={{4,12},{5,13},{6,14},{7,15},{8,0},{9,1},{10,2},{11,3},{12,20},{13,... | collective-permute-start | bytes 884744 | tf_op jit(solution)/shard_map/ppermute | solution.py:389
  60.2 2.1 %collective-permute-start.9 = (bf16[2,576,128]{2,1,0:T(8,128)(2,1)S(1)}, bf16[2,576,128]{2,1,0:T(8,128)(2,1)S(1)}, u32[]{:S(2)}, u32[]{:S(2)}) collective-permute-start(bf16[2,576,128]{2,1,0:T(8,128)(2,1)S(1)} %collective-permute-done.6.refs_5_), channel_id=1, source_target_pairs={{4,12},{5,13},{6,14},{7,15},{8,0},{9,1},{10,2},{11,3},{12,20},{13,... | collective-permute-start | bytes 884744 | tf_op jit(solution)/shard_map/ppermute | solution.py:389
  62.3 1.6 %collective-permute-start.26 = (bf16[2,576,128]{2,1,0:T(8,128)(2,1)S(1)}, bf16[2,576,128]{2,1,0:T(8,128)(2,1)S(1)}, u32[]{:S(2)}, u32[]{:S(2)}) collective-permute-start(bf16[2,576,128]{2,1,0:T(8,128)(2,1)S(1)} %collective-permute-done.25.refs_1_), channel_id=1, source_target_pairs={{0,1},{1,0},{2,3},{3,2},{4,5},{5,4},{6,7},{7,6},{8,9},{9,8},{10,11... | collective-permute-start | bytes 884744 | tf_op jit(solution)/shard_map/ppermute | solution.py:378
  64.0 4.0 %collective-permute-done.13.refs_13_ = bf16[2,576,128]{2,1,0:T(8,128)(2,1)S(1)} collective-permute-done((bf16[2,576,128]{2,1,0:T(8,128)(2,1)S(1)}, bf16[2,576,128]{2,1,0:T(8,128)(2,1)S(1)}, u32[]{:S(2)}, u32[]{:S(2)}) %collective-permute-start.13) | collective-permute-done | bytes 294944 | tf_op jit(solution)/shard_map/ppermute | solution.py:389
  68.0 1.2 %collective-permute-start.17 = (bf16[576,128]{1,0:T(8,128)(2,1)S(1)}, bf16[576,128]{1,0:T(8,128)(2,1)S(1)}, u32[]{:S(2)}, u32[]{:S(2)}) collective-permute-start(bf16[576,128]{1,0:T(8,128)(2,1)S(1)} %get-tuple-element.39), channel_id=1, source_target_pairs={{0,4},{1,5},{2,6},{3,7},{4,0},{5,1},{6,2},{7,3},{8,12},{9,13},{10,... | collective-permute-start | bytes 442376 | tf_op jit(solution)/shard_map/ppermute | solution.py:378
  69.2 2.0 %collective-permute-start.18 = (bf16[576,128]{1,0:T(8,128)(2,1)S(1)}, bf16[576,128]{1,0:T(8,128)(2,1)S(1)}, u32[]{:S(2)}, u32[]{:S(2)}) collective-permute-start(bf16[576,128]{1,0:T(8,128)(2,1)S(1)} %get-tuple-element.40), channel_id=1, source_target_pairs={{0,5},{1,4},{2,7},{3,6},{4,1},{5,0},{6,3},{7,2},{8,13},{9,12},{10,... | collective-permute-start | bytes 442376 | tf_op jit(solution)/shard_map/ppermute | solution.py:378
  71.3 3.1 %collective-permute-done.9.refs_9_ = bf16[2,576,128]{2,1,0:T(8,128)(2,1)S(1)} collective-permute-done((bf16[2,576,128]{2,1,0:T(8,128)(2,1)S(1)}, bf16[2,576,128]{2,1,0:T(8,128)(2,1)S(1)}, u32[]{:S(2)}, u32[]{:S(2)}) %collective-permute-start.9) | collective-permute-done | bytes 294944 | tf_op jit(solution)/shard_map/ppermute | solution.py:389
  74.4 0.2 collective-permute-start.19
  74.6 2.7 %collective-permute-start.20 = (bf16[576,128]{1,0:T(8,128)(2,1)S(1)}, bf16[576,128]{1,0:T(8,128)(2,1)S(1)}, u32[]{:S(2)}, u32[]{:S(2)}) collective-permute-start(bf16[576,128]{1,0:T(8,128)(2,1)S(1)} %get-tuple-element.42), channel_id=1, source_target_pairs={{0,3},{1,2},{2,1},{3,0},{4,7},{5,6},{6,5},{7,4},{8,11},{9,10},{10,... | collective-permute-start | bytes 442376 | tf_op jit(solution)/shard_map/ppermute | solution.py:378
  77.3 0.4 assemble.1
  77.7 3.5 %attend.5 = bf16[2,576,128]{2,1,0:T(8,128)(2,1)S(1)} custom-call(s32[6,8]{1,0:T(8,128)S(1)} %collective-permute-done.16.refs_0_, bf16[2,576,128]{2,1,0:T(8,128)(2,1)S(1)} %collective-permute-done.25.refs_1_, bf16[2,576,128]{2,1,0:T(8,128)(2,1)S(1)} %collective-permute-done.26.refs_2_, bf16[9216,128]{1,0:T(8,128)(2,1)S(1)} %get-tuple-element.35.refs_3_.refs_6_, ...), custom_call_target="tpu_custom_call" | custom-call | flops 905969664 | bytes 589824 | tf_op jit(solution)/shard_map/attend/pallas_call | solution.py:335
  81.2 3.1 %collective-permute-start.27 = (bf16[2,576,128]{2,1,0:T(8,128)(2,1)S(1)}, bf16[2,576,128]{2,1,0:T(8,128)(2,1)S(1)}, u32[]{:S(2)}, u32[]{:S(2)}) collective-permute-start(bf16[2,576,128]{2,1,0:T(8,128)(2,1)S(1)} %attend.5), channel_id=1, source_target_pairs={{0,6},{1,7},{2,4},{3,5},{4,2},{5,3},{6,0},{7,1},{8,14},{9,15},{10,... | collective-permute-start | bytes 884744 | tf_op jit(solution)/shard_map/ppermute | solution.py:378
  84.3 6.5 %attend.4 = (bf16[2,576,128]{2,1,0:T(8,128)(2,1)S(1)}, bf16[576,128]{1,0:T(8,128)(2,1)S(1)}, bf16[576,128]{1,0:T(8,128)(2,1)S(1)}) custom-call(s32[6,8]{1,0:T(8,128)S(1)} %collective-permute-done.16.refs_0_, s32[6,8]{1,0:T(8,128)S(1)} %pad_add_fusion.refs_0_.refs_1_, bf16[576,128]{1,0:T(8,128)(2,1)S(1)} %collective-permute-done.17.refs_2_, ...), custom_call_target="tpu_custom_call" | custom-call | flops 1811939328 | bytes 1179648 | tf_op jit(solution)/shard_map/attend/pallas_call | solution.py:335
  90.8 1.3 %collective-permute-start.23 = (bf16[2,576,128]{2,1,0:T(8,128)(2,1)S(1)}, bf16[2,576,128]{2,1,0:T(8,128)(2,1)S(1)}, u32[]{:S(2)}, u32[]{:S(2)}) collective-permute-start(bf16[2,576,128]{2,1,0:T(8,128)(2,1)S(1)} %get-tuple-element.45), channel_id=1, source_target_pairs={{0,4},{1,5},{2,6},{3,7},{4,0},{5,1},{6,2},{7,3},{8,12},{9,13},{10,... | collective-permute-start | bytes 884744 | tf_op jit(solution)/shard_map/ppermute | solution.py:378
  92.1 0.5 collective-permute-start.28
  92.6 6.8 %collective-permute-done.23.refs_4_ = bf16[2,576,128]{2,1,0:T(8,128)(2,1)S(1)} collective-permute-done((bf16[2,576,128]{2,1,0:T(8,128)(2,1)S(1)}, bf16[2,576,128]{2,1,0:T(8,128)(2,1)S(1)}, u32[]{:S(2)}, u32[]{:S(2)}) %collective-permute-start.23) | collective-permute-done | bytes 294944 | tf_op jit(solution)/shard_map/ppermute | solution.py:378
  99.4 1.0 collective-permute-start.24
  100.3 0.5 collective-permute-start.21
  100.8 1.1 %collective-permute-start.22 = (bf16[576,128]{1,0:T(8,128)(2,1)S(1)}, bf16[576,128]{1,0:T(8,128)(2,1)S(1)}, u32[]{:S(2)}, u32[]{:S(2)}) collective-permute-start(bf16[576,128]{1,0:T(8,128)(2,1)S(1)} %get-tuple-element.44), channel_id=1, source_target_pairs={{0,3},{1,2},{2,1},{3,0},{4,7},{5,6},{6,5},{7,4},{8,11},{9,10},{10,... | collective-permute-start | bytes 442376 | tf_op jit(solution)/shard_map/ppermute | solution.py:378
  102.0 5.4 %attend.3 = (bf16[576,128]{1,0:T(8,128)(2,1)S(1)}, bf16[576,128]{1,0:T(8,128)(2,1)S(1)}) custom-call(s32[6,8]{1,0:T(8,128)S(1)} %pad_add_fusion.refs_0_.refs_1_, bf16[2,576,128]{2,1,0:T(8,128)(2,1)S(1)} %get-tuple-element.26.refs_1_, bf16[2,576,128]{2,1,0:T(8,128)(2,1)S(1)} %collective-permute-done.refs_2_, ...), custom_call_target="tpu_custom_call" | custom-call | flops 905969664 | bytes 589824 | tf_op jit(solution)/shard_map/attend/pallas_call | solution.py:335
  107.3 0.3 collective-permute-start.15
  107.6 1.4 %collective-permute-done.22.refs_3_ = bf16[576,128]{1,0:T(8,128)(2,1)S(1)} collective-permute-done((bf16[576,128]{1,0:T(8,128)(2,1)S(1)}, bf16[576,128]{1,0:T(8,128)(2,1)S(1)}, u32[]{:S(2)}, u32[]{:S(2)}) %collective-permute-start.22) | collective-permute-done | bytes 147488 | tf_op jit(solution)/shard_map/ppermute | solution.py:378
  109.1 1.1 join_heads.1
  (28 shorter events, 0.1 us)
Async XLA Ops:
  0.0 5.3 %copy-start.3 = (s32[6]{0:T(128)S(1)}, s32[6]{0:T(128)}, u32[]{:S(2)}) copy-start(s32[6]{0:T(128)} %param.9) | copy-start | bytes 76
  0.0 5.4 %copy-start.2 = (s32[6,7]{1,0:T(8,128)S(1)}, s32[6,7]{1,0:T(8,128)}, u32[]{:S(2)}) copy-start(s32[6,7]{1,0:T(8,128)} %param.8) | copy-start | bytes 508
  0.0 22.8 %copy-start = (bf16[576,1024]{1,0:T(8,128)(2,1)S(1)}, bf16[576,1024]{1,0:T(8,128)(2,1)}, u32[]{:S(2)}) copy-start(bf16[576,1024]{1,0:T(8,128)(2,1)} %source.1) | copy-start | bytes 3538948
  2.8 33.5 %copy-start.1 = (bf16[2,576,128]{2,1,0:T(8,128)(2,1)S(1)}, bf16[2,576,128]{2,1,0:T(8,128)(2,1)}, u32[]{:S(2)}) copy-start(bf16[2,576,128]{2,1,0:T(8,128)(2,1)} %get-tuple-element.33.first.refs_6_) | copy-start | bytes 884740
  2.8 19.4 %collective-permute-start.7 = (bf16[2,576,128]{2,1,0:T(8,128)(2,1)}, bf16[2,576,128]{2,1,0:T(8,128)(2,1)S(1)}, u32[]{:S(2)}, u32[]{:S(2)}) collective-permute-start(bf16[2,576,128]{2,1,0:T(8,128)(2,1)} %get-tuple-element.34), channel_id=1, source_target_pairs={{0,1},{1,0},{2,3},{3,2},{4,5},{5,4},{6,7},{7,6},{8,9},{9,8},{10,11... | collective-permute-start | bytes 884744 | tf_op jit(solution)/shard_map/ppermute | solution.py:378
  3.6 18.9 %collective-permute-start.4 = (bf16[2,576,128]{2,1,0:T(8,128)(2,1)}, bf16[2,576,128]{2,1,0:T(8,128)(2,1)S(1)}, u32[]{:S(2)}, u32[]{:S(2)}) collective-permute-start(bf16[2,576,128]{2,1,0:T(8,128)(2,1)} %get-tuple-element.30), channel_id=1, source_target_pairs={{0,4},{1,5},{2,6},{3,7},{4,0},{5,1},{6,2},{7,3},{8,12},{9,13},{10,... | collective-permute-start | bytes 884744 | tf_op jit(solution)/shard_map/ppermute | solution.py:378
  4.8 19.4 %collective-permute-start.3 = (bf16[2,576,128]{2,1,0:T(8,128)(2,1)}, bf16[2,576,128]{2,1,0:T(8,128)(2,1)S(1)}, u32[]{:S(2)}, u32[]{:S(2)}) collective-permute-start(bf16[2,576,128]{2,1,0:T(8,128)(2,1)} %get-tuple-element.29), channel_id=1, source_target_pairs={{0,5},{1,4},{2,7},{3,6},{4,1},{5,0},{6,3},{7,2},{8,13},{9,12},{10,... | collective-permute-start | bytes 884744 | tf_op jit(solution)/shard_map/ppermute | solution.py:378
  5.4 13.1 %collective-permute-start.16 = (s32[6,8]{1,0:T(8,128)S(1)}, s32[6,8]{1,0:T(8,128)S(1)}, u32[]{:S(2)}, u32[]{:S(2)}) collective-permute-start(s32[6,8]{1,0:T(8,128)S(1)} %pad_add_fusion.refs_0_.refs_1_), channel_id=1, source_target_pairs={{0,4},{1,5},{2,6},{3,7},{4,0},{5,1},{6,2},{7,3},{8,12},{9,13},{10,... | collective-permute-start | bytes 584 | tf_op jit(solution)/shard_map/ppermute | solution.py:378
  6.6 19.3 %collective-permute-start.2 = (bf16[2,576,128]{2,1,0:T(8,128)(2,1)}, bf16[2,576,128]{2,1,0:T(8,128)(2,1)S(1)}, u32[]{:S(2)}, u32[]{:S(2)}) collective-permute-start(bf16[2,576,128]{2,1,0:T(8,128)(2,1)} %get-tuple-element.28), channel_id=1, source_target_pairs={{0,6},{1,7},{2,4},{3,5},{4,2},{5,3},{6,0},{7,1},{8,14},{9,15},{10,... | collective-permute-start | bytes 884744 | tf_op jit(solution)/shard_map/ppermute | solution.py:378
  18.6 14.6 %collective-permute-start.1 = (bf16[2,576,128]{2,1,0:T(8,128)(2,1)}, bf16[2,576,128]{2,1,0:T(8,128)(2,1)S(1)}, u32[]{:S(2)}, u32[]{:S(2)}) collective-permute-start(bf16[2,576,128]{2,1,0:T(8,128)(2,1)} %get-tuple-element.27), channel_id=1, source_target_pairs={{0,7},{1,6},{2,5},{3,4},{4,3},{5,2},{6,1},{7,0},{8,15},{9,14},{10,... | collective-permute-start | bytes 884744 | tf_op jit(solution)/shard_map/ppermute | solution.py:378
  22.2 23.2 %collective-permute-start.5 = (bf16[2,576,128]{2,1,0:T(8,128)(2,1)}, bf16[2,576,128]{2,1,0:T(8,128)(2,1)S(1)}, u32[]{:S(2)}, u32[]{:S(2)}) collective-permute-start(bf16[2,576,128]{2,1,0:T(8,128)(2,1)} %get-tuple-element.31), channel_id=1, source_target_pairs={{0,2},{1,3},{2,0},{3,1},{4,6},{5,7},{6,4},{7,5},{8,10},{9,11},{10,... | collective-permute-start | bytes 884744 | tf_op jit(solution)/shard_map/ppermute | solution.py:378
  22.4 29.3 %collective-permute-start.6 = (bf16[2,576,128]{2,1,0:T(8,128)(2,1)}, bf16[2,576,128]{2,1,0:T(8,128)(2,1)S(1)}, u32[]{:S(2)}, u32[]{:S(2)}) collective-permute-start(bf16[2,576,128]{2,1,0:T(8,128)(2,1)} %get-tuple-element.32), channel_id=1, source_target_pairs={{0,3},{1,2},{2,1},{3,0},{4,7},{5,6},{6,5},{7,4},{8,11},{9,10},{10,... | collective-permute-start | bytes 884744 | tf_op jit(solution)/shard_map/ppermute | solution.py:378
  24.1 30.8 %collective-permute-start.25 = (bf16[2,576,128]{2,1,0:T(8,128)(2,1)S(1)}, bf16[2,576,128]{2,1,0:T(8,128)(2,1)S(1)}, u32[]{:S(2)}, u32[]{:S(2)}) collective-permute-start(bf16[2,576,128]{2,1,0:T(8,128)(2,1)S(1)} %get-tuple-element.46), channel_id=1, source_target_pairs={{0,6},{1,7},{2,4},{3,5},{4,2},{5,3},{6,0},{7,1},{8,14},{9,15},{10,... | collective-permute-start | bytes 884744 | tf_op jit(solution)/shard_map/ppermute | solution.py:378
  25.9 30.9 %collective-permute-start.10 = (bf16[2,576,128]{2,1,0:T(8,128)(2,1)S(1)}, bf16[2,576,128]{2,1,0:T(8,128)(2,1)S(1)}, u32[]{:S(2)}, u32[]{:S(2)}) collective-permute-start(bf16[2,576,128]{2,1,0:T(8,128)(2,1)S(1)} %collective-permute-done.4.refs_3_), channel_id=1, source_target_pairs={{0,8},{1,9},{2,10},{3,11},{8,16},{9,17},{10,18},{11,19},{12,4},{13... | collective-permute-start | bytes 884744 | tf_op jit(solution)/shard_map/ppermute | solution.py:389
  33.1 27.1 %collective-permute-start.11 = (bf16[2,576,128]{2,1,0:T(8,128)(2,1)S(1)}, bf16[2,576,128]{2,1,0:T(8,128)(2,1)S(1)}, u32[]{:S(2)}, u32[]{:S(2)}) collective-permute-start(bf16[2,576,128]{2,1,0:T(8,128)(2,1)S(1)} %collective-permute-done.3.refs_2_), channel_id=1, source_target_pairs={{0,8},{1,9},{2,10},{3,11},{8,16},{9,17},{10,18},{11,19},{12,4},{13... | collective-permute-start | bytes 884744 | tf_op jit(solution)/shard_map/ppermute | solution.py:389
  45.4 29.2 %collective-permute-start.14 = (bf16[2,2,576,128]{3,2,1,0:T(8,128)(2,1)S(1)}, bf16[2,2,576,128]{3,2,1,0:T(8,128)(2,1)S(1)}, u32[]{:S(2)}, u32[]{:S(2)}) collective-permute-start(bf16[2,2,576,128]{3,2,1,0:T(8,128)(2,1)S(1)} %pack.1), channel_id=1, source_target_pairs={{4,12},{5,13},{6,14},{7,15},{8,0},{9,1},{10,2},{11,3},{12,20},{13,... | collective-permute-start | bytes 1769480 | tf_op jit(solution)/shard_map/ppermute | solution.py:389
  51.7 10.6 %collective-permute-start.12 = (bf16[2,576,128]{2,1,0:T(8,128)(2,1)S(1)}, bf16[2,576,128]{2,1,0:T(8,128)(2,1)S(1)}, u32[]{:S(2)}, u32[]{:S(2)}) collective-permute-start(bf16[2,576,128]{2,1,0:T(8,128)(2,1)S(1)} %collective-permute-done.2.refs_1_), channel_id=1, source_target_pairs={{0,8},{1,9},{2,10},{3,11},{8,16},{9,17},{10,18},{11,19},{12,4},{13... | collective-permute-start | bytes 884744 | tf_op jit(solution)/shard_map/ppermute | solution.py:389
  54.9 13.1 %collective-permute-start.13 = (bf16[2,576,128]{2,1,0:T(8,128)(2,1)S(1)}, bf16[2,576,128]{2,1,0:T(8,128)(2,1)S(1)}, u32[]{:S(2)}, u32[]{:S(2)}) collective-permute-start(bf16[2,576,128]{2,1,0:T(8,128)(2,1)S(1)} %collective-permute-done.1.refs_0_), channel_id=1, source_target_pairs={{0,8},{1,9},{2,10},{3,11},{8,16},{9,17},{10,18},{11,19},{12,4},{13... | collective-permute-start | bytes 884744 | tf_op jit(solution)/shard_map/ppermute | solution.py:389
  56.9 12.4 %collective-permute-start.8 = (bf16[2,576,128]{2,1,0:T(8,128)(2,1)S(1)}, bf16[2,576,128]{2,1,0:T(8,128)(2,1)S(1)}, u32[]{:S(2)}, u32[]{:S(2)}) collective-permute-start(bf16[2,576,128]{2,1,0:T(8,128)(2,1)S(1)} %collective-permute-done.5.refs_4_), channel_id=1, source_target_pairs={{4,12},{5,13},{6,14},{7,15},{8,0},{9,1},{10,2},{11,3},{12,20},{13,... | collective-permute-start | bytes 884744 | tf_op jit(solution)/shard_map/ppermute | solution.py:389
  60.2 14.2 %collective-permute-start.9 = (bf16[2,576,128]{2,1,0:T(8,128)(2,1)S(1)}, bf16[2,576,128]{2,1,0:T(8,128)(2,1)S(1)}, u32[]{:S(2)}, u32[]{:S(2)}) collective-permute-start(bf16[2,576,128]{2,1,0:T(8,128)(2,1)S(1)} %collective-permute-done.6.refs_5_), channel_id=1, source_target_pairs={{4,12},{5,13},{6,14},{7,15},{8,0},{9,1},{10,2},{11,3},{12,20},{13,... | collective-permute-start | bytes 884744 | tf_op jit(solution)/shard_map/ppermute | solution.py:389
  62.3 15.3 %collective-permute-start.26 = (bf16[2,576,128]{2,1,0:T(8,128)(2,1)S(1)}, bf16[2,576,128]{2,1,0:T(8,128)(2,1)S(1)}, u32[]{:S(2)}, u32[]{:S(2)}) collective-permute-start(bf16[2,576,128]{2,1,0:T(8,128)(2,1)S(1)} %collective-permute-done.25.refs_1_), channel_id=1, source_target_pairs={{0,1},{1,0},{2,3},{3,2},{4,5},{5,4},{6,7},{7,6},{8,9},{9,8},{10,11... | collective-permute-start | bytes 884744 | tf_op jit(solution)/shard_map/ppermute | solution.py:378
  68.0 16.3 %collective-permute-start.17 = (bf16[576,128]{1,0:T(8,128)(2,1)S(1)}, bf16[576,128]{1,0:T(8,128)(2,1)S(1)}, u32[]{:S(2)}, u32[]{:S(2)}) collective-permute-start(bf16[576,128]{1,0:T(8,128)(2,1)S(1)} %get-tuple-element.39), channel_id=1, source_target_pairs={{0,4},{1,5},{2,6},{3,7},{4,0},{5,1},{6,2},{7,3},{8,12},{9,13},{10,... | collective-permute-start | bytes 442376 | tf_op jit(solution)/shard_map/ppermute | solution.py:378
  69.2 15.1 %collective-permute-start.18 = (bf16[576,128]{1,0:T(8,128)(2,1)S(1)}, bf16[576,128]{1,0:T(8,128)(2,1)S(1)}, u32[]{:S(2)}, u32[]{:S(2)}) collective-permute-start(bf16[576,128]{1,0:T(8,128)(2,1)S(1)} %get-tuple-element.40), channel_id=1, source_target_pairs={{0,5},{1,4},{2,7},{3,6},{4,1},{5,0},{6,3},{7,2},{8,13},{9,12},{10,... | collective-permute-start | bytes 442376 | tf_op jit(solution)/shard_map/ppermute | solution.py:378
  74.4 9.9 %collective-permute-start.19 = (bf16[576,128]{1,0:T(8,128)(2,1)S(1)}, bf16[576,128]{1,0:T(8,128)(2,1)S(1)}, u32[]{:S(2)}, u32[]{:S(2)}) collective-permute-start(bf16[576,128]{1,0:T(8,128)(2,1)S(1)} %get-tuple-element.41), channel_id=1, source_target_pairs={{0,2},{1,3},{2,0},{3,1},{4,6},{5,7},{6,4},{7,5},{8,10},{9,11},{10,... | collective-permute-start | bytes 442376 | tf_op jit(solution)/shard_map/ppermute | solution.py:378
  74.6 9.7 %collective-permute-start.20 = (bf16[576,128]{1,0:T(8,128)(2,1)S(1)}, bf16[576,128]{1,0:T(8,128)(2,1)S(1)}, u32[]{:S(2)}, u32[]{:S(2)}) collective-permute-start(bf16[576,128]{1,0:T(8,128)(2,1)S(1)} %get-tuple-element.42), channel_id=1, source_target_pairs={{0,3},{1,2},{2,1},{3,0},{4,7},{5,6},{6,5},{7,4},{8,11},{9,10},{10,... | collective-permute-start | bytes 442376 | tf_op jit(solution)/shard_map/ppermute | solution.py:378
  81.2 10.8 %collective-permute-start.27 = (bf16[2,576,128]{2,1,0:T(8,128)(2,1)S(1)}, bf16[2,576,128]{2,1,0:T(8,128)(2,1)S(1)}, u32[]{:S(2)}, u32[]{:S(2)}) collective-permute-start(bf16[2,576,128]{2,1,0:T(8,128)(2,1)S(1)} %attend.5), channel_id=1, source_target_pairs={{0,6},{1,7},{2,4},{3,5},{4,2},{5,3},{6,0},{7,1},{8,14},{9,15},{10,... | collective-permute-start | bytes 884744 | tf_op jit(solution)/shard_map/ppermute | solution.py:378
  90.8 8.5 %collective-permute-start.23 = (bf16[2,576,128]{2,1,0:T(8,128)(2,1)S(1)}, bf16[2,576,128]{2,1,0:T(8,128)(2,1)S(1)}, u32[]{:S(2)}, u32[]{:S(2)}) collective-permute-start(bf16[2,576,128]{2,1,0:T(8,128)(2,1)S(1)} %get-tuple-element.45), channel_id=1, source_target_pairs={{0,4},{1,5},{2,6},{3,7},{4,0},{5,1},{6,2},{7,3},{8,12},{9,13},{10,... | collective-permute-start | bytes 884744 | tf_op jit(solution)/shard_map/ppermute | solution.py:378
  92.1 9.9 %collective-permute-start = (bf16[2,576,128]{2,1,0:T(8,128)(2,1)S(1)}, bf16[2,576,128]{2,1,0:T(8,128)(2,1)S(1)}, u32[]{:S(2)}, u32[]{:S(2)}) collective-permute-start(bf16[2,576,128]{2,1,0:T(8,128)(2,1)S(1)} %get-tuple-element.26.refs_1_), channel_id=1, source_target_pairs={{0,1},{1,0},{2,3},{3,2},{4,5},{5,4},{6,7},{7,6},{8,9},{9,8},{10,11... | collective-permute-start | bytes 884744 | tf_op jit(solution)/shard_map/ppermute | solution.py:378
  92.1 17.0 %collective-permute-start.28 = (bf16[2,576,128]{2,1,0:T(8,128)(2,1)S(1)}, bf16[2,576,128]{2,1,0:T(8,128)(2,1)S(1)}, u32[]{:S(2)}, u32[]{:S(2)}) collective-permute-start(bf16[2,576,128]{2,1,0:T(8,128)(2,1)S(1)} %collective-permute-done.27.refs_6_), channel_id=1, source_target_pairs={{0,1},{1,0},{2,3},{3,2},{4,5},{5,4},{6,7},{7,6},{8,9},{9,8},{10,11... | collective-permute-start | bytes 884744 | tf_op jit(solution)/shard_map/ppermute | solution.py:378
  99.4 9.7 %collective-permute-start.24 = (bf16[2,576,128]{2,1,0:T(8,128)(2,1)S(1)}, bf16[2,576,128]{2,1,0:T(8,128)(2,1)S(1)}, u32[]{:S(2)}, u32[]{:S(2)}) collective-permute-start(bf16[2,576,128]{2,1,0:T(8,128)(2,1)S(1)} %collective-permute-done.23.refs_4_), channel_id=1, source_target_pairs={{0,1},{1,0},{2,3},{3,2},{4,5},{5,4},{6,7},{7,6},{8,9},{9,8},{10,11... | collective-permute-start | bytes 884744 | tf_op jit(solution)/shard_map/ppermute | solution.py:378
  100.3 7.3 %collective-permute-start.21 = (bf16[576,128]{1,0:T(8,128)(2,1)S(1)}, bf16[576,128]{1,0:T(8,128)(2,1)S(1)}, u32[]{:S(2)}, u32[]{:S(2)}) collective-permute-start(bf16[576,128]{1,0:T(8,128)(2,1)S(1)} %get-tuple-element.43), channel_id=1, source_target_pairs={{0,2},{1,3},{2,0},{3,1},{4,6},{5,7},{6,4},{7,5},{8,10},{9,11},{10,... | collective-permute-start | bytes 442376 | tf_op jit(solution)/shard_map/ppermute | solution.py:378
  100.8 8.2 %collective-permute-start.22 = (bf16[576,128]{1,0:T(8,128)(2,1)S(1)}, bf16[576,128]{1,0:T(8,128)(2,1)S(1)}, u32[]{:S(2)}, u32[]{:S(2)}) collective-permute-start(bf16[576,128]{1,0:T(8,128)(2,1)S(1)} %get-tuple-element.44), channel_id=1, source_target_pairs={{0,3},{1,2},{2,1},{3,0},{4,7},{5,6},{6,5},{7,4},{8,11},{9,10},{10,... | collective-permute-start | bytes 442376 | tf_op jit(solution)/shard_map/ppermute | solution.py:378
  107.3 1.7 %collective-permute-start.15 = (bf16[576,128]{1,0:T(8,128)(2,1)S(1)}, bf16[576,128]{1,0:T(8,128)(2,1)S(1)}, u32[]{:S(2)}, u32[]{:S(2)}) collective-permute-start(bf16[576,128]{1,0:T(8,128)(2,1)S(1)} %get-tuple-element.38), channel_id=1, source_target_pairs={{0,1},{1,0},{2,3},{3,2},{4,5},{5,4},{6,7},{7,6},{8,9},{9,8},{10,11... | collective-permute-start | bytes 442376 | tf_op jit(solution)/shard_map/ppermute | solution.py:378
